TPU v7x, 32 devices: a whole 2x2x4 slice. The times are simulated.
32 devices in a mesh: group: 2 (over y), seq: 4 (over z), head: 4 (over x, core), pair: 1.
Axes of the slice: x: 2, y: 2, z: 4, core: 2. Of those that a mesh axis runs over, the one named last changes fastest.
Arguments:
- query_states: bfloat16 [2048, 4096], P(('group', 'seq'), ('head', 'pair')), parts along dimension 0, may hold values from -6 to 6
- key_states: bfloat16 [2048, 512], P(('group', 'seq'), 'head'), parts along dimension 0, may hold values from -6 to 6
- value_states: bfloat16 [2048, 512], P(('group', 'seq'), 'head'), parts along dimension 0, may hold values from -12 to 12
- sink_logits: float32 [64], P(('head', 'pair')), may hold values from 0 to 5
- segment_ids: int32 [2048], P('group'), parts along dimension 0, may hold values from 0 to 11, never falling along the last dimension, each value on 1 to 256 neighbouring positions
- residual: bfloat16 [2048, 1536], P(('group', 'seq', 'head', 'pair')), parts along dimension 0, may hold values from -6 to 6
- out_weight: bfloat16 [4096, 1536], P(('head', 'pair')), may hold values from -0.09375 to 0.09375
- norm_gain: float32 [1536], replicated, may hold values from 0.5 to 1.5
- expert_ids: int32 [2048, 4], P(('group', 'seq', 'head', 'pair')), parts along dimension 0, may hold values from 0 to 7, all different within a row; in each aligned block of 64 rows (0 to 63, 64 to 127, ...) at most 48 rows name the same one
- route_weights: float32 [2048, 4], P(('group', 'seq', 'head', 'pair')), parts along dimension 0, may hold values from 0.1 to 1
- gate_proj: bfloat16 [16, 1536, 768], P(('seq', 'head'), None, 'pair'), may hold values from -0.15625 to 0.15625
- up_proj: bfloat16 [16, 1536, 768], P(('seq', 'head'), None, 'pair'), may hold values from -0.15625 to 0.15625
- down_proj: bfloat16 [16, 768, 1536], P(('seq', 'head'), 'pair'), may hold values from -0.15625 to 0.15625
Outputs:
- layer_out: bfloat16 [2048, 1536], P(('group', 'seq', 'head', 'pair')), parts along dimension 0
There are 2 independent parts, one for each index of `group`. A program takes and returns all parts, laid end to end along the dimension named above; an argument that names none is the same for every part. Nothing has to cross between parts.
Inputs may be any that keep to these rules, and one draw needn't show every extreme that they name: `segment_ids`: never falling along the sequence; each passage holds 1 to 256 tokens and one holds exactly 256. `expert_ids`: each row names 4 different experts. Among the rows of one device (aligned blocks of 64 rows) no expert is named by more than 48 rows, a bound that some block reaches.
All inputs are finite; a program needn't handle non-finite values.
Results may differ from a plain program's by a relative error of at most 0.015.
Values may be sent and summed in bfloat16 or wider, within the bound.
No kernel may reach another device: no remote copies, remote signals or barrier semaphores. Data moves between devices by JAX's collectives and lax.ppermute only.
A program may use at most 64 MiB of HBM per device.

v0:
```python
import jax
import jax.numpy as jnp
from jax import lax
from jax.sharding import PartitionSpec as P

HEADS = 64
KV_HEADS = 8
HEAD_DIM = 64
WINDOW = 128


def passed_along(value, axis, by):
    peers = lax.axis_size(axis)
    pairs = [(i, i + by) for i in range(peers) if 0 <= i + by < peers]
    return lax.ppermute(value, axis, pairs)


def partner(value, axis, distance):
    return lax.ppermute(value, axis, [(i, i ^ 1 << distance) for i in range(lax.axis_size(axis))])


def round_keep(values):
    return lax.optimization_barrier(values.astype(jnp.bfloat16)).astype(jnp.float32)


def window_attention(
    query_block, key_block, value_block, query_pos, key_pos, query_seg, key_seg, sink_logits
):
    scores = jnp.einsum(
        "qhd,khd->hqk", query_block, key_block, preferred_element_type=jnp.float32
    ) * HEAD_DIM ** (-0.5)
    visible = (key_pos[None, :] <= query_pos[:, None]) & (
        query_pos[:, None] - key_pos[None, :] < WINDOW
    )
    visible = visible & (key_pos[None, :] >= 0) & (key_seg[None, :] == query_seg[:, None])
    masked = jnp.where(visible[None], scores, -1e30)
    row_max = jnp.maximum(jnp.max(masked, -1), sink_logits[:, None])
    weights_exp = jnp.exp(masked - row_max[..., None])
    denominator = jnp.sum(weights_exp, -1) + jnp.exp(sink_logits[:, None] - row_max)
    probs = (weights_exp / denominator[..., None]).astype(jnp.bfloat16)
    attended = jnp.einsum("hqk,khd->qhd", probs, value_block, preferred_element_type=jnp.float32)
    return attended.astype(jnp.bfloat16)


def per_device(
    query_states,
    key_states,
    value_states,
    sink_logits,
    segment_ids,
    residual,
    out_weight,
    norm_gain,
    expert_ids,
    route_weights,
    gate_proj,
    up_proj,
    down_proj,
):
    tok_rows = query_states.shape[0]
    local_heads = query_states.shape[1] // HEAD_DIM
    local_groups = key_states.shape[1] // HEAD_DIM
    group_size = HEADS // KV_HEADS
    tail_keys, tail_values = passed_along(
        (key_states[tok_rows - WINDOW :], value_states[tok_rows - WINDOW :]), "seq", 1
    )
    ext_keys = jnp.concatenate([tail_keys, key_states], 0).reshape(
        tok_rows + WINDOW, local_groups, HEAD_DIM
    )
    ext_values = jnp.concatenate([tail_values, value_states], 0).reshape(
        tok_rows + WINDOW, local_groups, HEAD_DIM
    )
    kv_owner = (
        lax.axis_index("pair") * local_heads + jnp.arange(local_heads, dtype=jnp.int32)
    ) // group_size
    head_select = (kv_owner[:, None] == jnp.arange(local_groups, dtype=jnp.int32)[None, :]).astype(
        jnp.bfloat16
    )
    keys_per_head = jnp.einsum(
        "kcd,hc->khd", ext_keys, head_select, preferred_element_type=jnp.float32
    ).astype(jnp.bfloat16)
    values_per_head = jnp.einsum(
        "kcd,hc->khd", ext_values, head_select, preferred_element_type=jnp.float32
    ).astype(jnp.bfloat16)
    query_heads = query_states.reshape(tok_rows, local_heads, HEAD_DIM)
    seq_start = lax.axis_index("seq") * tok_rows
    seg_padded = jnp.concatenate([jnp.full((WINDOW,), -1, jnp.int32), segment_ids], 0)
    block_rows = min(512, tok_rows)

    def attend(block_index):
        first_row = block_index * block_rows
        query_pos = seq_start + first_row + jnp.arange(block_rows, dtype=jnp.int32)
        key_pos = seq_start + first_row - WINDOW + jnp.arange(block_rows + WINDOW, dtype=jnp.int32)
        query_seg = lax.dynamic_slice_in_dim(segment_ids, seq_start + first_row, block_rows, 0)
        key_seg = lax.dynamic_slice_in_dim(
            seg_padded, seq_start + first_row, block_rows + WINDOW, 0
        )
        return window_attention(
            query_heads,
            keys_per_head,
            values_per_head,
            query_pos,
            key_pos,
            query_seg,
            key_seg,
            sink_logits,
        )

    attended = lax.map(attend, jnp.arange(tok_rows // block_rows, dtype=jnp.int32))
    attended = attended.reshape(tok_rows, local_heads * HEAD_DIM)
    shard_rows = residual.shape[0]
    width = residual.shape[1]
    projected = lax.psum_scatter(
        round_keep(jnp.dot(attended, out_weight, preferred_element_type=jnp.float32)).astype(
            jnp.bfloat16
        ),
        ("head", "pair"),
        scatter_dimension=0,
        tiled=True,
    ).astype(jnp.float32)
    hidden_state = residual.astype(jnp.float32) + projected
    variance = jnp.mean(hidden_state * hidden_state, -1, keepdims=True)
    normed = (hidden_state * lax.rsqrt(variance + 1e-05) * norm_gain).astype(jnp.bfloat16)
    top_count = expert_ids.shape[1]
    experts = lax.axis_size("seq") * lax.axis_size("head") // 2
    capacity = min(shard_rows, max(2, 3 * shard_rows * top_count // (2 * experts)))
    flat_ids = expert_ids.reshape(-1)
    onehot = (flat_ids[:, None] == jnp.arange(experts, dtype=jnp.int32)[None, :]).astype(jnp.int32)
    before = jnp.cumsum(onehot, axis=0, dtype=jnp.int32) - onehot
    slot_rank = jnp.sum(before * onehot, -1)
    slot_index = flat_ids * capacity + slot_rank
    dispatch_mat = (
        slot_index[None, :] == jnp.arange(experts * capacity, dtype=jnp.int32)[:, None]
    ).astype(jnp.bfloat16)
    repeated = jnp.repeat(normed, top_count, axis=0)
    outgoing = jnp.dot(dispatch_mat, repeated, preferred_element_type=jnp.float32).astype(
        jnp.bfloat16
    )
    outgoing = outgoing.reshape(experts, capacity, width)
    half_idx = lax.axis_index("head") % 2
    half_width = width // 2
    split_rows = outgoing.reshape(experts, capacity, 2, half_width).transpose(0, 2, 1, 3)
    split_rows = split_rows.reshape(2 * experts, capacity, half_width)
    own_half = lax.all_to_all(split_rows, ("seq", "head"), split_axis=0, concat_axis=0, tiled=True)
    other_half = partner(own_half, "head", 0)
    arrived = jnp.where(
        half_idx == 0,
        jnp.concatenate([own_half, other_half], -1),
        jnp.concatenate([other_half, own_half], -1),
    )
    gate_local = gate_proj[0]
    up_local = up_proj[0]
    down_local = down_proj[0]
    piece_rows = lax.all_gather(arrived, "pair", axis=0, tiled=True)
    flat_rows = piece_rows.reshape(-1, width)
    gate_val = jnp.minimum(jnp.dot(flat_rows, gate_local, preferred_element_type=jnp.float32), 7.0)
    up_val = jnp.clip(jnp.dot(flat_rows, up_local, preferred_element_type=jnp.float32), -7.0, 7.0)
    activated = ((up_val + 1.0) * gate_val * jax.nn.sigmoid(1.702 * gate_val)).astype(jnp.bfloat16)
    partial_value = round_keep(jnp.dot(activated, down_local, preferred_element_type=jnp.float32))
    quarter_terms = partial_value.reshape(piece_rows.shape)
    pair_sums = lax.psum_scatter(
        quarter_terms.astype(jnp.bfloat16), "pair", scatter_dimension=0, tiled=True
    ).astype(jnp.float32)
    kept_half = lax.dynamic_slice_in_dim(pair_sums, half_idx * half_width, half_width, 2)
    given_half = lax.dynamic_slice_in_dim(pair_sums, (1 - half_idx) * half_width, half_width, 2)
    partner_half = partner(given_half.astype(jnp.bfloat16), "head", 0).astype(given_half.dtype)
    merged = kept_half + partner_half
    returned = lax.all_to_all(
        merged.astype(jnp.bfloat16), ("seq", "head"), split_axis=0, concat_axis=0, tiled=True
    ).astype(merged.dtype)
    expert_out = (
        returned.reshape(experts, 2, capacity, half_width)
        .transpose(0, 2, 1, 3)
        .reshape(experts, capacity, width)
    )
    slot_table = slot_index.reshape(shard_rows, top_count)
    columns_all = jnp.arange(experts * capacity, dtype=jnp.int32)
    combine_mat = jnp.sum(
        jnp.where(
            slot_table[:, :, None] == columns_all[None, None, :], route_weights[:, :, None], 0.0
        ),
        axis=1,
    )
    mixture = jnp.dot(
        combine_mat, expert_out.reshape(experts * capacity, width), precision=lax.Precision.HIGHEST
    )
    return (hidden_state + mixture).astype(jnp.bfloat16)


def solution(mesh):
    in_specs = (
        P(("group", "seq"), ("head", "pair")),
        P(("group", "seq"), "head"),
        P(("group", "seq"), "head"),
        P(("head", "pair")),
        P("group"),
        P(("group", "seq", "head", "pair"), None),
        P(("head", "pair"), None),
        P(),
        P(("group", "seq", "head", "pair"), None),
        P(("group", "seq", "head", "pair"), None),
        P(("seq", "head"), None, "pair"),
        P(("seq", "head"), None, "pair"),
        P(("seq", "head"), "pair", None),
    )
    out_specs = P(("group", "seq", "head", "pair"), None)
    return jax.shard_map(
        per_device, mesh=mesh, in_specs=in_specs, out_specs=out_specs, check_vma=False
    )
```

profile of v0, /device:TPU:11, one launch (start us, length us, event | category | flops | bytes accessed | tf_op | source)
XLA Modules:
  0.0 174.1 jit_solution(3354271913761056211)
XLA Ops:
  6.5 0.0 copy-start
  6.5 0.0 reduce-scatter.2.cloned.1.call-start
  6.5 1.1 copy.67
  7.6 3.2 %collective-permute-start.1 = (bf16[128,128]{0,1:T(8,128)(2,1)S(1)}, bf16[128,128]{0,1:T(8,128)(2,1)S(1)}, u32[]{:S(2)}, u32[]{:S(2)}) collective-permute-start(bf16[128,128]{0,1:T(8,128)(2,1)S(1)} %slice.17), channel_id=1, source_target_pairs={{0,4},{4,8},{8,12},{1,5},{5,9},{9,13},{2,6},{6,10},{10,14},{3,7},{... | collective-permute-start | bytes 98312 | tf_op jit(solution)/shard_map/ppermute | solution.py:15
  10.9 0.9 copy.64
  11.8 3.2 %collective-permute-start = (bf16[128,128]{0,1:T(8,128)(2,1)S(1)}, bf16[128,128]{0,1:T(8,128)(2,1)S(1)}, u32[]{:S(2)}, u32[]{:S(2)}) collective-permute-start(bf16[128,128]{0,1:T(8,128)(2,1)S(1)} %slice.16), channel_id=1, source_target_pairs={{0,4},{4,8},{8,12},{1,5},{5,9},{9,13},{2,6},{6,10},{10,14},{3,7},{... | collective-permute-start | bytes 98312 | tf_op jit(solution)/shard_map/ppermute | solution.py:15
  15.1 0.8 pad_dynamic-slice_fusion
  15.8 0.8 dynamic_slice.18
  16.6 0.2 fusion.21
  16.8 2.0 %copy.70 = bf16[256,1024]{0,1:T(8,128)(2,1)} copy(bf16[256,1024]{1,0:T(8,128)(2,1)} %param.13) | data formatting | bytes 1048576 | tf_op args[0]
  18.9 0.0 collective-permute-done.1
  18.9 0.5 fusion.13
  19.4 0.0 copy-start.6
  19.4 2.2 %fusion.1 = (f32[16,256]{1,0:T(8,128)S(1)}, f32[16,384,256]{2,1,0:T(8,128)S(1)}) fusion(pred[256,384]{0,1:T(8,128)(4,1)S(1)} %fusion.21, bf16[256,16,64]{0,2,1:T(8,128)(2,1)} %bitcast.70, bf16[384,16,64]{0,1,2:T(8,128)(2,1)S(1)} %fusion.13), kind=kOutput, calls=%fused_computation.4 | convolution fusion | flops 206041088 | bytes 7716864 | tf_op jit(solution)/shard_map/while/body/eval_jaxpr/qhd,khd->hqk/dot_general | solution.py:29
  21.6 0.0 copy-done.6
  21.6 0.1 broadcast_maximum_fusion
  21.7 1.3 fusion
  23.0 0.1 exponential_add_fusion
  23.0 0.0 collective-permute-done
  23.1 0.5 fusion.12
  23.5 1.8 %fusion.11 = bf16[16,64,256]{2,1,0:T(8,128)(2,1)S(1)} fusion(f32[16,384,256]{2,1,0:T(8,128)S(1)} %get-tuple-element.22, f32[16,256]{1,0:T(8,128)S(1)} %exponential_add_fusion, f32[16,256]{1,0:T(8,128)S(1)} %broadcast_maximum_fusion, pred[256,384]{0,1:T(8,128)(4,1)S(1)} %fusion.21, bf16[384,16,64]{0,1,2:T(8,128)(2,1)S(1)} %fusion.12), kind=kOutput, calls=%fused_computation.22 | convolution fusion | flops 209453056 | bytes 7733248 | tf_op jit(solution)/shard_map/while/body/eval_jaxpr/hqk,khd->qhd/dot_general | solution.py:41
  25.3 0.0 copy-done
  25.4 0.0 copy-start.5
  25.4 0.0 copy-start.2
  25.4 0.0 copy-start.4
  25.4 1.9 %convolution_convert_fusion.2 = bf16[256,1536]{1,0:T(8,128)(2,1)} fusion(bf16[256,1024]{0,1:T(8,128)(2,1)S(1)} %bitcast.73, bf16[1024,1536]{1,0:T(8,128)(2,1)S(1)} %copy-done), kind=kOutput, calls=%fused_computation.8 | convolution fusion | flops 805699584 | bytes 4456448 | tf_op jit(solution)/shard_map/dot_general | solution.py:114
  27.3 0.0 reduce-scatter.2.cloned.1.call-update
  27.3 0.0 copy-done.5
  27.3 0.1 copy.74
  27.4 0.1 eq.109
  27.5 0.1 eq.105
  27.6 0.6 reduce-window.6
  28.2 0.2 slice_reduce_fusion
  28.5 0.1 fusion.26
  28.6 20.7 %reduce-scatter.2.cloned.1.call-done = bf16[64,1536]{1,0:T(8,128)(2,1)} async-done(((bf16[256,1536]{1,0:T(8,128)(2,1)}), bf16[64,1536]{1,0:T(8,128)(2,1)}) %reduce-scatter.2.cloned.1.call-update) | async-done | bytes 196624 | tf_op jit(solution)/shard_map/reduce_scatter | solution.py:113
  49.3 0.0 copy-done.2
  49.3 1.1 multiply_reduce_fusion
  50.4 0.0 copy-done.4
  50.4 1.0 multiply_convert_fusion.1
  51.4 1.1 broadcast_in_dim.69
  52.5 2.3 %reshape.253 = bf16[256,1536]{1,0:T(8,128)(2,1)} reshape(bf16[64,4,1536]{2,1,0:T(4,128)(2,1)} %broadcast_in_dim.69) | data formatting | bytes 1572864 | tf_op jit(solution)/shard_map/reshape | solution.py:135
  54.8 2.6 %convolution_convert_fusion.1 = bf16[384,1536]{1,0:T(8,128)(2,1)} fusion(bf16[256,1536]{1,0:T(8,128)(2,1)} %reshape.253, s32[256]{0:T(256)S(1)} %multiply_add_fusion.1), kind=kOutput, calls=%fused_computation.7 | convolution fusion | flops 302678016 | bytes 1967104 | tf_op jit(solution)/shard_map/dot_general | solution.py:136
  57.4 3.7 %reshape_reshape.6 = bf16[8,48,2,768]{3,2,1,0:T(2,128)(2,1)} reshape(bf16[384,1536]{1,0:T(8,128)(2,1)} %convolution_convert_fusion.1) | data formatting | bytes 2359296 | tf_op jit(solution)/shard_map/reshape;reshape | solution.py:142
  61.1 1.4 copy.77
  62.5 34.0 %all_to_all.10 = bf16[16,48,768]{2,1,0:T(8,128)(2,1)} all-to-all(bf16[16,48,768]{2,1,0:T(8,128)(2,1)S(1)} %bitcast.67), channel_id=1, replica_groups=mesh['group'=2,'seq'=4,'head'=4,'pair'=1] {'seq','head'}, dimensions={0} | all-to-all | bytes 2359296 | tf_op jit(solution)/shard_map/all_to_all | solution.py:144
  96.5 0.3 collective-permute-start.2
  96.9 2.9 %collective-permute-done.2 = bf16[16,48,768]{2,1,0:T(8,128)(2,1)} collective-permute-done((bf16[16,48,768]{2,1,0:T(8,128)(2,1)}, bf16[16,48,768]{2,1,0:T(8,128)(2,1)}, u32[]{:S(2)}, u32[]{:S(2)}) %collective-permute-start.2) | collective-permute-done | bytes 1179680 | tf_op jit(solution)/shard_map/ppermute | solution.py:19
  99.7 6.6 %fusion.6 = f32[768,768]{1,0:T(8,128)} fusion(bf16[1,1536,768]{2,1,0:T(8,128)(2,1)} %param.24, bf16[768,768]{1,0:T(8,128)(2,1)} %bitcast.14, bf16[768,768]{1,0:T(8,128)(2,1)} %bitcast.13, pred[]{:T(512)S(6)} %eq.116), kind=kOutput, calls=%fused_computation.13 | convolution fusion | flops 1822556160 | bytes 7077889 | tf_op jit(solution)/shard_map/dot_general | solution.py:157
  106.3 10.8 %convolution_convert_fusion = bf16[768,1536]{1,0:T(8,128)(2,1)} fusion(bf16[1,768,1536]{2,1,0:T(8,128)(2,1)} %param.25, f32[768,768]{1,0:T(8,128)} %fusion.6, bf16[1,1536,768]{2,1,0:T(8,128)(2,1)} %param.23, bf16[768,768]{1,0:T(8,128)(2,1)} %bitcast.14, bf16[768,768]{1,0:T(8,128)(2,1)} %bitcast.13, pred[]{:T(512)S(6)} %eq.116), kind=kOutput, calls=%fused_computation.5 | convolution fusion | flops 3641573376 | bytes 11796481 | tf_op jit(solution)/shard_map/dot_general | solution.py:159
  117.1 2.3 %convert.1 = f32[16,48,1536]{2,1,0:T(8,128)S(1)} convert(bf16[16,48,1536]{2,1,0:T(8,128)(2,1)} %bitcast.69) | non-fusion elementwise | flops 1179648 | bytes 7077888 | tf_op jit(solution)/shard_map/convert_element_type | solution.py:163
  119.4 2.1 %copy-done.1 = f32[16,48,1536]{2,1,0:T(8,128)} copy-done((f32[16,48,1536]{2,1,0:T(8,128)}, f32[16,48,1536]{2,1,0:T(8,128)S(1)}, u32[]{:S(2)}) %copy-start.1) | copy-done | bytes 4718616
  121.5 1.2 dynamic-slice_convert_fusion
  122.7 0.3 collective-permute-start.3
  123.0 2.9 %collective-permute-done.3 = bf16[16,48,768]{2,1,0:T(8,128)(2,1)} collective-permute-done((bf16[16,48,768]{2,1,0:T(8,128)(2,1)}, bf16[16,48,768]{2,1,0:T(8,128)(2,1)}, u32[]{:S(2)}, u32[]{:S(2)}) %collective-permute-start.3) | collective-permute-done | bytes 1179680 | tf_op jit(solution)/shard_map/ppermute | solution.py:19
  125.9 3.3 %add_convert_fusion = bf16[16,48,768]{2,1,0:T(8,128)(2,1)} fusion(bf16[16,48,768]{2,1,0:T(8,128)(2,1)} %collective-permute-done.3, f32[16,48,1536]{2,1,0:T(8,128)} %copy-done.1, s32[]{:T(128)S(6)} %select_n.58), kind=kLoop, calls=%fused_computation.15 | loop fusion | flops 1769472 | bytes 4718596 | tf_op jit(solution)/shard_map/convert_element_type | solution.py:169
  129.2 6.3 %all-to-all-start.1 = ((bf16[16,48,768]{2,1,0:T(8,128)(2,1)}), bf16[16,48,768]{2,1,0:T(8,128)(2,1)}, u32[]{:S(2)}, u32[]{:S(2)}) async-start(bf16[16,48,768]{2,1,0:T(8,128)(2,1)} %add_convert_fusion), calls=%async_computation.2 | async-start | bytes 2359296 | tf_op jit(solution)/shard_map/all_to_all | solution.py:168
  135.5 0.1 reduce_sum.41
  135.6 0.1 copy.76
  135.7 0.0 copy-done.7
  135.7 0.1 select_reduce_fusion
  135.9 27.5 %all-to-all-done.1 = bf16[16,48,768]{2,1,0:T(8,128)(2,1)} async-done(((bf16[16,48,768]{2,1,0:T(8,128)(2,1)}), bf16[16,48,768]{2,1,0:T(8,128)(2,1)}, u32[]{:S(2)}, u32[]{:S(2)}) %all-to-all-start.1) | async-done | bytes 1179680 | tf_op jit(solution)/shard_map/all_to_all | solution.py:168
  163.4 2.3 %copy.78 = bf16[8,48,2,768]{3,2,1,0:T(2,128)(2,1)S(1)} copy(bf16[8,48,2,768]{3,1,2,0:T(8,128)(2,1)} %bitcast.21) | data formatting | bytes 2359296 | tf_op jit(solution)/shard_map/transpose | solution.py:173
  165.7 0.2 copy.80
  165.9 1.4 fusion.8
  (17 shorter events, 0.1 us)
Async XLA Ops:
  6.5 18.8 %copy-start = (bf16[1024,1536]{1,0:T(8,128)(2,1)S(1)}, bf16[1024,1536]{1,0:T(8,128)(2,1)}, u32[]{:S(2)}) copy-start(bf16[1024,1536]{1,0:T(8,128)(2,1)} %param.19) | copy-start | bytes 9437188
  6.5 42.7 %reduce-scatter.2.cloned.1.call-start = ((), (), s32[]{:S(2)}) async-start(), calls=%async_computation.3 | async-start | bytes 983040 | tf_op jit(solution)/shard_map/reduce_scatter | solution.py:113
  7.6 11.2 %collective-permute-start.1 = (bf16[128,128]{0,1:T(8,128)(2,1)S(1)}, bf16[128,128]{0,1:T(8,128)(2,1)S(1)}, u32[]{:S(2)}, u32[]{:S(2)}) collective-permute-start(bf16[128,128]{0,1:T(8,128)(2,1)S(1)} %slice.17), channel_id=1, source_target_pairs={{0,4},{4,8},{8,12},{1,5},{5,9},{9,13},{2,6},{6,10},{10,14},{3,7},{... | collective-permute-start | bytes 98312 | tf_op jit(solution)/shard_map/ppermute | solution.py:15
  11.8 11.2 %collective-permute-start = (bf16[128,128]{0,1:T(8,128)(2,1)S(1)}, bf16[128,128]{0,1:T(8,128)(2,1)S(1)}, u32[]{:S(2)}, u32[]{:S(2)}) collective-permute-start(bf16[128,128]{0,1:T(8,128)(2,1)S(1)} %slice.16), channel_id=1, source_target_pairs={{0,4},{4,8},{8,12},{1,5},{5,9},{9,13},{2,6},{6,10},{10,14},{3,7},{... | collective-permute-start | bytes 98312 | tf_op jit(solution)/shard_map/ppermute | solution.py:15
  19.4 2.2 %copy-start.6 = (f32[16]{0:T(128)S(1)}, f32[16]{0:T(128)}, u32[]{:S(2)}) copy-start(f32[16]{0:T(128)} %param.16) | copy-start | bytes 196
  25.4 1.9 %copy-start.5 = (s32[64,4]{0,1:T(4,128)S(1)}, s32[64,4]{0,1:T(4,128)}, u32[]{:S(2)}) copy-start(s32[64,4]{0,1:T(4,128)} %param.21) | copy-start | bytes 3076
  25.4 23.9 %copy-start.2 = (bf16[64,1536]{1,0:T(8,128)(2,1)S(1)}, bf16[64,1536]{1,0:T(8,128)(2,1)}, u32[]{:S(2)}) copy-start(bf16[64,1536]{1,0:T(8,128)(2,1)} %param.18) | copy-start | bytes 589828
  25.4 25.0 %copy-start.4 = (f32[1536]{0:T(1024)S(1)}, f32[1536]{0:T(1024)}, u32[]{:S(2)}) copy-start(f32[1536]{0:T(1024)} %param.20) | copy-start | bytes 18436
  96.5 3.2 %collective-permute-start.2 = (bf16[16,48,768]{2,1,0:T(8,128)(2,1)}, bf16[16,48,768]{2,1,0:T(8,128)(2,1)}, u32[]{:S(2)}, u32[]{:S(2)}) collective-permute-start(bf16[16,48,768]{2,1,0:T(8,128)(2,1)} %all_to_all.10), channel_id=1, source_target_pairs={{0,1},{1,0},{2,3},{3,2},{4,5},{5,4},{6,7},{7,6},{8,9},{9,8},{10,11... | collective-permute-start | bytes 3538952 | tf_op jit(solution)/shard_map/ppermute | solution.py:19
  119.4 2.1 %copy-start.1 = (f32[16,48,1536]{2,1,0:T(8,128)}, f32[16,48,1536]{2,1,0:T(8,128)S(1)}, u32[]{:S(2)}) copy-start(f32[16,48,1536]{2,1,0:T(8,128)S(1)} %convert.1) | copy-start | bytes 14155780
  122.7 3.2 %collective-permute-start.3 = (bf16[16,48,768]{2,1,0:T(8,128)(2,1)}, bf16[16,48,768]{2,1,0:T(8,128)(2,1)}, u32[]{:S(2)}, u32[]{:S(2)}) collective-permute-start(bf16[16,48,768]{2,1,0:T(8,128)(2,1)} %dynamic-slice_convert_fusion), channel_id=1, source_target_pairs={{0,1},{1,0},{2,3},{3,2},{4,5},{5,4},{6,7},{7,6},{8,9},{9,8},{10,11... | collective-permute-start | bytes 3538952 | tf_op jit(solution)/shard_map/ppermute | solution.py:19
  129.2 6.5 %copy-start.7 = (f32[64,4]{0,1:T(4,128)S(1)}, f32[64,4]{0,1:T(4,128)}, u32[]{:S(2)}) copy-start(f32[64,4]{0,1:T(4,128)} %param.22) | copy-start | bytes 3076
  129.2 34.2 %all-to-all-start.1 = ((bf16[16,48,768]{2,1,0:T(8,128)(2,1)}), bf16[16,48,768]{2,1,0:T(8,128)(2,1)}, u32[]{:S(2)}, u32[]{:S(2)}) async-start(bf16[16,48,768]{2,1,0:T(8,128)(2,1)} %add_convert_fusion), calls=%async_computation.2 | async-start | bytes 2359296 | tf_op jit(solution)/shard_map/all_to_all | solution.py:168
  163.4 2.5 %copy-start.3 = (bf16[64,1536]{1,0:T(8,128)(2,1)S(1)}, bf16[64,1536]{1,0:T(8,128)(2,1)}, u32[]{:S(2)}) copy-start(bf16[64,1536]{1,0:T(8,128)(2,1)} %reduce-scatter.2.cloned.1.call-done) | copy-start | bytes 589828
Sparse Core Ops, SparseCore 0:
  27.4 21.8 reduce-scatter.1
where the time goes:
time: 175 us; the launch traced here: 174 us
  waiting for transfers between devices  54 us (31%)
  blocking collectives  34 us (19%)
  matrix products  28.2 us (16%)
  local copies, waits for them, and re-layouts  19.8 us (11%)
  between operations  13.7 us (8%)
  starting transfers between devices  13.4 us (8%)
  other arithmetic  11.1 us (6%)
    all_to_all x1, blocking collectives, per_device(): lax.all_to_all(split_rows, ('seq', 'head'), split_axis=0, concat_axis=0,...  34 us
    all_to_all x1, waiting for transfers between devices, per_device(): lax.all_to_all(merged.astype(jnp.bfloat16), ('seq', 'head'), split_axis=0...  27.5 us
    reduce_scatter x1, waiting for transfers between devices, per_device(): lax.psum_scatter(round_keep(jnp.dot(attended, out_weight, preferred_eleme...  20.7 us
    dot_general x1, matrix products, per_device(): jnp.dot(activated, down_local, preferred_element_type=jnp.float32)  10.8 us
    dot_general x1, matrix products, per_device(): jnp.dot(flat_rows, up_local, preferred_element_type=jnp.float32)  6.56 us
    unnamed x21, local copies, waits for them, and re-layouts  6.48 us
    ppermute x2, starting transfers between devices, passed_along(): return lax.ppermute(value, axis, pairs)  6.41 us
    all_to_all x1, starting transfers between devices, per_device(): lax.all_to_all(merged.astype(jnp.bfloat16), ('seq', 'head'), split_axis=0...  6.28 us
  transfers between devices with their start and end apart: 6, of which 4 were waited for; matrix products, arithmetic and copies ran while one was open for 6% of the time, Pallas kernels for 0%

commit v1 on v0

--- a/solution.py
+++ b/solution.py
@@ -1,12 +1,18 @@
+import functools
+
 import jax
 import jax.numpy as jnp
 from jax import lax
+from jax.experimental import pallas as pl
+from jax.experimental.pallas import tpu as pltpu
 from jax.sharding import PartitionSpec as P
+
 
 HEADS = 64
 KV_HEADS = 8
 HEAD_DIM = 64
 WINDOW = 128
+LANES = 128
 
 
 def passed_along(value, axis, by):
@@ -42,21 +48,7 @@
     return attended.astype(jnp.bfloat16)
 
 
-def per_device(
-    query_states,
-    key_states,
-    value_states,
-    sink_logits,
-    segment_ids,
-    residual,
-    out_weight,
-    norm_gain,
-    expert_ids,
-    route_weights,
-    gate_proj,
-    up_proj,
-    down_proj,
-):
+def attention(query_states, key_states, value_states, sink_logits, segment_ids):
     tok_rows = query_states.shape[0]
     local_heads = query_states.shape[1] // HEAD_DIM
     local_groups = key_states.shape[1] // HEAD_DIM
@@ -107,7 +99,25 @@
         )
 
     attended = lax.map(attend, jnp.arange(tok_rows // block_rows, dtype=jnp.int32))
-    attended = attended.reshape(tok_rows, local_heads * HEAD_DIM)
+    return attended.reshape(tok_rows, local_heads * HEAD_DIM)
+
+
+def rms_normed(hidden_state, norm_gain):
+    variance = jnp.mean(hidden_state * hidden_state, -1, keepdims=True)
+    return (hidden_state * lax.rsqrt(variance + 1e-05) * norm_gain).astype(jnp.bfloat16)
+
+
+def exchanged_layer(
+    attended,
+    residual,
+    out_weight,
+    norm_gain,
+    expert_ids,
+    route_weights,
+    gate_proj,
+    up_proj,
+    down_proj,
+):
     shard_rows = residual.shape[0]
     width = residual.shape[1]
     projected = lax.psum_scatter(
@@ -119,8 +129,7 @@
         tiled=True,
     ).astype(jnp.float32)
     hidden_state = residual.astype(jnp.float32) + projected
-    variance = jnp.mean(hidden_state * hidden_state, -1, keepdims=True)
-    normed = (hidden_state * lax.rsqrt(variance + 1e-05) * norm_gain).astype(jnp.bfloat16)
+    normed = rms_normed(hidden_state, norm_gain)
     top_count = expert_ids.shape[1]
     experts = lax.axis_size("seq") * lax.axis_size("head") // 2
     capacity = min(shard_rows, max(2, 3 * shard_rows * top_count // (2 * experts)))
@@ -148,15 +157,16 @@
         jnp.concatenate([own_half, other_half], -1),
         jnp.concatenate([other_half, own_half], -1),
     )
-    gate_local = gate_proj[0]
-    up_local = up_proj[0]
-    down_local = down_proj[0]
     piece_rows = lax.all_gather(arrived, "pair", axis=0, tiled=True)
     flat_rows = piece_rows.reshape(-1, width)
-    gate_val = jnp.minimum(jnp.dot(flat_rows, gate_local, preferred_element_type=jnp.float32), 7.0)
-    up_val = jnp.clip(jnp.dot(flat_rows, up_local, preferred_element_type=jnp.float32), -7.0, 7.0)
+    gate_val = jnp.minimum(
+        jnp.dot(flat_rows, gate_proj[0], preferred_element_type=jnp.float32), 7.0
+    )
+    up_val = jnp.clip(
+        jnp.dot(flat_rows, up_proj[0], preferred_element_type=jnp.float32), -7.0, 7.0
+    )
     activated = ((up_val + 1.0) * gate_val * jax.nn.sigmoid(1.702 * gate_val)).astype(jnp.bfloat16)
-    partial_value = round_keep(jnp.dot(activated, down_local, preferred_element_type=jnp.float32))
+    partial_value = round_keep(jnp.dot(activated, down_proj[0], preferred_element_type=jnp.float32))
     quarter_terms = partial_value.reshape(piece_rows.shape)
     pair_sums = lax.psum_scatter(
         quarter_terms.astype(jnp.bfloat16), "pair", scatter_dimension=0, tiled=True
@@ -187,6 +197,435 @@
     return (hidden_state + mixture).astype(jnp.bfloat16)
 
 
+def attend_block(
+    query, window_keys, window_values, bias, sink_ref, score_ref, prob_ref, inverse_ref, store
+):
+    rows = query.shape[0]
+    span = window_keys.shape[0]
+    groups = window_keys.shape[1] // HEAD_DIM
+    tiles = query.shape[1] // LANES // groups
+    lane = lax.broadcasted_iota(jnp.int32, (span, LANES), 1)
+    out_lane = lax.broadcasted_iota(jnp.int32, (rows, LANES), 1)
+
+    def both_sides(values, group):
+        tile = values[:, group // 2 * LANES : (group // 2 + 1) * LANES]
+        here = jnp.where(lane // HEAD_DIM == group % 2, tile, 0.0)
+        there = pltpu.roll(here, HEAD_DIM, 1)
+        sides = [here, there] if group % 2 == 0 else [there, here]
+        return jnp.concatenate(sides, 0).astype(jnp.bfloat16)
+
+    for group in range(groups):
+        keys = both_sides(window_keys.astype(jnp.float32) * HEAD_DIM**-0.5, group)
+        first = group * tiles
+        stacked = jnp.concatenate(
+            [query[:, (first + t) * LANES : (first + t + 1) * LANES] for t in range(tiles)], 0
+        )
+        score_ref[group] = lax.dot_general(
+            stacked, keys, (((1,), (1,)), ((), ())), preferred_element_type=jnp.float32
+        )
+    for group in range(groups):
+        first = group * tiles
+        for t in range(tiles):
+            at = slice(t * rows, (t + 1) * rows)
+            inverses = []
+            for side in range(2):
+                cols = slice(side * span, (side + 1) * span)
+                sink = sink_ref[2 * (first + t) + side]
+                masked = score_ref[group, at, cols] + bias
+                top = jnp.maximum(jnp.max(masked, -1, keepdims=True), sink)
+                weights = jnp.exp(masked - top)
+                total = jnp.sum(weights, -1, keepdims=True) + jnp.exp(sink - top)
+                prob_ref[group, at, cols] = weights.astype(jnp.bfloat16)
+                inverses.append(1.0 / total)
+            inverse_ref[group, at, :] = jnp.where(out_lane < HEAD_DIM, inverses[0], inverses[1])
+    for group in range(groups):
+        first = group * tiles
+        values = both_sides(window_values.astype(jnp.float32), group)
+        out = jnp.dot(prob_ref[group], values, preferred_element_type=jnp.float32)
+        out = (out * inverse_ref[group]).astype(jnp.bfloat16)
+        for t in range(tiles):
+            store(first + t, out[t * rows : (t + 1) * rows])
+
+
+def visible_bias(segment_ref, before, here, starts):
+    row = segment_ref[pl.ds(here, 1), :]
+    prior = jnp.where(starts, -1, segment_ref[pl.ds(before, 1), :])
+    block = (WINDOW, WINDOW)
+    own = jnp.transpose(jnp.broadcast_to(row, block).astype(jnp.float32))
+    query_at = lax.broadcasted_iota(jnp.int32, block, 0)
+    key_at = lax.broadcasted_iota(jnp.int32, block, 1)
+    earlier = (key_at > query_at) & (own == prior.astype(jnp.float32))
+    later = (key_at <= query_at) & (own == row.astype(jnp.float32))
+    seen = jnp.concatenate([earlier, later], 1)
+    return jnp.where(seen, 0.0, -1e30)
+
+
+def later_body(seq_ref, sink_ref, query_ref, key_ref, value_ref, segment_ref, out_ref, *scratch):
+    blocks = query_ref.shape[0] // WINDOW
+    for block in range(1, blocks):
+        here = seq_ref[0] * blocks + block
+        bias = visible_bias(segment_ref, here - 1, here, False)
+        rows = slice(block * WINDOW, (block + 1) * WINDOW)
+        window = slice((block - 1) * WINDOW, (block + 1) * WINDOW)
+
+        def store(tile, value, block=block):
+            at = slice((block - 1) * WINDOW, block * WINDOW)
+            out_ref[at, tile * LANES : (tile + 1) * LANES] = value
+
+        attend_block(
+            query_ref[rows, :],
+            key_ref[window, :],
+            value_ref[window, :],
+            bias,
+            sink_ref,
+            *scratch,
+            store,
+        )
+
+
+def first_body(
+    seq_ref,
+    sink_ref,
+    query_ref,
+    key_ref,
+    value_ref,
+    segment_ref,
+    tail_ref,
+    later_ref,
+    weight_ref,
+    kept_ref,
+    given_ref,
+    sorted_ref,
+    *scratch,
+):
+    tokens = later_ref.shape[0] + WINDOW
+    half = tokens // 2
+    shard_rows = kept_ref.shape[1]
+    piece = min(shard_rows, WINDOW)
+    core = seq_ref[1]
+    blocks = tokens // WINDOW
+    here = seq_ref[0] * blocks
+    starts = seq_ref[0] == 0
+    bias = visible_bias(segment_ref, jnp.maximum(here - 1, 0), here, starts)
+    kv_width = key_ref.shape[1]
+
+    def goal(row):
+        owner = row // shard_rows
+        side = jnp.where(core == owner % 2, 0, half)
+        return pl.multiple_of(side + owner // 2 * shard_rows + row % shard_rows, piece)
+
+    for row in range(WINDOW, tokens, piece):
+        sorted_ref[pl.ds(goal(row), piece), :] = later_ref[row - WINDOW : row - WINDOW + piece, :]
+
+    def store(tile, value):
+        for row in range(0, WINDOW, piece):
+            sorted_ref[pl.ds(goal(row), piece), tile * LANES : (tile + 1) * LANES] = value[
+                row : row + piece
+            ]
+
+    attend_block(
+        query_ref[...],
+        jnp.concatenate([tail_ref[:, :kv_width], key_ref[...]], 0),
+        jnp.concatenate([tail_ref[:, kv_width:], value_ref[...]], 0),
+        bias,
+        sink_ref,
+        *scratch,
+        store,
+    )
+    width = weight_ref.shape[1]
+    columns = kept_ref.shape[0]
+    tile = 512 if width % 512 == 0 else width
+    for low in range(0, width, tile):
+        cols = slice(low, low + tile)
+        value = jnp.dot(
+            sorted_ref[...], weight_ref[:, cols], preferred_element_type=jnp.float32
+        ).astype(jnp.bfloat16)
+        for column in range(columns):
+            at = column * shard_rows
+            kept_ref[column, :, cols] = value[at : at + shard_rows]
+            given_ref[column, :, cols] = value[half + at : half + at + shard_rows]
+
+
+VMEM = pl.BlockSpec(memory_space=pltpu.VMEM)
+SMEM = pl.BlockSpec(memory_space=pltpu.SMEM)
+
+
+def call(body, outs, args, specs, scratch=(), flops=0, limit=16 << 20):
+    moved = sum(a.size * a.dtype.itemsize for a in args)
+    return pl.pallas_call(
+        body,
+        out_shape=outs,
+        in_specs=specs,
+        out_specs=jax.tree.map(lambda _: VMEM, outs),
+        scratch_shapes=list(scratch),
+        compiler_params=pltpu.CompilerParams(vmem_limit_bytes=limit),
+        cost_estimate=pl.CostEstimate(flops=flops, bytes_accessed=moved, transcendentals=0),
+    )(*args)
+
+
+def projected_heads(
+    query_states, key_states, value_states, sink_logits, segment_ids, out_weight, shard_rows
+):
+    tokens, width = query_states.shape
+    kv_width = key_states.shape[1]
+    groups = kv_width // HEAD_DIM
+    stack = width // LANES // groups * WINDOW
+    where_at = jnp.stack([lax.axis_index("seq"), lax.axis_index("head") % 2]).astype(jnp.int32)
+    segment_rows = segment_ids.reshape(-1, WINDOW)
+    tail = passed_along(
+        jnp.concatenate([key_states[tokens - WINDOW :], value_states[tokens - WINDOW :]], 1),
+        "seq",
+        1,
+    )
+    scratch = [
+        pltpu.VMEM((groups, stack, 4 * WINDOW), jnp.float32),
+        pltpu.VMEM((groups, stack, 4 * WINDOW), jnp.bfloat16),
+        pltpu.VMEM((groups, stack, LANES), jnp.float32),
+    ]
+    flops = 16 * WINDOW * WINDOW * width
+    later = call(
+        later_body,
+        jax.ShapeDtypeStruct((tokens - WINDOW, width), jnp.bfloat16),
+        [where_at, sink_logits, query_states, key_states, value_states, segment_rows],
+        [SMEM, SMEM] + [VMEM] * 4,
+        scratch,
+        flops * (tokens // WINDOW - 1),
+    )
+    columns = tokens // (2 * shard_rows)
+    out_width = out_weight.shape[1]
+    side = jax.ShapeDtypeStruct((columns, shard_rows, out_width), jnp.bfloat16)
+    return call(
+        first_body,
+        [side, side],
+        [
+            where_at,
+            sink_logits,
+            query_states[:WINDOW],
+            key_states[:WINDOW],
+            value_states[:WINDOW],
+            segment_rows,
+            tail,
+            later,
+            out_weight,
+        ],
+        [SMEM, SMEM] + [VMEM] * 7,
+        [pltpu.VMEM((tokens, width), jnp.bfloat16)] + scratch,
+        flops + 2 * tokens * width * out_width,
+        24 << 20,
+    )
+
+
+def chip_body(at_ref, kept_ref, taken_ref, residual_ref, hidden_ref, *away_refs):
+    columns = kept_ref.shape[0]
+    column = at_ref[0]
+    total = kept_ref[column].astype(jnp.float32) + taken_ref[column].astype(jnp.float32)
+    hidden_ref[...] = residual_ref[...].astype(jnp.float32) + total
+    for step, away_ref in enumerate(away_refs):
+        target = lax.rem(column + step + 1, columns)
+        total = kept_ref[target].astype(jnp.float32) + taken_ref[target].astype(jnp.float32)
+        away_ref[...] = total.astype(away_ref.dtype)
+
+
+def norm_body(count, experts, partial_ref, gain_ref, ids_ref, route_ref, *refs):
+    arrived = refs[:count]
+    hidden_ref, packed_ref = refs[count:]
+    hidden = partial_ref[...]
+    for ref in arrived:
+        hidden = hidden + ref[...].astype(jnp.float32)
+    hidden_ref[...] = hidden
+    width = hidden.shape[1]
+    variance = jnp.mean(hidden * hidden, -1, keepdims=True)
+    normed = hidden * lax.rsqrt(variance + 1e-05) * gain_ref[...]
+    packed_ref[:, :width] = normed.astype(packed_ref.dtype)
+    lane = lax.broadcasted_iota(jnp.int32, (hidden.shape[0], LANES), 1)
+    name = lax.rem(lane, experts)
+    dense = jnp.zeros((hidden.shape[0], LANES), jnp.float32)
+    for choice in range(ids_ref.shape[1]):
+        ids = ids_ref[:, choice : choice + 1]
+        dense = dense + jnp.where(ids == name, route_ref[:, choice : choice + 1], 0.0)
+    high = dense.astype(jnp.bfloat16)
+    rest = dense - high.astype(jnp.float32)
+    middle = rest.astype(jnp.bfloat16)
+    low = (rest - middle.astype(jnp.float32)).astype(jnp.bfloat16)
+    third = lane // experts
+    coded = jnp.where(
+        third == 0,
+        high.astype(jnp.float32),
+        jnp.where(
+            third == 1,
+            middle.astype(jnp.float32),
+            jnp.where(third == 2, low.astype(jnp.float32), 0.0),
+        ),
+    )
+    packed_ref[:, width:] = coded.astype(packed_ref.dtype)
+
+
+def ffn_body(experts, expert_ref, gate_ref, up_ref, down_ref, *refs):
+    ins, (keep_ref, give_ref, rows_ref, act_ref) = refs[:-4], refs[-4:]
+    width, hidden = gate_ref.shape[1], gate_ref.shape[2]
+    half = keep_ref.shape[0]
+    expert = expert_ref[0]
+    scales = []
+    start = 0
+    for ref in ins:
+        count = ref.shape[0]
+        rows_ref[start : start + count, :] = ref[:, :width]
+        coded = ref[:, width:].astype(jnp.float32)
+        lane = lax.broadcasted_iota(jnp.int32, coded.shape, 1)
+        mine = (lane == expert) | (lane == expert + experts) | (lane == expert + 2 * experts)
+        scales.append(jnp.sum(jnp.where(mine, coded, 0.0), -1, keepdims=True))
+        start += count
+    scale = jnp.concatenate(scales, 0)
+    tile = 256 if hidden % 256 == 0 else hidden
+    for low in range(0, hidden, tile):
+        cols = slice(low, low + tile)
+        gate_val = jnp.minimum(
+            jnp.dot(rows_ref[...], gate_ref[0, :, cols], preferred_element_type=jnp.float32), 7.0
+        )
+        up_val = jnp.clip(
+            jnp.dot(rows_ref[...], up_ref[0, :, cols], preferred_element_type=jnp.float32),
+            -7.0,
+            7.0,
+        )
+        act_ref[:, cols] = ((up_val + 1.0) * gate_val * jax.nn.sigmoid(1.702 * gate_val)).astype(
+            act_ref.dtype
+        )
+    tile = 512 if width % 512 == 0 else width
+    for low in range(0, width, tile):
+        cols = slice(low, low + tile)
+        value = jnp.dot(act_ref[...], down_ref[0, :, cols], preferred_element_type=jnp.float32)
+        value = (value * scale).astype(keep_ref.dtype)
+        keep_ref[:, cols] = value[:half]
+        give_ref[:, cols] = value[half:]
+
+
+def ring_layer(
+    query_states,
+    key_states,
+    value_states,
+    sink_logits,
+    segment_ids,
+    residual,
+    out_weight,
+    norm_gain,
+    expert_ids,
+    route_weights,
+    gate_proj,
+    up_proj,
+    down_proj,
+):
+    shard_rows, width = residual.shape
+    hidden_units = gate_proj.shape[2]
+    seq, head = lax.axis_size("seq"), lax.axis_size("head")
+    columns = head // 2
+    chips = seq * columns
+    column = lax.axis_index("head") // 2
+
+    order = [
+        (col, row if col % 2 == 0 else seq - 1 - row) for col in range(columns) for row in range(seq)
+    ]
+
+    def device(place, which):
+        col, row = order[place % chips]
+        return row * head + col * 2 + which
+
+    onward = [(device(p, c), device(p + 1, c)) for p in range(chips) for c in range(2)]
+    back = [(b, a) for a, b in onward]
+
+    def ring(pair):
+        on = lax.ppermute(pair[0], ("seq", "head"), onward)
+        off = lax.ppermute(pair[1], ("seq", "head"), back)
+        return on, off
+
+    def swap(value):
+        return partner(value, "head", 0)
+
+    kept, given = projected_heads(
+        query_states, key_states, value_states, sink_logits, segment_ids, out_weight, shard_rows
+    )
+    rows_f32 = jax.ShapeDtypeStruct((shard_rows, width), jnp.float32)
+    rows_bf16 = jax.ShapeDtypeStruct((shard_rows, width), jnp.bfloat16)
+    hidden_state, *away = call(
+        chip_body,
+        [rows_f32] + [rows_bf16] * (columns - 1),
+        [column.reshape(1), kept, swap(given), residual],
+        [SMEM] + [VMEM] * 3,
+    )
+    arrived = []
+    for step, value in enumerate(away):
+        pairs = [(i, (i + 2 * (step + 1)) % head) for i in range(head)]
+        arrived.append(lax.ppermute(value, "head", pairs))
+    packed_width = width + LANES
+    hidden_state, mine = call(
+        functools.partial(norm_body, len(arrived), chips),
+        [rows_f32, jax.ShapeDtypeStruct((shard_rows, packed_width), jnp.bfloat16)],
+        [hidden_state, norm_gain.reshape(1, -1), expert_ids, route_weights] + arrived,
+        [VMEM] * (4 + len(arrived)),
+    )
+
+    expert = (lax.axis_index("seq") * columns + column).reshape(1)
+
+    def terms(blocks):
+        rows = 2 * sum(block.shape[0] for block in blocks)
+        others = [swap(block) for block in blocks]
+        out = jax.ShapeDtypeStruct((rows // 2, width), jnp.bfloat16)
+        keep, give = call(
+            functools.partial(ffn_body, chips),
+            [out, out],
+            [expert, gate_proj, up_proj, down_proj] + blocks + others,
+            [SMEM] + [VMEM] * (3 + 2 * len(blocks)),
+            [
+                pltpu.VMEM((rows, width), jnp.bfloat16),
+                pltpu.VMEM((rows, hidden_units), jnp.bfloat16),
+            ],
+            6 * rows * width * hidden_units,
+            24 << 20,
+        )
+        taken = swap(give)
+        return keep.astype(jnp.float32) + taken.astype(jnp.float32)
+
+    half = shard_rows // 2
+    own_term = terms([mine])
+    sums = []
+    travelling = (mine, mine)
+    for _ in range(1, chips // 2):
+        travelling = ring(travelling)
+        sums.append(terms(list(travelling)))
+    travelling = ring((travelling[0][:half], travelling[1][half:]))
+    total = terms(list(travelling)).astype(jnp.bfloat16)
+    passing = ring((total[:half], total[half:]))
+    for total in reversed(sums):
+        on, off = (value.astype(jnp.float32) for value in passing)
+        if on.shape[0] < shard_rows:
+            on = jnp.pad(on, ((0, half), (0, 0)))
+            off = jnp.pad(off, ((half, 0), (0, 0)))
+        on = (total[shard_rows:] + on).astype(jnp.bfloat16)
+        off = (total[:shard_rows] + off).astype(jnp.bfloat16)
+        passing = ring((on, off))
+    on, off = (value.astype(jnp.float32) for value in passing)
+    if on.shape[0] < shard_rows:
+        on = jnp.concatenate([on, off], 0)
+        off = 0.0
+    return (hidden_state + (on + off + own_term)).astype(jnp.bfloat16)
+
+
+def per_device(query_states, key_states, value_states, sink_logits, segment_ids, *rest):
+    residual, _, _, expert_ids = rest[:4]
+    seq, head, pair = lax.axis_size("seq"), lax.axis_size("head"), lax.axis_size("pair")
+    experts = seq * head // 2
+    dense_pays = 2 * expert_ids.shape[1] >= experts
+    ring_fits = pair == 1 and head % 2 == 0 and experts % 2 == 0 and 3 * experts <= LANES
+    shard_rows = residual.shape[0]
+    tokens, width = query_states.shape
+    kv_width = key_states.shape[1]
+    rows_fit = shard_rows % 32 == 0 and tokens % WINDOW == 0 and WINDOW % min(shard_rows, WINDOW) == 0
+    heads_fit = kv_width % LANES == 0 and width % (2 * kv_width) == 0
+    if dense_pays and ring_fits and rows_fit and heads_fit:
+        return ring_layer(query_states, key_states, value_states, sink_logits, segment_ids, *rest)
+    attended = attention(query_states, key_states, value_states, sink_logits, segment_ids)
+    return exchanged_layer(attended, *rest)
+
+
 def solution(mesh):
     in_specs = (
         P(("group", "seq"), ("head", "pair")),

time: 175 us -> 99.6 us (0.57)
  the two profiles are of different devices: /device:TPU:11 before, /device:TPU:0 now
where the time goes in v1:
time: 99.6 us; the launch traced here: 99 us
  waiting for transfers between devices  36.7 us (37%)
  starting transfers between devices  27.3 us (27%)
  Pallas kernels  17.7 us (18%)
  local copies, waits for them, and re-layouts  15.6 us (16%)
  other arithmetic  1.41 us (1%)
    ppermute x8, waiting for transfers between devices, ring(): on = lax.ppermute(pair[0], ('seq', 'head'), onward)  24.9 us
    pallas_call x9, Pallas kernels, call(): pl.pallas_call(body, out_shape=outs, in_specs=specs, out_specs=jax.tree.m...  17.7 us
    unnamed x36, local copies, waits for them, and re-layouts  12.5 us
    ppermute x8, starting transfers between devices, ring(): on = lax.ppermute(pair[0], ('seq', 'head'), onward)  11.2 us
    ppermute x8, starting transfers between devices, ring(): off = lax.ppermute(pair[1], ('seq', 'head'), back)  6.03 us
    ppermute x1, waiting for transfers between devices, ring_layer(): arrived.append(lax.ppermute(value, 'head', pairs))  5.45 us
    ppermute x1, starting transfers between devices, passed_along(): return lax.ppermute(value, axis, pairs)  4.96 us
    ppermute x8, waiting for transfers between devices, ring(): off = lax.ppermute(pair[1], ('seq', 'head'), back)  4.58 us
  transfers between devices with their start and end apart: 33, of which 14 were waited for; matrix products, arithmetic and copies ran while one was open for 3% of the time, Pallas kernels for 14%

profile of v1, /device:TPU:0, one launch (start us, length us, event | category | flops | bytes accessed | tf_op | source)
XLA Modules:
  0.0 99.0 jit_solution(5919644395388679989)
XLA Ops:
  0.0 0.8 fusion.7
  0.8 5.0 %collective-permute-start = (bf16[128,256]{1,0:T(8,128)(2,1)S(1)}, bf16[128,256]{1,0:T(8,128)(2,1)S(1)}, u32[]{:S(2)}, u32[]{:S(2)}) collective-permute-start(bf16[128,256]{1,0:T(8,128)(2,1)S(1)} %pad_maximum_fusion), channel_id=1, source_target_pairs={{0,4},{4,8},{8,12},{1,5},{5,9},{9,13},{2,6},{6,10},{10,14},{3,7},{... | collective-permute-start | bytes 196616 | tf_op jit(solution)/shard_map/ppermute | solution.py:21
  5.9 1.0 slice.45.query_ref
  6.9 1.0 %copy-done.6 = bf16[256,1024]{1,0:T(8,128)(2,1)S(1)} copy-done((bf16[256,1024]{1,0:T(8,128)(2,1)S(1)}, bf16[256,1024]{1,0:T(8,128)(2,1)}, u32[]{:S(2)}) %copy-start.6) | copy-done | bytes 524312
  7.9 0.8 copy-done.7
  8.8 0.8 copy-done.8
  9.6 0.7 copy-done.10
  10.3 0.7 copy-done.12
  10.9 1.8 %shard_map.127.later_ref = bf16[128,1024]{1,0:T(8,128)(2,1)S(1)} custom-call(s32[2]{0:T(128)S(1)} %pad_add_fusion.seq_ref, f32[16]{0:T(128)S(1)} %copy-done.12, bf16[256,1024]{1,0:T(8,128)(2,1)S(1)} %copy-done.6, bf16[256,128]{1,0:T(8,128)(2,1)S(1)} %copy-done.7, bf16[256,128]{1,0:T(8,128)(2,1)S(1)} %copy-done.8, s32[8,128]{1,0:T(8,128)S(1)} %bitcast.5), custom_call_target="tpu_custom_call" | custom-call | flops 268435456 | bytes 659528 | tf_op jit(solution)/shard_map/pallas_call | solution.py:355
  12.7 1.9 %copy-done.9 = bf16[1024,1536]{1,0:T(8,128)(2,1)S(1)} copy-done((bf16[1024,1536]{1,0:T(8,128)(2,1)S(1)}, bf16[1024,1536]{1,0:T(8,128)(2,1)}, u32[]{:S(2)}) %copy-start.9) | copy-done | bytes 3145752
  14.6 0.7 copy-done.11
  15.3 0.7 copy-done.13
  16.0 2.7 %shard_map.128 = (bf16[2,64,1536]{2,1,0:T(8,128)(2,1)S(1)}, bf16[2,64,1536]{2,1,0:T(8,128)(2,1)S(1)}) custom-call(s32[2]{0:T(128)S(1)} %pad_add_fusion.seq_ref, f32[16]{0:T(128)S(1)} %copy-done.13, bf16[128,1024]{1,0:T(8,128)(2,1)S(1)} %slice.45.query_ref, bf16[128,128]{1,0:T(8,128)(2,1)S(1)} %get-tuple-element.46.key_ref, ...), custom_call_target="tpu_custom_call" | custom-call | flops 1073741824 | bytes 3805256 | tf_op jit(solution)/shard_map/pallas_call | solution.py:355
  18.7 1.7 %collective-permute-done.1.taken_ref = bf16[2,64,1536]{2,1,0:T(8,128)(2,1)S(1)} collective-permute-done((bf16[2,64,1536]{2,1,0:T(8,128)(2,1)S(1)}, bf16[2,64,1536]{2,1,0:T(8,128)(2,1)S(1)}, u32[]{:S(2)}, u32[]{:S(2)}) %collective-permute-start.1) | collective-permute-done | bytes 393248 | tf_op jit(solution)/shard_map/ppermute | solution.py:25
  20.4 0.9 copy-done.5
  21.3 0.7 shard_map.129
  22.1 1.5 %collective-permute-start.2 = (bf16[64,1536]{1,0:T(8,128)(2,1)}, bf16[64,1536]{1,0:T(8,128)(2,1)S(1)}, u32[]{:S(2)}, u32[]{:S(2)}) collective-permute-start(bf16[64,1536]{1,0:T(8,128)(2,1)} %get-tuple-element.24), channel_id=1, source_target_pairs={{0,2},{1,3},{2,0},{3,1},{4,6},{5,7},{6,4},{7,5},{8,10},{9,11},{10,... | collective-permute-start | bytes 589832 | tf_op jit(solution)/shard_map/ppermute | solution.py:557
  23.8 5.5 %collective-permute-done.2.refs_0_ = bf16[64,1536]{1,0:T(8,128)(2,1)S(1)} collective-permute-done((bf16[64,1536]{1,0:T(8,128)(2,1)}, bf16[64,1536]{1,0:T(8,128)(2,1)S(1)}, u32[]{:S(2)}, u32[]{:S(2)}) %collective-permute-start.2) | collective-permute-done | bytes 196640 | tf_op jit(solution)/shard_map/ppermute | solution.py:557
  29.2 0.9 shard_map.130
  30.2 0.7 copy-done.3
  30.9 1.6 %collective-permute-start.3 = (bf16[64,1664]{1,0:T(8,128)(2,1)}, bf16[64,1664]{1,0:T(8,128)(2,1)S(1)}, u32[]{:S(2)}, u32[]{:S(2)}) collective-permute-start(bf16[64,1664]{1,0:T(8,128)(2,1)} %get-tuple-element.26.refs_0_), channel_id=1, source_target_pairs={{0,4},{1,5},{4,8},{5,9},{8,12},{9,13},{12,14},{13,15},{14,10},{15,... | collective-permute-start | bytes 638984 | tf_op jit(solution)/shard_map/ppermute | solution.py:536
  32.5 0.4 collective-permute-start.4
  32.9 4.6 %collective-permute-done.3.refs_0_ = bf16[64,1664]{1,0:T(8,128)(2,1)S(1)} collective-permute-done((bf16[64,1664]{1,0:T(8,128)(2,1)}, bf16[64,1664]{1,0:T(8,128)(2,1)S(1)}, u32[]{:S(2)}, u32[]{:S(2)}) %collective-permute-start.3) | collective-permute-done | bytes 213024 | tf_op jit(solution)/shard_map/ppermute | solution.py:536
  37.6 1.6 %collective-permute-start.8 = (bf16[64,1664]{1,0:T(8,128)(2,1)S(1)}, bf16[64,1664]{1,0:T(8,128)(2,1)S(1)}, u32[]{:S(2)}, u32[]{:S(2)}) collective-permute-start(bf16[64,1664]{1,0:T(8,128)(2,1)S(1)} %collective-permute-done.3.refs_0_), channel_id=1, source_target_pairs={{0,4},{1,5},{4,8},{5,9},{8,12},{9,13},{12,14},{13,15},{14,10},{15,... | collective-permute-start | bytes 638984 | tf_op jit(solution)/shard_map/ppermute | solution.py:536
  39.1 0.4 collective-permute-start.9
  39.6 3.9 %collective-permute-done.8.refs_0_ = bf16[64,1664]{1,0:T(8,128)(2,1)S(1)} collective-permute-done((bf16[64,1664]{1,0:T(8,128)(2,1)S(1)}, bf16[64,1664]{1,0:T(8,128)(2,1)S(1)}, u32[]{:S(2)}, u32[]{:S(2)}) %collective-permute-start.8) | collective-permute-done | bytes 213024 | tf_op jit(solution)/shard_map/ppermute | solution.py:536
  43.5 1.6 %collective-permute-start.13 = (bf16[64,1664]{1,0:T(8,128)(2,1)S(1)}, bf16[64,1664]{1,0:T(8,128)(2,1)S(1)}, u32[]{:S(2)}, u32[]{:S(2)}) collective-permute-start(bf16[64,1664]{1,0:T(8,128)(2,1)S(1)} %collective-permute-done.8.refs_0_), channel_id=1, source_target_pairs={{0,4},{1,5},{4,8},{5,9},{8,12},{9,13},{12,14},{13,15},{14,10},{15,... | collective-permute-start | bytes 638984 | tf_op jit(solution)/shard_map/ppermute | solution.py:536
  45.1 0.2 collective-permute-done.9.refs_1_
  45.3 0.4 collective-permute-start.14
  45.8 0.5 collective-permute-start.5
  46.3 3.1 %collective-permute-done.13.refs_0_ = bf16[64,1664]{1,0:T(8,128)(2,1)S(1)} collective-permute-done((bf16[64,1664]{1,0:T(8,128)(2,1)S(1)}, bf16[64,1664]{1,0:T(8,128)(2,1)S(1)}, u32[]{:S(2)}, u32[]{:S(2)}) %collective-permute-start.13) | collective-permute-done | bytes 213024 | tf_op jit(solution)/shard_map/ppermute | solution.py:536
  49.4 0.7 slice.63
  50.0 1.6 %collective-permute-start.18 = (bf16[32,1664]{1,0:T(8,128)(2,1)}, bf16[32,1664]{1,0:T(8,128)(2,1)S(1)}, u32[]{:S(2)}, u32[]{:S(2)}) collective-permute-start(bf16[32,1664]{1,0:T(8,128)(2,1)} %slice.63), channel_id=1, source_target_pairs={{0,4},{1,5},{4,8},{5,9},{8,12},{9,13},{12,14},{13,15},{14,10},{15,... | collective-permute-start | bytes 319496 | tf_op jit(solution)/shard_map/ppermute | solution.py:536
  51.6 0.6 slice.64
  52.2 0.4 collective-permute-start.19
  52.7 1.7 %copy-done.1 = bf16[1,1536,768]{2,1,0:T(8,128)(2,1)S(1)} copy-done((bf16[1,1536,768]{2,1,0:T(8,128)(2,1)S(1)}, bf16[1,1536,768]{2,1,0:T(8,128)(2,1)}, u32[]{:S(2)}) %copy-start.1) | copy-done | bytes 2359320
  54.4 1.7 %copy-done.2 = bf16[1,768,1536]{2,1,0:T(8,128)(2,1)S(1)} copy-done((bf16[1,768,1536]{2,1,0:T(8,128)(2,1)S(1)}, bf16[1,768,1536]{2,1,0:T(8,128)(2,1)}, u32[]{:S(2)}) %copy-start.2) | copy-done | bytes 2359320
  56.0 2.2 %shard_map.135 = (bf16[64,1536]{1,0:T(8,128)(2,1)S(1)}, bf16[64,1536]{1,0:T(8,128)(2,1)S(1)}) custom-call(s32[1]{0:T(128)} %bitcast.4.expert_ref, bf16[1,1536,768]{2,1,0:T(8,128)(2,1)S(1)} %copy-done, bf16[1,1536,768]{2,1,0:T(8,128)(2,1)S(1)} %copy-done.1, bf16[1,768,1536]{2,1,0:T(8,128)(2,1)S(1)} %copy-done.2, bf16[64,1664]{1,0:T(8,128)(2,1)} %get-tuple-element.26.refs_0_, ...), custom_call_target="tpu_custom_call" | custom-call | flops 905969664 | bytes 7503876 | tf_op jit(solution)/shard_map/pallas_call | solution.py:355
  58.3 0.5 collective-permute-start.10
  58.9 0.4 collective-permute-start.20
  59.4 3.2 %shard_map.131 = (bf16[128,1536]{1,0:T(8,128)(2,1)S(1)}, bf16[128,1536]{1,0:T(8,128)(2,1)S(1)}) custom-call(s32[1]{0:T(128)} %bitcast.4.expert_ref, bf16[1,1536,768]{2,1,0:T(8,128)(2,1)S(1)} %copy-done, bf16[1,1536,768]{2,1,0:T(8,128)(2,1)S(1)} %copy-done.1, bf16[1,768,1536]{2,1,0:T(8,128)(2,1)S(1)} %copy-done.2, ...), custom_call_target="tpu_custom_call" | custom-call | flops 1811939328 | bytes 7929860 | tf_op jit(solution)/shard_map/pallas_call | solution.py:355
  62.7 0.5 collective-permute-start.15
  63.3 2.1 %shard_map.134 = (bf16[64,1536]{1,0:T(8,128)(2,1)S(1)}, bf16[64,1536]{1,0:T(8,128)(2,1)S(1)}) custom-call(s32[1]{0:T(128)} %bitcast.4.expert_ref, bf16[1,1536,768]{2,1,0:T(8,128)(2,1)S(1)} %copy-done, bf16[1,1536,768]{2,1,0:T(8,128)(2,1)S(1)} %copy-done.1, bf16[1,768,1536]{2,1,0:T(8,128)(2,1)S(1)} %copy-done.2, ...), custom_call_target="tpu_custom_call" | custom-call | flops 905969664 | bytes 7503876 | tf_op jit(solution)/shard_map/pallas_call | solution.py:355
  65.3 0.5 collective-permute-start.7
  65.9 2.1 %shard_map.132 = (bf16[128,1536]{1,0:T(8,128)(2,1)S(1)}, bf16[128,1536]{1,0:T(8,128)(2,1)S(1)}) custom-call(s32[1]{0:T(128)} %bitcast.4.expert_ref, bf16[1,1536,768]{2,1,0:T(8,128)(2,1)S(1)} %copy-done, bf16[1,1536,768]{2,1,0:T(8,128)(2,1)S(1)} %copy-done.1, bf16[1,768,1536]{2,1,0:T(8,128)(2,1)S(1)} %copy-done.2, ...), custom_call_target="tpu_custom_call" | custom-call | flops 1811939328 | bytes 7929860 | tf_op jit(solution)/shard_map/pallas_call | solution.py:355
  68.0 0.5 collective-permute-start.12
  68.5 2.1 %shard_map.133 = (bf16[128,1536]{1,0:T(8,128)(2,1)S(1)}, bf16[128,1536]{1,0:T(8,128)(2,1)S(1)}) custom-call(s32[1]{0:T(128)} %bitcast.4.expert_ref, bf16[1,1536,768]{2,1,0:T(8,128)(2,1)S(1)} %copy-done, bf16[1,1536,768]{2,1,0:T(8,128)(2,1)S(1)} %copy-done.1, bf16[1,768,1536]{2,1,0:T(8,128)(2,1)S(1)} %copy-done.2, ...), custom_call_target="tpu_custom_call" | custom-call | flops 1811939328 | bytes 7929860 | tf_op jit(solution)/shard_map/pallas_call | solution.py:355
  70.8 1.6 %collective-permute-start.23 = (bf16[32,1536]{1,0:T(8,128)(2,1)S(1)}, bf16[32,1536]{1,0:T(8,128)(2,1)S(1)}, u32[]{:S(2)}, u32[]{:S(2)}) collective-permute-start(bf16[32,1536]{1,0:T(8,128)(2,1)S(1)} %get-tuple-element.43), channel_id=1, source_target_pairs={{0,4},{1,5},{4,8},{5,9},{8,12},{9,13},{12,14},{13,15},{14,10},{15,... | collective-permute-start | bytes 294920 | tf_op jit(solution)/shard_map/ppermute | solution.py:536
  72.5 1.3 %collective-permute-start.27 = (bf16[32,1536]{1,0:T(8,128)(2,1)S(1)}, bf16[32,1536]{1,0:T(8,128)(2,1)S(1)}, u32[]{:S(2)}, u32[]{:S(2)}) collective-permute-start(bf16[32,1536]{1,0:T(8,128)(2,1)S(1)} %get-tuple-element.44), channel_id=1, source_target_pairs={{4,0},{5,1},{8,4},{9,5},{12,8},{13,9},{14,12},{15,13},{10,14},{11,... | collective-permute-start | bytes 294920 | tf_op jit(solution)/shard_map/ppermute | solution.py:537
  73.9 2.1 %collective-permute-done.23 = bf16[32,1536]{1,0:T(8,128)(2,1)S(1)} collective-permute-done((bf16[32,1536]{1,0:T(8,128)(2,1)S(1)}, bf16[32,1536]{1,0:T(8,128)(2,1)S(1)}, u32[]{:S(2)}, u32[]{:S(2)}) %collective-permute-start.23) | collective-permute-done | bytes 98336 | tf_op jit(solution)/shard_map/ppermute | solution.py:536
  76.0 1.3 %collective-permute-done.27 = bf16[32,1536]{1,0:T(8,128)(2,1)S(1)} collective-permute-done((bf16[32,1536]{1,0:T(8,128)(2,1)S(1)}, bf16[32,1536]{1,0:T(8,128)(2,1)S(1)}, u32[]{:S(2)}, u32[]{:S(2)}) %collective-permute-start.27) | collective-permute-done | bytes 98336 | tf_op jit(solution)/shard_map/ppermute | solution.py:537
  77.4 1.5 %collective-permute-start.24 = (bf16[64,1536]{1,0:T(8,128)(2,1)S(1)}, bf16[64,1536]{1,0:T(8,128)(2,1)S(1)}, u32[]{:S(2)}, u32[]{:S(2)}) collective-permute-start(bf16[64,1536]{1,0:T(8,128)(2,1)S(1)} %get-tuple-element.41), channel_id=1, source_target_pairs={{0,4},{1,5},{4,8},{5,9},{8,12},{9,13},{12,14},{13,15},{14,10},{15,... | collective-permute-start | bytes 589832 | tf_op jit(solution)/shard_map/ppermute | solution.py:536
  78.9 0.5 collective-permute-start.28
  79.6 4.0 %collective-permute-done.24 = bf16[64,1536]{1,0:T(8,128)(2,1)S(1)} collective-permute-done((bf16[64,1536]{1,0:T(8,128)(2,1)S(1)}, bf16[64,1536]{1,0:T(8,128)(2,1)S(1)}, u32[]{:S(2)}, u32[]{:S(2)}) %collective-permute-start.24) | collective-permute-done | bytes 196640 | tf_op jit(solution)/shard_map/ppermute | solution.py:536
  83.5 1.2 %collective-permute-done.28 = bf16[64,1536]{1,0:T(8,128)(2,1)S(1)} collective-permute-done((bf16[64,1536]{1,0:T(8,128)(2,1)S(1)}, bf16[64,1536]{1,0:T(8,128)(2,1)S(1)}, u32[]{:S(2)}, u32[]{:S(2)}) %collective-permute-start.28) | collective-permute-done | bytes 196640 | tf_op jit(solution)/shard_map/ppermute | solution.py:537
  84.8 1.5 %collective-permute-start.25 = (bf16[64,1536]{1,0:T(8,128)(2,1)S(1)}, bf16[64,1536]{1,0:T(8,128)(2,1)S(1)}, u32[]{:S(2)}, u32[]{:S(2)}) collective-permute-start(bf16[64,1536]{1,0:T(8,128)(2,1)S(1)} %get-tuple-element.39), channel_id=1, source_target_pairs={{0,4},{1,5},{4,8},{5,9},{8,12},{9,13},{12,14},{13,15},{14,10},{15,... | collective-permute-start | bytes 589832 | tf_op jit(solution)/shard_map/ppermute | solution.py:536
  86.3 0.6 collective-permute-start.29
  87.0 3.5 %collective-permute-done.25 = bf16[64,1536]{1,0:T(8,128)(2,1)S(1)} collective-permute-done((bf16[64,1536]{1,0:T(8,128)(2,1)S(1)}, bf16[64,1536]{1,0:T(8,128)(2,1)S(1)}, u32[]{:S(2)}, u32[]{:S(2)}) %collective-permute-start.25) | collective-permute-done | bytes 196640 | tf_op jit(solution)/shard_map/ppermute | solution.py:536
  90.5 1.7 %collective-permute-done.29 = bf16[64,1536]{1,0:T(8,128)(2,1)S(1)} collective-permute-done((bf16[64,1536]{1,0:T(8,128)(2,1)S(1)}, bf16[64,1536]{1,0:T(8,128)(2,1)S(1)}, u32[]{:S(2)}, u32[]{:S(2)}) %collective-permute-start.29) | collective-permute-done | bytes 196640 | tf_op jit(solution)/shard_map/ppermute | solution.py:537
  92.3 0.2 collective-permute-start.26
  92.5 1.8 %collective-permute-start.30 = (bf16[64,1536]{1,0:T(8,128)(2,1)S(1)}, bf16[64,1536]{1,0:T(8,128)(2,1)S(1)}, u32[]{:S(2)}, u32[]{:S(2)}) collective-permute-start(bf16[64,1536]{1,0:T(8,128)(2,1)S(1)} %get-tuple-element.38), channel_id=1, source_target_pairs={{4,0},{5,1},{8,4},{9,5},{12,8},{13,9},{14,12},{15,13},{10,14},{11,... | collective-permute-start | bytes 589832 | tf_op jit(solution)/shard_map/ppermute | solution.py:537
  94.3 3.6 %collective-permute-done.26 = bf16[64,1536]{1,0:T(8,128)(2,1)S(1)} collective-permute-done((bf16[64,1536]{1,0:T(8,128)(2,1)S(1)}, bf16[64,1536]{1,0:T(8,128)(2,1)S(1)}, u32[]{:S(2)}, u32[]{:S(2)}) %collective-permute-start.26) | collective-permute-done | bytes 196640 | tf_op jit(solution)/shard_map/ppermute | solution.py:536
  98.0 0.2 collective-permute-done.30
  98.2 0.8 add_convert_fusion
  (63 shorter events, 1.6 us)
Async XLA Ops:
  0.8 11.9 %collective-permute-start = (bf16[128,256]{1,0:T(8,128)(2,1)S(1)}, bf16[128,256]{1,0:T(8,128)(2,1)S(1)}, u32[]{:S(2)}, u32[]{:S(2)}) collective-permute-start(bf16[128,256]{1,0:T(8,128)(2,1)S(1)} %pad_maximum_fusion), channel_id=1, source_target_pairs={{0,4},{4,8},{8,12},{1,5},{5,9},{9,13},{2,6},{6,10},{10,14},{3,7},{... | collective-permute-start | bytes 196616 | tf_op jit(solution)/shard_map/ppermute | solution.py:21
  6.9 1.0 %copy-start.6 = (bf16[256,1024]{1,0:T(8,128)(2,1)S(1)}, bf16[256,1024]{1,0:T(8,128)(2,1)}, u32[]{:S(2)}) copy-start(bf16[256,1024]{1,0:T(8,128)(2,1)} %query_ref.1) | copy-start | bytes 1572868
  7.9 0.8 copy-start.7
  8.8 0.8 copy-start.8
  9.6 0.7 copy-start.10
  10.3 0.7 copy-start.12
  12.7 1.9 %copy-start.9 = (bf16[1024,1536]{1,0:T(8,128)(2,1)S(1)}, bf16[1024,1536]{1,0:T(8,128)(2,1)}, u32[]{:S(2)}) copy-start(bf16[1024,1536]{1,0:T(8,128)(2,1)} %weight_ref.1) | copy-start | bytes 9437188
  14.6 0.7 copy-start.11
  15.3 0.7 copy-start.13
  15.9 7.6 %copy-start.15 = (s32[64,4]{0,1:T(4,128)S(1)}, s32[64,4]{0,1:T(4,128)}, u32[]{:S(2)}) copy-start(s32[64,4]{0,1:T(4,128)} %param.21) | copy-start | bytes 3076
  15.9 7.7 %copy-start.16 = (f32[64,4]{0,1:T(4,128)S(1)}, f32[64,4]{0,1:T(4,128)}, u32[]{:S(2)}) copy-start(f32[64,4]{0,1:T(4,128)} %param.22) | copy-start | bytes 3076
  16.0 7.8 %copy-start.14 = (f32[1536]{0:T(1024)S(1)}, f32[1536]{0:T(1024)}, u32[]{:S(2)}) copy-start(f32[1536]{0:T(1024)} %param.20) | copy-start | bytes 18436
  16.0 36.7 %copy-start = (bf16[1,1536,768]{2,1,0:T(8,128)(2,1)S(1)}, bf16[1,1536,768]{2,1,0:T(8,128)(2,1)}, u32[]{:S(2)}) copy-start(bf16[1,1536,768]{2,1,0:T(8,128)(2,1)} %gate_ref.9) | copy-start | bytes 7077892
  18.6 1.8 %collective-permute-start.1 = (bf16[2,64,1536]{2,1,0:T(8,128)(2,1)S(1)}, bf16[2,64,1536]{2,1,0:T(8,128)(2,1)S(1)}, u32[]{:S(2)}, u32[]{:S(2)}) collective-permute-start(bf16[2,64,1536]{2,1,0:T(8,128)(2,1)S(1)} %get-tuple-element.22), channel_id=1, source_target_pairs={{0,1},{1,0},{2,3},{3,2},{4,5},{5,4},{6,7},{7,6},{8,9},{9,8},{10,11... | collective-permute-start | bytes 1179656 | tf_op jit(solution)/shard_map/ppermute | solution.py:25
  20.4 0.9 copy-start.5
  22.1 7.2 %collective-permute-start.2 = (bf16[64,1536]{1,0:T(8,128)(2,1)}, bf16[64,1536]{1,0:T(8,128)(2,1)S(1)}, u32[]{:S(2)}, u32[]{:S(2)}) collective-permute-start(bf16[64,1536]{1,0:T(8,128)(2,1)} %get-tuple-element.24), channel_id=1, source_target_pairs={{0,2},{1,3},{2,0},{3,1},{4,6},{5,7},{6,4},{7,5},{8,10},{9,11},{10,... | collective-permute-start | bytes 589832 | tf_op jit(solution)/shard_map/ppermute | solution.py:557
  30.1 0.8 copy-start.3
  30.9 6.6 %collective-permute-start.3 = (bf16[64,1664]{1,0:T(8,128)(2,1)}, bf16[64,1664]{1,0:T(8,128)(2,1)S(1)}, u32[]{:S(2)}, u32[]{:S(2)}) collective-permute-start(bf16[64,1664]{1,0:T(8,128)(2,1)} %get-tuple-element.26.refs_0_), channel_id=1, source_target_pairs={{0,4},{1,5},{4,8},{5,9},{8,12},{9,13},{12,14},{13,15},{14,10},{15,... | collective-permute-start | bytes 638984 | tf_op jit(solution)/shard_map/ppermute | solution.py:536
  32.5 6.7 %collective-permute-start.4 = (bf16[64,1664]{1,0:T(8,128)(2,1)}, bf16[64,1664]{1,0:T(8,128)(2,1)}, u32[]{:S(2)}, u32[]{:S(2)}) collective-permute-start(bf16[64,1664]{1,0:T(8,128)(2,1)} %get-tuple-element.26.refs_0_), channel_id=1, source_target_pairs={{4,0},{5,1},{8,4},{9,5},{12,8},{13,9},{14,12},{15,13},{10,14},{11,... | collective-permute-start | bytes 638984 | tf_op jit(solution)/shard_map/ppermute | solution.py:537
  37.6 6.0 %collective-permute-start.8 = (bf16[64,1664]{1,0:T(8,128)(2,1)S(1)}, bf16[64,1664]{1,0:T(8,128)(2,1)S(1)}, u32[]{:S(2)}, u32[]{:S(2)}) collective-permute-start(bf16[64,1664]{1,0:T(8,128)(2,1)S(1)} %collective-permute-done.3.refs_0_), channel_id=1, source_target_pairs={{0,4},{1,5},{4,8},{5,9},{8,12},{9,13},{12,14},{13,15},{14,10},{15,... | collective-permute-start | bytes 638984 | tf_op jit(solution)/shard_map/ppermute | solution.py:536
  39.1 6.2 %collective-permute-start.9 = (bf16[64,1664]{1,0:T(8,128)(2,1)}, bf16[64,1664]{1,0:T(8,128)(2,1)S(1)}, u32[]{:S(2)}, u32[]{:S(2)}) collective-permute-start(bf16[64,1664]{1,0:T(8,128)(2,1)} %collective-permute-done.4.refs_1_), channel_id=1, source_target_pairs={{4,0},{5,1},{8,4},{9,5},{12,8},{13,9},{14,12},{15,13},{10,14},{11,... | collective-permute-start | bytes 638984 | tf_op jit(solution)/shard_map/ppermute | solution.py:537
  43.5 5.8 %collective-permute-start.13 = (bf16[64,1664]{1,0:T(8,128)(2,1)S(1)}, bf16[64,1664]{1,0:T(8,128)(2,1)S(1)}, u32[]{:S(2)}, u32[]{:S(2)}) collective-permute-start(bf16[64,1664]{1,0:T(8,128)(2,1)S(1)} %collective-permute-done.8.refs_0_), channel_id=1, source_target_pairs={{0,4},{1,5},{4,8},{5,9},{8,12},{9,13},{12,14},{13,15},{14,10},{15,... | collective-permute-start | bytes 638984 | tf_op jit(solution)/shard_map/ppermute | solution.py:536
  45.3 6.3 %collective-permute-start.14 = (bf16[64,1664]{1,0:T(8,128)(2,1)S(1)}, bf16[64,1664]{1,0:T(8,128)(2,1)S(1)}, u32[]{:S(2)}, u32[]{:S(2)}) collective-permute-start(bf16[64,1664]{1,0:T(8,128)(2,1)S(1)} %collective-permute-done.9.refs_1_), channel_id=1, source_target_pairs={{4,0},{5,1},{8,4},{9,5},{12,8},{13,9},{14,12},{15,13},{10,14},{11,... | collective-permute-start | bytes 638984 | tf_op jit(solution)/shard_map/ppermute | solution.py:537
  45.8 6.9 %collective-permute-start.31 = (bf16[64,1664]{1,0:T(8,128)(2,1)}, bf16[64,1664]{1,0:T(8,128)(2,1)}, u32[]{:S(2)}, u32[]{:S(2)}) collective-permute-start(bf16[64,1664]{1,0:T(8,128)(2,1)} %get-tuple-element.26.refs_0_), channel_id=1, source_target_pairs={{0,1},{1,0},{2,3},{3,2},{4,5},{5,4},{6,7},{7,6},{8,9},{9,8},{10,11... | collective-permute-start | bytes 638984 | tf_op jit(solution)/shard_map/ppermute | solution.py:25
  45.8 12.6 %collective-permute-start.5 = (bf16[64,1664]{1,0:T(8,128)(2,1)S(1)}, bf16[64,1664]{1,0:T(8,128)(2,1)}, u32[]{:S(2)}, u32[]{:S(2)}) collective-permute-start(bf16[64,1664]{1,0:T(8,128)(2,1)S(1)} %collective-permute-done.3.refs_0_), channel_id=1, source_target_pairs={{0,1},{1,0},{2,3},{3,2},{4,5},{5,4},{6,7},{7,6},{8,9},{9,8},{10,11... | collective-permute-start | bytes 638984 | tf_op jit(solution)/shard_map/ppermute | solution.py:25
  46.3 12.6 %collective-permute-start.6 = (bf16[64,1664]{1,0:T(8,128)(2,1)}, bf16[64,1664]{1,0:T(8,128)(2,1)}, u32[]{:S(2)}, u32[]{:S(2)}) collective-permute-start(bf16[64,1664]{1,0:T(8,128)(2,1)} %collective-permute-done.4.refs_1_), channel_id=1, source_target_pairs={{0,1},{1,0},{2,3},{3,2},{4,5},{5,4},{6,7},{7,6},{8,9},{9,8},{10,11... | collective-permute-start | bytes 638984 | tf_op jit(solution)/shard_map/ppermute | solution.py:25
  50.0 8.9 %collective-permute-start.18 = (bf16[32,1664]{1,0:T(8,128)(2,1)}, bf16[32,1664]{1,0:T(8,128)(2,1)S(1)}, u32[]{:S(2)}, u32[]{:S(2)}) collective-permute-start(bf16[32,1664]{1,0:T(8,128)(2,1)} %slice.63), channel_id=1, source_target_pairs={{0,4},{1,5},{4,8},{5,9},{8,12},{9,13},{12,14},{13,15},{14,10},{15,... | collective-permute-start | bytes 319496 | tf_op jit(solution)/shard_map/ppermute | solution.py:536
  52.2 7.1 %collective-permute-start.19 = (bf16[32,1664]{1,0:T(8,128)(2,1)}, bf16[32,1664]{1,0:T(8,128)(2,1)}, u32[]{:S(2)}, u32[]{:S(2)}) collective-permute-start(bf16[32,1664]{1,0:T(8,128)(2,1)} %slice.64), channel_id=1, source_target_pairs={{4,0},{5,1},{8,4},{9,5},{12,8},{13,9},{14,12},{15,13},{10,14},{11,... | collective-permute-start | bytes 319496 | tf_op jit(solution)/shard_map/ppermute | solution.py:537
  52.7 1.7 %copy-start.1 = (bf16[1,1536,768]{2,1,0:T(8,128)(2,1)S(1)}, bf16[1,1536,768]{2,1,0:T(8,128)(2,1)}, u32[]{:S(2)}) copy-start(bf16[1,1536,768]{2,1,0:T(8,128)(2,1)} %up_ref.9) | copy-start | bytes 7077892
  54.4 1.7 %copy-start.2 = (bf16[1,768,1536]{2,1,0:T(8,128)(2,1)S(1)}, bf16[1,768,1536]{2,1,0:T(8,128)(2,1)}, u32[]{:S(2)}) copy-start(bf16[1,768,1536]{2,1,0:T(8,128)(2,1)} %down_ref.9) | copy-start | bytes 7077892
  58.2 36.1 %collective-permute-start.32 = (bf16[64,1536]{1,0:T(8,128)(2,1)S(1)}, bf16[64,1536]{1,0:T(8,128)(2,1)S(1)}, u32[]{:S(2)}, u32[]{:S(2)}) collective-permute-start(bf16[64,1536]{1,0:T(8,128)(2,1)S(1)} %get-tuple-element.36), channel_id=1, source_target_pairs={{0,1},{1,0},{2,3},{3,2},{4,5},{5,4},{6,7},{7,6},{8,9},{9,8},{10,11... | collective-permute-start | bytes 589832 | tf_op jit(solution)/shard_map/ppermute | solution.py:25
  58.3 7.0 %collective-permute-start.10 = (bf16[64,1664]{1,0:T(8,128)(2,1)S(1)}, bf16[64,1664]{1,0:T(8,128)(2,1)S(1)}, u32[]{:S(2)}, u32[]{:S(2)}) collective-permute-start(bf16[64,1664]{1,0:T(8,128)(2,1)S(1)} %collective-permute-done.8.refs_0_), channel_id=1, source_target_pairs={{0,1},{1,0},{2,3},{3,2},{4,5},{5,4},{6,7},{7,6},{8,9},{9,8},{10,11... | collective-permute-start | bytes 638984 | tf_op jit(solution)/shard_map/ppermute | solution.py:25
  58.8 7.0 %collective-permute-start.11 = (bf16[64,1664]{1,0:T(8,128)(2,1)S(1)}, bf16[64,1664]{1,0:T(8,128)(2,1)S(1)}, u32[]{:S(2)}, u32[]{:S(2)}) collective-permute-start(bf16[64,1664]{1,0:T(8,128)(2,1)S(1)} %collective-permute-done.9.refs_1_), channel_id=1, source_target_pairs={{0,1},{1,0},{2,3},{3,2},{4,5},{5,4},{6,7},{7,6},{8,9},{9,8},{10,11... | collective-permute-start | bytes 638984 | tf_op jit(solution)/shard_map/ppermute | solution.py:25
  58.9 3.7 %collective-permute-start.20 = (bf16[32,1664]{1,0:T(8,128)(2,1)S(1)}, bf16[32,1664]{1,0:T(8,128)(2,1)S(1)}, u32[]{:S(2)}, u32[]{:S(2)}) collective-permute-start(bf16[32,1664]{1,0:T(8,128)(2,1)S(1)} %collective-permute-done.18.refs_0_), channel_id=1, source_target_pairs={{0,1},{1,0},{2,3},{3,2},{4,5},{5,4},{6,7},{7,6},{8,9},{9,8},{10,11... | collective-permute-start | bytes 319496 | tf_op jit(solution)/shard_map/ppermute | solution.py:25
  59.4 3.8 %collective-permute-start.21 = (bf16[32,1664]{1,0:T(8,128)(2,1)}, bf16[32,1664]{1,0:T(8,128)(2,1)S(1)}, u32[]{:S(2)}, u32[]{:S(2)}) collective-permute-start(bf16[32,1664]{1,0:T(8,128)(2,1)} %collective-permute-done.19.refs_1_), channel_id=1, source_target_pairs={{0,1},{1,0},{2,3},{3,2},{4,5},{5,4},{6,7},{7,6},{8,9},{9,8},{10,11... | collective-permute-start | bytes 319496 | tf_op jit(solution)/shard_map/ppermute | solution.py:25
  62.7 5.3 %collective-permute-start.15 = (bf16[64,1664]{1,0:T(8,128)(2,1)S(1)}, bf16[64,1664]{1,0:T(8,128)(2,1)S(1)}, u32[]{:S(2)}, u32[]{:S(2)}) collective-permute-start(bf16[64,1664]{1,0:T(8,128)(2,1)S(1)} %collective-permute-done.13.refs_0_), channel_id=1, source_target_pairs={{0,1},{1,0},{2,3},{3,2},{4,5},{5,4},{6,7},{7,6},{8,9},{9,8},{10,11... | collective-permute-start | bytes 638984 | tf_op jit(solution)/shard_map/ppermute | solution.py:25
  63.2 5.3 %collective-permute-start.16 = (bf16[64,1664]{1,0:T(8,128)(2,1)S(1)}, bf16[64,1664]{1,0:T(8,128)(2,1)S(1)}, u32[]{:S(2)}, u32[]{:S(2)}) collective-permute-start(bf16[64,1664]{1,0:T(8,128)(2,1)S(1)} %collective-permute-done.14.refs_1_), channel_id=1, source_target_pairs={{0,1},{1,0},{2,3},{3,2},{4,5},{5,4},{6,7},{7,6},{8,9},{9,8},{10,11... | collective-permute-start | bytes 638984 | tf_op jit(solution)/shard_map/ppermute | solution.py:25
  65.3 21.5 %collective-permute-start.7 = (bf16[128,1536]{1,0:T(8,128)(2,1)S(1)}, bf16[128,1536]{1,0:T(8,128)(2,1)S(1)}, u32[]{:S(2)}, u32[]{:S(2)}) collective-permute-start(bf16[128,1536]{1,0:T(8,128)(2,1)S(1)} %get-tuple-element.28), channel_id=1, source_target_pairs={{0,1},{1,0},{2,3},{3,2},{4,5},{5,4},{6,7},{7,6},{8,9},{9,8},{10,11... | collective-permute-start | bytes 1179656 | tf_op jit(solution)/shard_map/ppermute | solution.py:25
  65.8 4.9 %collective-permute-start.22 = (bf16[64,1536]{1,0:T(8,128)(2,1)S(1)}, bf16[64,1536]{1,0:T(8,128)(2,1)S(1)}, u32[]{:S(2)}, u32[]{:S(2)}) collective-permute-start(bf16[64,1536]{1,0:T(8,128)(2,1)S(1)} %get-tuple-element.34), channel_id=1, source_target_pairs={{0,1},{1,0},{2,3},{3,2},{4,5},{5,4},{6,7},{7,6},{8,9},{9,8},{10,11... | collective-permute-start | bytes 589832 | tf_op jit(solution)/shard_map/ppermute | solution.py:25
  68.0 11.4 %collective-permute-start.12 = (bf16[128,1536]{1,0:T(8,128)(2,1)S(1)}, bf16[128,1536]{1,0:T(8,128)(2,1)S(1)}, u32[]{:S(2)}, u32[]{:S(2)}) collective-permute-start(bf16[128,1536]{1,0:T(8,128)(2,1)S(1)} %get-tuple-element.30), channel_id=1, source_target_pairs={{0,1},{1,0},{2,3},{3,2},{4,5},{5,4},{6,7},{7,6},{8,9},{9,8},{10,11... | collective-permute-start | bytes 1179656 | tf_op jit(solution)/shard_map/ppermute | solution.py:25
  70.6 1.9 %collective-permute-start.17 = (bf16[128,1536]{1,0:T(8,128)(2,1)S(1)}, bf16[128,1536]{1,0:T(8,128)(2,1)S(1)}, u32[]{:S(2)}, u32[]{:S(2)}) collective-permute-start(bf16[128,1536]{1,0:T(8,128)(2,1)S(1)} %get-tuple-element.32), channel_id=1, source_target_pairs={{0,1},{1,0},{2,3},{3,2},{4,5},{5,4},{6,7},{7,6},{8,9},{9,8},{10,11... | collective-permute-start | bytes 1179656 | tf_op jit(solution)/shard_map/ppermute | solution.py:25
  70.8 5.2 %collective-permute-start.23 = (bf16[32,1536]{1,0:T(8,128)(2,1)S(1)}, bf16[32,1536]{1,0:T(8,128)(2,1)S(1)}, u32[]{:S(2)}, u32[]{:S(2)}) collective-permute-start(bf16[32,1536]{1,0:T(8,128)(2,1)S(1)} %get-tuple-element.43), channel_id=1, source_target_pairs={{0,4},{1,5},{4,8},{5,9},{8,12},{9,13},{12,14},{13,15},{14,10},{15,... | collective-permute-start | bytes 294920 | tf_op jit(solution)/shard_map/ppermute | solution.py:536
  72.5 4.8 %collective-permute-start.27 = (bf16[32,1536]{1,0:T(8,128)(2,1)S(1)}, bf16[32,1536]{1,0:T(8,128)(2,1)S(1)}, u32[]{:S(2)}, u32[]{:S(2)}) collective-permute-start(bf16[32,1536]{1,0:T(8,128)(2,1)S(1)} %get-tuple-element.44), channel_id=1, source_target_pairs={{4,0},{5,1},{8,4},{9,5},{12,8},{13,9},{14,12},{15,13},{10,14},{11,... | collective-permute-start | bytes 294920 | tf_op jit(solution)/shard_map/ppermute | solution.py:537
  77.4 6.1 %collective-permute-start.24 = (bf16[64,1536]{1,0:T(8,128)(2,1)S(1)}, bf16[64,1536]{1,0:T(8,128)(2,1)S(1)}, u32[]{:S(2)}, u32[]{:S(2)}) collective-permute-start(bf16[64,1536]{1,0:T(8,128)(2,1)S(1)} %get-tuple-element.41), channel_id=1, source_target_pairs={{0,4},{1,5},{4,8},{5,9},{8,12},{9,13},{12,14},{13,15},{14,10},{15,... | collective-permute-start | bytes 589832 | tf_op jit(solution)/shard_map/ppermute | solution.py:536
  78.9 5.8 %collective-permute-start.28 = (bf16[64,1536]{1,0:T(8,128)(2,1)S(1)}, bf16[64,1536]{1,0:T(8,128)(2,1)S(1)}, u32[]{:S(2)}, u32[]{:S(2)}) collective-permute-start(bf16[64,1536]{1,0:T(8,128)(2,1)S(1)} %get-tuple-element.42), channel_id=1, source_target_pairs={{4,0},{5,1},{8,4},{9,5},{12,8},{13,9},{14,12},{15,13},{10,14},{11,... | collective-permute-start | bytes 589832 | tf_op jit(solution)/shard_map/ppermute | solution.py:537
  79.6 18.6 %copy-start.4 = (f32[64,1536]{1,0:T(8,128)S(1)}, f32[64,1536]{1,0:T(8,128)}, u32[]{:S(2)}) copy-start(f32[64,1536]{1,0:T(8,128)} %copy-done.3) | copy-start | bytes 1179652
  84.8 5.7 %collective-permute-start.25 = (bf16[64,1536]{1,0:T(8,128)(2,1)S(1)}, bf16[64,1536]{1,0:T(8,128)(2,1)S(1)}, u32[]{:S(2)}, u32[]{:S(2)}) collective-permute-start(bf16[64,1536]{1,0:T(8,128)(2,1)S(1)} %get-tuple-element.39), channel_id=1, source_target_pairs={{0,4},{1,5},{4,8},{5,9},{8,12},{9,13},{12,14},{13,15},{14,10},{15,... | collective-permute-start | bytes 589832 | tf_op jit(solution)/shard_map/ppermute | solution.py:536
  86.3 5.9 %collective-permute-start.29 = (bf16[64,1536]{1,0:T(8,128)(2,1)S(1)}, bf16[64,1536]{1,0:T(8,128)(2,1)S(1)}, u32[]{:S(2)}, u32[]{:S(2)}) collective-permute-start(bf16[64,1536]{1,0:T(8,128)(2,1)S(1)} %get-tuple-element.40), channel_id=1, source_target_pairs={{4,0},{5,1},{8,4},{9,5},{12,8},{13,9},{14,12},{15,13},{10,14},{11,... | collective-permute-start | bytes 589832 | tf_op jit(solution)/shard_map/ppermute | solution.py:537
  92.3 5.7 %collective-permute-start.26 = (bf16[64,1536]{1,0:T(8,128)(2,1)S(1)}, bf16[64,1536]{1,0:T(8,128)(2,1)S(1)}, u32[]{:S(2)}, u32[]{:S(2)}) collective-permute-start(bf16[64,1536]{1,0:T(8,128)(2,1)S(1)} %get-tuple-element.37), channel_id=1, source_target_pairs={{0,4},{1,5},{4,8},{5,9},{8,12},{9,13},{12,14},{13,15},{14,10},{15,... | collective-permute-start | bytes 589832 | tf_op jit(solution)/shard_map/ppermute | solution.py:536
  92.5 5.7 %collective-permute-start.30 = (bf16[64,1536]{1,0:T(8,128)(2,1)S(1)}, bf16[64,1536]{1,0:T(8,128)(2,1)S(1)}, u32[]{:S(2)}, u32[]{:S(2)}) collective-permute-start(bf16[64,1536]{1,0:T(8,128)(2,1)S(1)} %get-tuple-element.38), channel_id=1, source_target_pairs={{4,0},{5,1},{8,4},{9,5},{12,8},{13,9},{14,12},{15,13},{10,14},{11,... | collective-permute-start | bytes 589832 | tf_op jit(solution)/shard_map/ppermute | solution.py:537

commit v2 on v1

--- a/solution.py
+++ b/solution.py
@@ -260,17 +260,56 @@
     return jnp.where(seen, 0.0, -1e30)
 
 
-def later_body(seq_ref, sink_ref, query_ref, key_ref, value_ref, segment_ref, out_ref, *scratch):
-    blocks = query_ref.shape[0] // WINDOW
+def fetch(sources, targets, sems):
+    copies = [
+        pltpu.make_async_copy(source, target, sems.at[i])
+        for i, (source, target) in enumerate(zip(sources, targets))
+    ]
+    for copy in copies:
+        copy.start()
+    for copy in copies:
+        copy.wait()
+
+
+def load_body(*refs):
+    count = len(refs) // 2
+    fetch(refs[:count], refs[count:-1], refs[-1])
+
+
+def later_body(
+    sink_any,
+    query_any,
+    key_any,
+    value_any,
+    segment_any,
+    out_ref,
+    tail_ref,
+    sems,
+    sink_ref,
+    query_ref,
+    key_ref,
+    value_ref,
+    segment_ref,
+    *scratch,
+):
+    tokens = key_ref.shape[0]
+    blocks = tokens // WINDOW
+    kv_width = key_ref.shape[1]
+    fetch(
+        [sink_any, query_any.at[WINDOW:, :], key_any, value_any, segment_any],
+        [sink_ref, query_ref, key_ref, value_ref, segment_ref],
+        sems,
+    )
+    tail_ref[:, :kv_width] = key_ref[tokens - WINDOW :, :]
+    tail_ref[:, kv_width:] = value_ref[tokens - WINDOW :, :]
     for block in range(1, blocks):
-        here = seq_ref[0] * blocks + block
+        here = lax.axis_index("seq") * blocks + block
         bias = visible_bias(segment_ref, here - 1, here, False)
-        rows = slice(block * WINDOW, (block + 1) * WINDOW)
+        rows = slice((block - 1) * WINDOW, block * WINDOW)
         window = slice((block - 1) * WINDOW, (block + 1) * WINDOW)
 
-        def store(tile, value, block=block):
-            at = slice((block - 1) * WINDOW, block * WINDOW)
-            out_ref[at, tile * LANES : (tile + 1) * LANES] = value
+        def store(tile, value, rows=rows):
+            out_ref[rows, tile * LANES : (tile + 1) * LANES] = value
 
         attend_block(
             query_ref[rows, :],
@@ -284,17 +323,22 @@
 
 
 def first_body(
-    seq_ref,
+    sink_any,
+    query_any,
+    key_any,
+    value_any,
+    segment_any,
+    tail_ref,
+    later_ref,
+    weight_ref,
+    kept_ref,
+    given_ref,
+    sems,
     sink_ref,
     query_ref,
     key_ref,
     value_ref,
     segment_ref,
-    tail_ref,
-    later_ref,
-    weight_ref,
-    kept_ref,
-    given_ref,
     sorted_ref,
     *scratch,
 ):
@@ -302,12 +346,21 @@
     half = tokens // 2
     shard_rows = kept_ref.shape[1]
     piece = min(shard_rows, WINDOW)
-    core = seq_ref[1]
-    blocks = tokens // WINDOW
-    here = seq_ref[0] * blocks
-    starts = seq_ref[0] == 0
-    bias = visible_bias(segment_ref, jnp.maximum(here - 1, 0), here, starts)
+    core = lax.axis_index("head") % 2
+    here = lax.axis_index("seq") * (tokens // WINDOW)
     kv_width = key_ref.shape[1]
+    fetch(
+        [
+            sink_any,
+            query_any.at[:WINDOW, :],
+            key_any.at[:WINDOW, :],
+            value_any.at[:WINDOW, :],
+            segment_any,
+        ],
+        [sink_ref, query_ref, key_ref, value_ref, segment_ref],
+        sems,
+    )
+    bias = visible_bias(segment_ref, jnp.maximum(here - 1, 0), here, here == 0)
 
     def goal(row):
         owner = row // shard_rows
@@ -347,20 +400,31 @@
 
 
 VMEM = pl.BlockSpec(memory_space=pltpu.VMEM)
-SMEM = pl.BlockSpec(memory_space=pltpu.SMEM)
+HBM = pl.BlockSpec(memory_space=pltpu.HBM)
 
 
 def call(body, outs, args, specs, scratch=(), flops=0, limit=16 << 20):
     moved = sum(a.size * a.dtype.itemsize for a in args)
     return pl.pallas_call(
         body,
-        out_shape=outs,
+        out_shape=[pltpu.VMEM(shape, dtype) for shape, dtype in outs],
         in_specs=specs,
-        out_specs=jax.tree.map(lambda _: VMEM, outs),
+        out_specs=[VMEM] * len(outs),
         scratch_shapes=list(scratch),
         compiler_params=pltpu.CompilerParams(vmem_limit_bytes=limit),
         cost_estimate=pl.CostEstimate(flops=flops, bytes_accessed=moved, transcendentals=0),
     )(*args)
+
+
+def loaded(args):
+    return call(
+        load_body,
+        [(a.shape, a.dtype) for a in args],
+        args,
+        [HBM] * len(args),
+        [pltpu.SemaphoreType.DMA((len(args),))],
+        limit=32 << 20,
+    )
 
 
 def projected_heads(
@@ -370,54 +434,53 @@
     kv_width = key_states.shape[1]
     groups = kv_width // HEAD_DIM
     stack = width // LANES // groups * WINDOW
-    where_at = jnp.stack([lax.axis_index("seq"), lax.axis_index("head") % 2]).astype(jnp.int32)
     segment_rows = segment_ids.reshape(-1, WINDOW)
-    tail = passed_along(
-        jnp.concatenate([key_states[tokens - WINDOW :], value_states[tokens - WINDOW :]], 1),
-        "seq",
-        1,
-    )
+    inputs = [sink_logits, query_states, key_states, value_states, segment_rows]
+    bf16, f32 = jnp.bfloat16, jnp.float32
+
+    def local(query_rows, key_rows):
+        return [
+            pltpu.SemaphoreType.DMA((len(inputs),)),
+            pltpu.SMEM(sink_logits.shape, f32),
+            pltpu.VMEM((query_rows, width), bf16),
+            pltpu.VMEM((key_rows, kv_width), bf16),
+            pltpu.VMEM((key_rows, kv_width), bf16),
+            pltpu.VMEM(segment_rows.shape, jnp.int32),
+        ]
+
     scratch = [
-        pltpu.VMEM((groups, stack, 4 * WINDOW), jnp.float32),
-        pltpu.VMEM((groups, stack, 4 * WINDOW), jnp.bfloat16),
-        pltpu.VMEM((groups, stack, LANES), jnp.float32),
+        pltpu.VMEM((groups, stack, 4 * WINDOW), f32),
+        pltpu.VMEM((groups, stack, 4 * WINDOW), bf16),
+        pltpu.VMEM((groups, stack, LANES), f32),
     ]
     flops = 16 * WINDOW * WINDOW * width
-    later = call(
+    later, tail = call(
         later_body,
-        jax.ShapeDtypeStruct((tokens - WINDOW, width), jnp.bfloat16),
-        [where_at, sink_logits, query_states, key_states, value_states, segment_rows],
-        [SMEM, SMEM] + [VMEM] * 4,
-        scratch,
+        [((tokens - WINDOW, width), bf16), ((WINDOW, 2 * kv_width), bf16)],
+        inputs,
+        [HBM] * 5,
+        local(tokens - WINDOW, tokens) + scratch,
         flops * (tokens // WINDOW - 1),
     )
+    peers = lax.axis_size("seq")
+    tail = lax.ppermute(tail, "seq", [(i, (i + 1) % peers) for i in range(peers)])
     columns = tokens // (2 * shard_rows)
     out_width = out_weight.shape[1]
-    side = jax.ShapeDtypeStruct((columns, shard_rows, out_width), jnp.bfloat16)
+    side = ((columns, shard_rows, out_width), bf16)
     return call(
         first_body,
         [side, side],
-        [
-            where_at,
-            sink_logits,
-            query_states[:WINDOW],
-            key_states[:WINDOW],
-            value_states[:WINDOW],
-            segment_rows,
-            tail,
-            later,
-            out_weight,
-        ],
-        [SMEM, SMEM] + [VMEM] * 7,
-        [pltpu.VMEM((tokens, width), jnp.bfloat16)] + scratch,
+        inputs + [tail, later, out_weight],
+        [HBM] * 5 + [VMEM] * 3,
+        local(WINDOW, WINDOW) + [pltpu.VMEM((tokens, width), bf16)] + scratch,
         flops + 2 * tokens * width * out_width,
         24 << 20,
     )
 
 
-def chip_body(at_ref, kept_ref, taken_ref, residual_ref, hidden_ref, *away_refs):
+def chip_body(kept_ref, taken_ref, residual_ref, hidden_ref, *away_refs):
     columns = kept_ref.shape[0]
-    column = at_ref[0]
+    column = lax.axis_index("head") // 2
     total = kept_ref[column].astype(jnp.float32) + taken_ref[column].astype(jnp.float32)
     hidden_ref[...] = residual_ref[...].astype(jnp.float32) + total
     for step, away_ref in enumerate(away_refs):
@@ -460,11 +523,11 @@
     packed_ref[:, width:] = coded.astype(packed_ref.dtype)
 
 
-def ffn_body(experts, expert_ref, gate_ref, up_ref, down_ref, *refs):
+def ffn_body(experts, gate_ref, up_ref, down_ref, *refs):
     ins, (keep_ref, give_ref, rows_ref, act_ref) = refs[:-4], refs[-4:]
     width, hidden = gate_ref.shape[1], gate_ref.shape[2]
     half = keep_ref.shape[0]
-    expert = expert_ref[0]
+    expert = (lax.axis_index("seq") * lax.axis_size("head") + lax.axis_index("head")) // 2
     scales = []
     start = 0
     for ref in ins:
@@ -519,7 +582,6 @@
     seq, head = lax.axis_size("seq"), lax.axis_size("head")
     columns = head // 2
     chips = seq * columns
-    column = lax.axis_index("head") // 2
 
     order = [
         (col, row if col % 2 == 0 else seq - 1 - row) for col in range(columns) for row in range(seq)
@@ -540,45 +602,44 @@
     def swap(value):
         return partner(value, "head", 0)
 
+    bf16, f32 = jnp.bfloat16, jnp.float32
+    out_weight, residual = loaded([out_weight, residual])
     kept, given = projected_heads(
         query_states, key_states, value_states, sink_logits, segment_ids, out_weight, shard_rows
     )
-    rows_f32 = jax.ShapeDtypeStruct((shard_rows, width), jnp.float32)
-    rows_bf16 = jax.ShapeDtypeStruct((shard_rows, width), jnp.bfloat16)
+    rows = (shard_rows, width)
     hidden_state, *away = call(
         chip_body,
-        [rows_f32] + [rows_bf16] * (columns - 1),
-        [column.reshape(1), kept, swap(given), residual],
-        [SMEM] + [VMEM] * 3,
+        [(rows, f32)] + [(rows, bf16)] * (columns - 1),
+        [kept, swap(given), residual],
+        [VMEM] * 3,
     )
     arrived = []
     for step, value in enumerate(away):
         pairs = [(i, (i + 2 * (step + 1)) % head) for i in range(head)]
         arrived.append(lax.ppermute(value, "head", pairs))
-    packed_width = width + LANES
+    gate_proj, up_proj, down_proj = loaded([gate_proj, up_proj, down_proj])
+    packed = (shard_rows, width + LANES)
     hidden_state, mine = call(
         functools.partial(norm_body, len(arrived), chips),
-        [rows_f32, jax.ShapeDtypeStruct((shard_rows, packed_width), jnp.bfloat16)],
+        [(rows, f32), (packed, bf16)],
         [hidden_state, norm_gain.reshape(1, -1), expert_ids, route_weights] + arrived,
         [VMEM] * (4 + len(arrived)),
     )
 
-    expert = (lax.axis_index("seq") * columns + column).reshape(1)
-
     def terms(blocks):
-        rows = 2 * sum(block.shape[0] for block in blocks)
-        others = [swap(block) for block in blocks]
-        out = jax.ShapeDtypeStruct((rows // 2, width), jnp.bfloat16)
+        count = 2 * sum(block.shape[0] for block in blocks)
+        others = []
+        for block in blocks:
+            others.append(swap(block))
+        out = ((count // 2, width), bf16)
         keep, give = call(
             functools.partial(ffn_body, chips),
             [out, out],
-            [expert, gate_proj, up_proj, down_proj] + blocks + others,
-            [SMEM] + [VMEM] * (3 + 2 * len(blocks)),
-            [
-                pltpu.VMEM((rows, width), jnp.bfloat16),
-                pltpu.VMEM((rows, hidden_units), jnp.bfloat16),
-            ],
-            6 * rows * width * hidden_units,
+            [gate_proj, up_proj, down_proj] + blocks + others,
+            [VMEM] * (3 + 2 * len(blocks)),
+            [pltpu.VMEM((count, width), bf16), pltpu.VMEM((count, hidden_units), bf16)],
+            6 * count * width * hidden_units,
             24 << 20,
         )
         taken = swap(give)

time: 99.6 us -> 89.7 us (0.901)
  local copies, waits for them, and re-layouts: 15.6 us -> 10.5 us
  Pallas kernels: 17.7 us -> 14.2 us
  starting transfers between devices: 27.3 us -> 25.7 us
    ppermute x8, starting transfers between devices: 6.03 us -> 11 us  [ring(): off = lax.ppermute(pair[1], ('seq', 'head'), back)]
    ppermute x8, starting transfers between devices: 11.2 us -> 6.29 us  [ring(): on = lax.ppermute(pair[0], ('seq', 'head'), onward)]
    pallas_call x9 -> x11, Pallas kernels: 17.7 us -> 14.2 us  [call(): pl.pallas_call(body, out_shape=[pltpu.VMEM(shape, dtype) for shape, dtype...]
    unnamed x36 -> x38, local copies, waits for them, and re-layouts: 12.5 us -> 10.5 us
    ppermute x1, starting transfers between devices: 4.96 us -> 3.1 us  [projected_heads(): lax.ppermute(tail, 'seq', [(i, (i + 1) % peers) for i in range(peers)])]
    slice x2 -> x0, local copies, waits for them, and re-layouts: 1.78 us -> none  [the longest x1 0.97 us: projected_heads(): query_states[:WINDOW]]
    slice x2, local copies, waits for them, and re-layouts: 1.29 us -> 0.02 us  [ring_layer(): travelling = ring((travelling[0][:half], travelling[1][half:]))]
    ppermute x15, waiting for transfers between devices: 1.73 us -> 2.84 us  [partner(): lax.ppermute(value, axis, [(i, i ^ 1 << distance) for i in range(lax.axis...]
  transfers between devices with their start and end apart: 33 -> 33, of which waited for: 14 -> 15; matrix products, arithmetic and copies ran while one was open for 3% -> 1% of each run, Pallas kernels for 14% -> 11%
where the time goes in v2:
time: 89.7 us; the launch traced here: 89.3 us
  waiting for transfers between devices  37.2 us (41%)
  starting transfers between devices  25.7 us (29%)
  Pallas kernels  14.2 us (16%)
  local copies, waits for them, and re-layouts  10.5 us (12%)
  other arithmetic  1.38 us (2%)
    ppermute x8, waiting for transfers between devices, ring(): on = lax.ppermute(pair[0], ('seq', 'head'), onward)  24.5 us
    pallas_call x11, Pallas kernels, call(): pl.pallas_call(body, out_shape=[pltpu.VMEM(shape, dtype) for shape, dtype...  14.2 us
    ppermute x8, starting transfers between devices, ring(): off = lax.ppermute(pair[1], ('seq', 'head'), back)  11 us
    unnamed x38, local copies, waits for them, and re-layouts  10.5 us
    ppermute x8, starting transfers between devices, ring(): on = lax.ppermute(pair[0], ('seq', 'head'), onward)  6.29 us
    ppermute x1, waiting for transfers between devices, ring_layer(): arrived.append(lax.ppermute(value, 'head', pairs))  5.02 us
    ppermute x8, waiting for transfers between devices, ring(): off = lax.ppermute(pair[1], ('seq', 'head'), back)  3.85 us
    ppermute x15, starting transfers between devices, partner(): lax.ppermute(value, axis, [(i, i ^ 1 << distance) for i in range(lax.axis...  3.54 us
  transfers between devices with their start and end apart: 33, of which 15 were waited for; matrix products, arithmetic and copies ran while one was open for 1% of the time, Pallas kernels for 11%

profile of v2, /device:TPU:0, one launch (start us, length us, event | category | flops | bytes accessed | tf_op | source)
XLA Modules:
  0.0 89.3 jit_solution(7981162670344645413)
XLA Ops:
  0.0 1.1 %copy-done.4 = bf16[256,1024]{1,0:T(8,128)(2,1)S(1)} copy-done((bf16[256,1024]{1,0:T(8,128)(2,1)S(1)}, bf16[256,1024]{1,0:T(8,128)(2,1)}, u32[]{:S(2)}) %copy-start.4) | copy-done | bytes 524312
  1.1 0.8 copy-done.7
  1.9 0.8 copy-done.9
  2.7 0.7 copy-done.11
  3.4 0.7 copy-done.13
  4.1 1.8 %shard_map.127 = (bf16[128,1024]{1,0:T(8,128)(2,1)S(1)}, bf16[128,256]{1,0:T(8,128)(2,1)S(1)}) custom-call(f32[16]{0:T(128)S(1)} %copy-done.13, bf16[256,1024]{1,0:T(8,128)(2,1)S(1)} %copy-done.4, bf16[256,128]{1,0:T(8,128)(2,1)S(1)} %copy-done.7, bf16[256,128]{1,0:T(8,128)(2,1)S(1)} %copy-done.9, s32[8,128]{1,0:T(8,128)S(1)} %bitcast.1), custom_call_target="tpu_custom_call" | custom-call | flops 268435456 | bytes 659520 | tf_op jit(solution)/shard_map/pallas_call | solution.py:408
  5.9 3.1 %collective-permute-start = (bf16[128,256]{1,0:T(8,128)(2,1)S(1)}, bf16[128,256]{1,0:T(8,128)(2,1)S(1)}, u32[]{:S(2)}, u32[]{:S(2)}) collective-permute-start(bf16[128,256]{1,0:T(8,128)(2,1)S(1)} %get-tuple-element.28), channel_id=1, source_target_pairs={{0,4},{4,8},{8,12},{12,0},{1,5},{5,9},{9,13},{13,1},{2,6},{6,10},{... | collective-permute-start | bytes 196616 | tf_op jit(solution)/shard_map/ppermute | solution.py:466
  9.0 1.9 %copy-done = bf16[1024,1536]{1,0:T(8,128)(2,1)S(1)} copy-done((bf16[1024,1536]{1,0:T(8,128)(2,1)S(1)}, bf16[1024,1536]{1,0:T(8,128)(2,1)}, u32[]{:S(2)}) %copy-start) | copy-done | bytes 3145752
  10.9 0.9 %copy-done.6 = bf16[64,1536]{1,0:T(8,128)(2,1)S(1)} copy-done((bf16[64,1536]{1,0:T(8,128)(2,1)S(1)}, bf16[64,1536]{1,0:T(8,128)(2,1)}, u32[]{:S(2)}) %copy-start.6) | copy-done | bytes 196632
  11.9 0.5 shard_map.128
  12.3 1.0 %collective-permute-done.tail_ref = bf16[128,256]{1,0:T(8,128)(2,1)S(1)} collective-permute-done((bf16[128,256]{1,0:T(8,128)(2,1)S(1)}, bf16[128,256]{1,0:T(8,128)(2,1)S(1)}, u32[]{:S(2)}, u32[]{:S(2)}) %collective-permute-start) | collective-permute-done | bytes 65568 | tf_op jit(solution)/shard_map/ppermute | solution.py:466
  13.4 2.6 %shard_map.129 = (bf16[2,64,1536]{2,1,0:T(8,128)(2,1)S(1)}, bf16[2,64,1536]{2,1,0:T(8,128)(2,1)S(1)}) custom-call(f32[16]{0:T(128)S(1)} %copy-done.14, bf16[256,1024]{1,0:T(8,128)(2,1)S(1)} %copy-done.5, bf16[256,128]{1,0:T(8,128)(2,1)S(1)} %copy-done.8, bf16[256,128]{1,0:T(8,128)(2,1)S(1)} %copy-done.10, s32[8,128]{1,0:T(8,128)S(1)} %bitcast.2, ...), custom_call_target="tpu_custom_call" | custom-call | flops 1073741824 | bytes 4132928 | tf_op jit(solution)/shard_map/pallas_call | solution.py:408
  16.1 1.7 %collective-permute-done.1.taken_ref = bf16[2,64,1536]{2,1,0:T(8,128)(2,1)S(1)} collective-permute-done((bf16[2,64,1536]{2,1,0:T(8,128)(2,1)S(1)}, bf16[2,64,1536]{2,1,0:T(8,128)(2,1)S(1)}, u32[]{:S(2)}, u32[]{:S(2)}) %collective-permute-start.1) | collective-permute-done | bytes 393248 | tf_op jit(solution)/shard_map/ppermute | solution.py:25
  17.8 0.1 shard_map.130
  17.9 1.8 %collective-permute-start.2 = (bf16[64,1536]{1,0:T(8,128)(2,1)S(1)}, bf16[64,1536]{1,0:T(8,128)(2,1)S(1)}, u32[]{:S(2)}, u32[]{:S(2)}) collective-permute-start(bf16[64,1536]{1,0:T(8,128)(2,1)S(1)} %get-tuple-element.35), channel_id=1, source_target_pairs={{0,2},{1,3},{2,0},{3,1},{4,6},{5,7},{6,4},{7,5},{8,10},{9,11},{10,... | collective-permute-start | bytes 589832 | tf_op jit(solution)/shard_map/ppermute | solution.py:620
  19.7 0.1 copy.14.ids_ref
  19.9 5.0 %collective-permute-done.2.refs_0_ = bf16[64,1536]{1,0:T(8,128)(2,1)S(1)} collective-permute-done((bf16[64,1536]{1,0:T(8,128)(2,1)S(1)}, bf16[64,1536]{1,0:T(8,128)(2,1)S(1)}, u32[]{:S(2)}, u32[]{:S(2)}) %collective-permute-start.2) | collective-permute-done | bytes 196640 | tf_op jit(solution)/shard_map/ppermute | solution.py:620
  25.0 0.2 shard_map.131
  25.2 0.7 collective-permute-start.3
  25.9 1.4 %collective-permute-start.4 = (bf16[64,1664]{1,0:T(8,128)(2,1)S(1)}, bf16[64,1664]{1,0:T(8,128)(2,1)S(1)}, u32[]{:S(2)}, u32[]{:S(2)}) collective-permute-start(bf16[64,1664]{1,0:T(8,128)(2,1)S(1)} %get-tuple-element.40.refs_0_), channel_id=1, source_target_pairs={{4,0},{5,1},{8,4},{9,5},{12,8},{13,9},{14,12},{15,13},{10,14},{11,... | collective-permute-start | bytes 638984 | tf_op jit(solution)/shard_map/ppermute | solution.py:599
  27.3 4.4 %collective-permute-done.3.refs_0_ = bf16[64,1664]{1,0:T(8,128)(2,1)S(1)} collective-permute-done((bf16[64,1664]{1,0:T(8,128)(2,1)S(1)}, bf16[64,1664]{1,0:T(8,128)(2,1)S(1)}, u32[]{:S(2)}, u32[]{:S(2)}) %collective-permute-start.3) | collective-permute-done | bytes 213024 | tf_op jit(solution)/shard_map/ppermute | solution.py:598
  31.7 0.6 collective-permute-start.8
  32.3 1.4 %collective-permute-start.9 = (bf16[64,1664]{1,0:T(8,128)(2,1)S(1)}, bf16[64,1664]{1,0:T(8,128)(2,1)S(1)}, u32[]{:S(2)}, u32[]{:S(2)}) collective-permute-start(bf16[64,1664]{1,0:T(8,128)(2,1)S(1)} %collective-permute-done.4.refs_1_), channel_id=1, source_target_pairs={{4,0},{5,1},{8,4},{9,5},{12,8},{13,9},{14,12},{15,13},{10,14},{11,... | collective-permute-start | bytes 638984 | tf_op jit(solution)/shard_map/ppermute | solution.py:599
  33.7 3.9 %collective-permute-done.8.refs_0_ = bf16[64,1664]{1,0:T(8,128)(2,1)S(1)} collective-permute-done((bf16[64,1664]{1,0:T(8,128)(2,1)S(1)}, bf16[64,1664]{1,0:T(8,128)(2,1)S(1)}, u32[]{:S(2)}, u32[]{:S(2)}) %collective-permute-start.8) | collective-permute-done | bytes 213024 | tf_op jit(solution)/shard_map/ppermute | solution.py:598
  37.7 0.6 collective-permute-start.13
  38.3 1.7 %collective-permute-start.14 = (bf16[64,1664]{1,0:T(8,128)(2,1)S(1)}, bf16[64,1664]{1,0:T(8,128)(2,1)S(1)}, u32[]{:S(2)}, u32[]{:S(2)}) collective-permute-start(bf16[64,1664]{1,0:T(8,128)(2,1)S(1)} %collective-permute-done.9.refs_1_), channel_id=1, source_target_pairs={{4,0},{5,1},{8,4},{9,5},{12,8},{13,9},{14,12},{15,13},{10,14},{11,... | collective-permute-start | bytes 638984 | tf_op jit(solution)/shard_map/ppermute | solution.py:599
  40.0 0.5 collective-permute-start.5
  40.5 3.0 %collective-permute-done.13.refs_0_ = bf16[64,1664]{1,0:T(8,128)(2,1)S(1)} collective-permute-done((bf16[64,1664]{1,0:T(8,128)(2,1)S(1)}, bf16[64,1664]{1,0:T(8,128)(2,1)S(1)}, u32[]{:S(2)}, u32[]{:S(2)}) %collective-permute-start.13) | collective-permute-done | bytes 213024 | tf_op jit(solution)/shard_map/ppermute | solution.py:598
  43.5 0.8 collective-permute-start.18
  44.3 1.9 %collective-permute-start.19 = (bf16[32,1664]{1,0:T(8,128)(2,1)S(1)}, bf16[32,1664]{1,0:T(8,128)(2,1)S(1)}, u32[]{:S(2)}, u32[]{:S(2)}) collective-permute-start(bf16[32,1664]{1,0:T(8,128)(2,1)S(1)} %slice.44), channel_id=1, source_target_pairs={{4,0},{5,1},{8,4},{9,5},{12,8},{13,9},{14,12},{15,13},{10,14},{11,... | collective-permute-start | bytes 319496 | tf_op jit(solution)/shard_map/ppermute | solution.py:599
  46.2 1.7 %copy-done.2 = bf16[1,1536,768]{2,1,0:T(8,128)(2,1)S(1)} copy-done((bf16[1,1536,768]{2,1,0:T(8,128)(2,1)S(1)}, bf16[1,1536,768]{2,1,0:T(8,128)(2,1)}, u32[]{:S(2)}) %copy-start.2) | copy-done | bytes 2359320
  47.9 1.7 %copy-done.3 = bf16[1,768,1536]{2,1,0:T(8,128)(2,1)S(1)} copy-done((bf16[1,768,1536]{2,1,0:T(8,128)(2,1)S(1)}, bf16[1,768,1536]{2,1,0:T(8,128)(2,1)}, u32[]{:S(2)}) %copy-start.3) | copy-done | bytes 2359320
  49.6 0.5 shard_map.132
  50.1 1.1 %shard_map.137 = (bf16[64,1536]{1,0:T(8,128)(2,1)S(1)}, bf16[64,1536]{1,0:T(8,128)(2,1)S(1)}) custom-call(bf16[1,1536,768]{2,1,0:T(8,128)(2,1)S(1)} %get-tuple-element.37.gate_ref, bf16[1,1536,768]{2,1,0:T(8,128)(2,1)S(1)} %get-tuple-element.38.up_ref, bf16[1,768,1536]{2,1,0:T(8,128)(2,1)S(1)} %get-tuple-element.39.down_ref, ...), custom_call_target="tpu_custom_call" | custom-call | flops 905969664 | bytes 7503872 | tf_op jit(solution)/shard_map/pallas_call | solution.py:408
  51.3 0.5 collective-permute-start.10
  51.9 0.4 collective-permute-start.20
  52.4 2.0 %shard_map.133 = (bf16[128,1536]{1,0:T(8,128)(2,1)S(1)}, bf16[128,1536]{1,0:T(8,128)(2,1)S(1)}) custom-call(bf16[1,1536,768]{2,1,0:T(8,128)(2,1)S(1)} %get-tuple-element.37.gate_ref, bf16[1,1536,768]{2,1,0:T(8,128)(2,1)S(1)} %get-tuple-element.38.up_ref, bf16[1,768,1536]{2,1,0:T(8,128)(2,1)S(1)} %get-tuple-element.39.down_ref, ...), custom_call_target="tpu_custom_call" | custom-call | flops 1811939328 | bytes 7929856 | tf_op jit(solution)/shard_map/pallas_call | solution.py:408
  54.5 0.5 collective-permute-start.15
  55.1 1.1 %shard_map.136 = (bf16[64,1536]{1,0:T(8,128)(2,1)S(1)}, bf16[64,1536]{1,0:T(8,128)(2,1)S(1)}) custom-call(bf16[1,1536,768]{2,1,0:T(8,128)(2,1)S(1)} %get-tuple-element.37.gate_ref, bf16[1,1536,768]{2,1,0:T(8,128)(2,1)S(1)} %get-tuple-element.38.up_ref, bf16[1,768,1536]{2,1,0:T(8,128)(2,1)S(1)} %get-tuple-element.39.down_ref, ...), custom_call_target="tpu_custom_call" | custom-call | flops 905969664 | bytes 7503872 | tf_op jit(solution)/shard_map/pallas_call | solution.py:408
  56.2 0.5 collective-permute-start.7
  56.8 2.0 %shard_map.134 = (bf16[128,1536]{1,0:T(8,128)(2,1)S(1)}, bf16[128,1536]{1,0:T(8,128)(2,1)S(1)}) custom-call(bf16[1,1536,768]{2,1,0:T(8,128)(2,1)S(1)} %get-tuple-element.37.gate_ref, bf16[1,1536,768]{2,1,0:T(8,128)(2,1)S(1)} %get-tuple-element.38.up_ref, bf16[1,768,1536]{2,1,0:T(8,128)(2,1)S(1)} %get-tuple-element.39.down_ref, ...), custom_call_target="tpu_custom_call" | custom-call | flops 1811939328 | bytes 7929856 | tf_op jit(solution)/shard_map/pallas_call | solution.py:408
  58.9 0.5 collective-permute-start.12
  59.4 2.0 %shard_map.135 = (bf16[128,1536]{1,0:T(8,128)(2,1)S(1)}, bf16[128,1536]{1,0:T(8,128)(2,1)S(1)}) custom-call(bf16[1,1536,768]{2,1,0:T(8,128)(2,1)S(1)} %get-tuple-element.37.gate_ref, bf16[1,1536,768]{2,1,0:T(8,128)(2,1)S(1)} %get-tuple-element.38.up_ref, bf16[1,768,1536]{2,1,0:T(8,128)(2,1)S(1)} %get-tuple-element.39.down_ref, ...), custom_call_target="tpu_custom_call" | custom-call | flops 1811939328 | bytes 7929856 | tf_op jit(solution)/shard_map/pallas_call | solution.py:408
  61.4 0.2 collective-permute-start.17
  61.7 0.5 collective-permute-start.23
  62.1 1.1 %collective-permute-done.17 = bf16[128,1536]{1,0:T(8,128)(2,1)S(1)} collective-permute-done((bf16[128,1536]{1,0:T(8,128)(2,1)S(1)}, bf16[128,1536]{1,0:T(8,128)(2,1)S(1)}, u32[]{:S(2)}, u32[]{:S(2)}) %collective-permute-start.17) | collective-permute-done | bytes 393248 | tf_op jit(solution)/shard_map/ppermute | solution.py:25
  63.2 1.5 %collective-permute-start.27 = (bf16[32,1536]{1,0:T(8,128)(2,1)S(1)}, bf16[32,1536]{1,0:T(8,128)(2,1)S(1)}, u32[]{:S(2)}, u32[]{:S(2)}) collective-permute-start(bf16[32,1536]{1,0:T(8,128)(2,1)S(1)} %get-tuple-element.58), channel_id=1, source_target_pairs={{4,0},{5,1},{8,4},{9,5},{12,8},{13,9},{14,12},{15,13},{10,14},{11,... | collective-permute-start | bytes 294920 | tf_op jit(solution)/shard_map/ppermute | solution.py:599
  64.8 2.0 %collective-permute-done.23 = bf16[32,1536]{1,0:T(8,128)(2,1)S(1)} collective-permute-done((bf16[32,1536]{1,0:T(8,128)(2,1)S(1)}, bf16[32,1536]{1,0:T(8,128)(2,1)S(1)}, u32[]{:S(2)}, u32[]{:S(2)}) %collective-permute-start.23) | collective-permute-done | bytes 98336 | tf_op jit(solution)/shard_map/ppermute | solution.py:598
  66.8 1.2 %collective-permute-done.27 = bf16[32,1536]{1,0:T(8,128)(2,1)S(1)} collective-permute-done((bf16[32,1536]{1,0:T(8,128)(2,1)S(1)}, bf16[32,1536]{1,0:T(8,128)(2,1)S(1)}, u32[]{:S(2)}, u32[]{:S(2)}) %collective-permute-start.27) | collective-permute-done | bytes 98336 | tf_op jit(solution)/shard_map/ppermute | solution.py:599
  68.1 0.5 collective-permute-start.24
  68.6 1.6 %collective-permute-start.28 = (bf16[64,1536]{1,0:T(8,128)(2,1)S(1)}, bf16[64,1536]{1,0:T(8,128)(2,1)S(1)}, u32[]{:S(2)}, u32[]{:S(2)}) collective-permute-start(bf16[64,1536]{1,0:T(8,128)(2,1)S(1)} %get-tuple-element.56), channel_id=1, source_target_pairs={{4,0},{5,1},{8,4},{9,5},{12,8},{13,9},{14,12},{15,13},{10,14},{11,... | collective-permute-start | bytes 589832 | tf_op jit(solution)/shard_map/ppermute | solution.py:599
  70.2 0.1 convert_add_fusion.1
  70.3 3.9 %collective-permute-done.24 = bf16[64,1536]{1,0:T(8,128)(2,1)S(1)} collective-permute-done((bf16[64,1536]{1,0:T(8,128)(2,1)S(1)}, bf16[64,1536]{1,0:T(8,128)(2,1)S(1)}, u32[]{:S(2)}, u32[]{:S(2)}) %collective-permute-start.24) | collective-permute-done | bytes 196640 | tf_op jit(solution)/shard_map/ppermute | solution.py:598
  74.3 0.2 collective-permute-done.28
  74.5 1.5 %collective-permute-start.25 = (bf16[64,1536]{1,0:T(8,128)(2,1)S(1)}, bf16[64,1536]{1,0:T(8,128)(2,1)S(1)}, u32[]{:S(2)}, u32[]{:S(2)}) collective-permute-start(bf16[64,1536]{1,0:T(8,128)(2,1)S(1)} %get-tuple-element.53), channel_id=1, source_target_pairs={{0,4},{1,5},{4,8},{5,9},{8,12},{9,13},{12,14},{13,15},{14,10},{15,... | collective-permute-start | bytes 589832 | tf_op jit(solution)/shard_map/ppermute | solution.py:598
  76.1 0.5 collective-permute-start.29
  76.6 0.1 convert_add_fusion.2
  76.7 3.5 %collective-permute-done.25 = bf16[64,1536]{1,0:T(8,128)(2,1)S(1)} collective-permute-done((bf16[64,1536]{1,0:T(8,128)(2,1)S(1)}, bf16[64,1536]{1,0:T(8,128)(2,1)S(1)}, u32[]{:S(2)}, u32[]{:S(2)}) %collective-permute-start.25) | collective-permute-done | bytes 196640 | tf_op jit(solution)/shard_map/ppermute | solution.py:598
  80.3 1.5 %collective-permute-done.29 = bf16[64,1536]{1,0:T(8,128)(2,1)S(1)} collective-permute-done((bf16[64,1536]{1,0:T(8,128)(2,1)S(1)}, bf16[64,1536]{1,0:T(8,128)(2,1)S(1)}, u32[]{:S(2)}, u32[]{:S(2)}) %collective-permute-start.29) | collective-permute-done | bytes 196640 | tf_op jit(solution)/shard_map/ppermute | solution.py:599
  81.8 1.0 %collective-permute-start.26 = (bf16[64,1536]{1,0:T(8,128)(2,1)S(1)}, bf16[64,1536]{1,0:T(8,128)(2,1)S(1)}, u32[]{:S(2)}, u32[]{:S(2)}) collective-permute-start(bf16[64,1536]{1,0:T(8,128)(2,1)S(1)} %get-tuple-element.51), channel_id=1, source_target_pairs={{0,4},{1,5},{4,8},{5,9},{8,12},{9,13},{12,14},{13,15},{14,10},{15,... | collective-permute-start | bytes 589832 | tf_op jit(solution)/shard_map/ppermute | solution.py:598
  82.8 1.1 %collective-permute-start.30 = (bf16[64,1536]{1,0:T(8,128)(2,1)S(1)}, bf16[64,1536]{1,0:T(8,128)(2,1)S(1)}, u32[]{:S(2)}, u32[]{:S(2)}) collective-permute-start(bf16[64,1536]{1,0:T(8,128)(2,1)S(1)} %get-tuple-element.52), channel_id=1, source_target_pairs={{4,0},{5,1},{8,4},{9,5},{12,8},{13,9},{14,12},{15,13},{10,14},{11,... | collective-permute-start | bytes 589832 | tf_op jit(solution)/shard_map/ppermute | solution.py:599
  83.9 3.6 %collective-permute-done.26 = bf16[64,1536]{1,0:T(8,128)(2,1)S(1)} collective-permute-done((bf16[64,1536]{1,0:T(8,128)(2,1)S(1)}, bf16[64,1536]{1,0:T(8,128)(2,1)S(1)}, u32[]{:S(2)}, u32[]{:S(2)}) %collective-permute-start.26) | collective-permute-done | bytes 196640 | tf_op jit(solution)/shard_map/ppermute | solution.py:598
  87.5 0.9 %collective-permute-done.30 = bf16[64,1536]{1,0:T(8,128)(2,1)S(1)} collective-permute-done((bf16[64,1536]{1,0:T(8,128)(2,1)S(1)}, bf16[64,1536]{1,0:T(8,128)(2,1)S(1)}, u32[]{:S(2)}, u32[]{:S(2)}) %collective-permute-start.30) | collective-permute-done | bytes 196640 | tf_op jit(solution)/shard_map/ppermute | solution.py:599
  88.5 0.8 add_convert_fusion
  (63 shorter events, 1.1 us)
Async XLA Ops:
  0.0 13.3 %copy-start.14 = (f32[16]{0:T(128)S(1)}, f32[16]{0:T(128)}, u32[]{:S(2)}) copy-start(f32[16]{0:T(128)} %sink_any.3) | copy-start | bytes 196
  0.0 1.1 %copy-start.4 = (bf16[256,1024]{1,0:T(8,128)(2,1)S(1)}, bf16[256,1024]{1,0:T(8,128)(2,1)}, u32[]{:S(2)}) copy-start(bf16[256,1024]{1,0:T(8,128)(2,1)} %query_any.3) | copy-start | bytes 1572868
  1.1 0.8 copy-start.7
  1.9 0.8 copy-start.9
  2.7 0.7 copy-start.11
  3.4 0.7 copy-start.13
  4.1 9.2 %copy-start.5 = (bf16[256,1024]{1,0:T(8,128)(2,1)S(1)}, bf16[256,1024]{1,0:T(8,128)(2,1)}, u32[]{:S(2)}) copy-start(bf16[256,1024]{1,0:T(8,128)(2,1)} %query_any.3) | copy-start | bytes 1572868
  4.1 9.2 %copy-start.8 = (bf16[256,128]{1,0:T(8,128)(2,1)S(1)}, bf16[256,128]{1,0:T(8,128)(2,1)}, u32[]{:S(2)}) copy-start(bf16[256,128]{1,0:T(8,128)(2,1)} %key_any.3) | copy-start | bytes 196612
  4.1 9.2 %copy-start.10 = (bf16[256,128]{1,0:T(8,128)(2,1)S(1)}, bf16[256,128]{1,0:T(8,128)(2,1)}, u32[]{:S(2)}) copy-start(bf16[256,128]{1,0:T(8,128)(2,1)} %value_any.3) | copy-start | bytes 196612
  4.1 9.2 %copy-start.12 = (s32[1024]{0:T(1024)S(1)}, s32[1024]{0:T(1024)}, u32[]{:S(2)}) copy-start(s32[1024]{0:T(1024)} %param.17) | copy-start | bytes 12292
  5.9 7.4 %collective-permute-start = (bf16[128,256]{1,0:T(8,128)(2,1)S(1)}, bf16[128,256]{1,0:T(8,128)(2,1)S(1)}, u32[]{:S(2)}, u32[]{:S(2)}) collective-permute-start(bf16[128,256]{1,0:T(8,128)(2,1)S(1)} %get-tuple-element.28), channel_id=1, source_target_pairs={{0,4},{4,8},{8,12},{12,0},{1,5},{5,9},{9,13},{13,1},{2,6},{6,10},{... | collective-permute-start | bytes 196616 | tf_op jit(solution)/shard_map/ppermute | solution.py:466
  9.0 1.9 %copy-start = (bf16[1024,1536]{1,0:T(8,128)(2,1)S(1)}, bf16[1024,1536]{1,0:T(8,128)(2,1)}, u32[]{:S(2)}) copy-start(bf16[1024,1536]{1,0:T(8,128)(2,1)} %refs_0_.2) | copy-start | bytes 9437188
  10.9 0.9 %copy-start.6 = (bf16[64,1536]{1,0:T(8,128)(2,1)S(1)}, bf16[64,1536]{1,0:T(8,128)(2,1)}, u32[]{:S(2)}) copy-start(bf16[64,1536]{1,0:T(8,128)(2,1)} %refs_1_.2) | copy-start | bytes 589828
  13.3 6.4 %copy-start.16 = (s32[64,4]{0,1:T(4,128)S(1)}, s32[64,4]{0,1:T(4,128)}, u32[]{:S(2)}) copy-start(s32[64,4]{0,1:T(4,128)} %param.21) | copy-start | bytes 3076
  13.4 6.5 %copy-start.17 = (f32[64,4]{0,1:T(4,128)S(1)}, f32[64,4]{0,1:T(4,128)}, u32[]{:S(2)}) copy-start(f32[64,4]{0,1:T(4,128)} %param.22) | copy-start | bytes 3076
  13.4 6.5 %copy-start.15 = (f32[1536]{0:T(1024)S(1)}, f32[1536]{0:T(1024)}, u32[]{:S(2)}) copy-start(f32[1536]{0:T(1024)} %param.20) | copy-start | bytes 18436
  13.4 32.8 %copy-start.1 = (bf16[1,1536,768]{2,1,0:T(8,128)(2,1)S(1)}, bf16[1,1536,768]{2,1,0:T(8,128)(2,1)}, u32[]{:S(2)}) copy-start(bf16[1,1536,768]{2,1,0:T(8,128)(2,1)} %refs_0_.3) | copy-start | bytes 7077892
  16.0 1.8 %collective-permute-start.1 = (bf16[2,64,1536]{2,1,0:T(8,128)(2,1)S(1)}, bf16[2,64,1536]{2,1,0:T(8,128)(2,1)S(1)}, u32[]{:S(2)}, u32[]{:S(2)}) collective-permute-start(bf16[2,64,1536]{2,1,0:T(8,128)(2,1)S(1)} %get-tuple-element.32), channel_id=1, source_target_pairs={{0,1},{1,0},{2,3},{3,2},{4,5},{5,4},{6,7},{7,6},{8,9},{9,8},{10,11... | collective-permute-start | bytes 1179656 | tf_op jit(solution)/shard_map/ppermute | solution.py:25
  17.9 7.0 %collective-permute-start.2 = (bf16[64,1536]{1,0:T(8,128)(2,1)S(1)}, bf16[64,1536]{1,0:T(8,128)(2,1)S(1)}, u32[]{:S(2)}, u32[]{:S(2)}) collective-permute-start(bf16[64,1536]{1,0:T(8,128)(2,1)S(1)} %get-tuple-element.35), channel_id=1, source_target_pairs={{0,2},{1,3},{2,0},{3,1},{4,6},{5,7},{6,4},{7,5},{8,10},{9,11},{10,... | collective-permute-start | bytes 589832 | tf_op jit(solution)/shard_map/ppermute | solution.py:620
  25.2 6.5 %collective-permute-start.3 = (bf16[64,1664]{1,0:T(8,128)(2,1)S(1)}, bf16[64,1664]{1,0:T(8,128)(2,1)S(1)}, u32[]{:S(2)}, u32[]{:S(2)}) collective-permute-start(bf16[64,1664]{1,0:T(8,128)(2,1)S(1)} %get-tuple-element.40.refs_0_), channel_id=1, source_target_pairs={{0,4},{1,5},{4,8},{5,9},{8,12},{9,13},{12,14},{13,15},{14,10},{15,... | collective-permute-start | bytes 638984 | tf_op jit(solution)/shard_map/ppermute | solution.py:598
  25.9 6.4 %collective-permute-start.4 = (bf16[64,1664]{1,0:T(8,128)(2,1)S(1)}, bf16[64,1664]{1,0:T(8,128)(2,1)S(1)}, u32[]{:S(2)}, u32[]{:S(2)}) collective-permute-start(bf16[64,1664]{1,0:T(8,128)(2,1)S(1)} %get-tuple-element.40.refs_0_), channel_id=1, source_target_pairs={{4,0},{5,1},{8,4},{9,5},{12,8},{13,9},{14,12},{15,13},{10,14},{11,... | collective-permute-start | bytes 638984 | tf_op jit(solution)/shard_map/ppermute | solution.py:599
  31.7 6.0 %collective-permute-start.8 = (bf16[64,1664]{1,0:T(8,128)(2,1)S(1)}, bf16[64,1664]{1,0:T(8,128)(2,1)S(1)}, u32[]{:S(2)}, u32[]{:S(2)}) collective-permute-start(bf16[64,1664]{1,0:T(8,128)(2,1)S(1)} %collective-permute-done.3.refs_0_), channel_id=1, source_target_pairs={{0,4},{1,5},{4,8},{5,9},{8,12},{9,13},{12,14},{13,15},{14,10},{15,... | collective-permute-start | bytes 638984 | tf_op jit(solution)/shard_map/ppermute | solution.py:598
  32.3 6.0 %collective-permute-start.9 = (bf16[64,1664]{1,0:T(8,128)(2,1)S(1)}, bf16[64,1664]{1,0:T(8,128)(2,1)S(1)}, u32[]{:S(2)}, u32[]{:S(2)}) collective-permute-start(bf16[64,1664]{1,0:T(8,128)(2,1)S(1)} %collective-permute-done.4.refs_1_), channel_id=1, source_target_pairs={{4,0},{5,1},{8,4},{9,5},{12,8},{13,9},{14,12},{15,13},{10,14},{11,... | collective-permute-start | bytes 638984 | tf_op jit(solution)/shard_map/ppermute | solution.py:599
  37.7 5.8 %collective-permute-start.13 = (bf16[64,1664]{1,0:T(8,128)(2,1)S(1)}, bf16[64,1664]{1,0:T(8,128)(2,1)S(1)}, u32[]{:S(2)}, u32[]{:S(2)}) collective-permute-start(bf16[64,1664]{1,0:T(8,128)(2,1)S(1)} %collective-permute-done.8.refs_0_), channel_id=1, source_target_pairs={{0,4},{1,5},{4,8},{5,9},{8,12},{9,13},{12,14},{13,15},{14,10},{15,... | collective-permute-start | bytes 638984 | tf_op jit(solution)/shard_map/ppermute | solution.py:598
  38.3 6.0 %collective-permute-start.14 = (bf16[64,1664]{1,0:T(8,128)(2,1)S(1)}, bf16[64,1664]{1,0:T(8,128)(2,1)S(1)}, u32[]{:S(2)}, u32[]{:S(2)}) collective-permute-start(bf16[64,1664]{1,0:T(8,128)(2,1)S(1)} %collective-permute-done.9.refs_1_), channel_id=1, source_target_pairs={{4,0},{5,1},{8,4},{9,5},{12,8},{13,9},{14,12},{15,13},{10,14},{11,... | collective-permute-start | bytes 638984 | tf_op jit(solution)/shard_map/ppermute | solution.py:599
  40.0 10.1 %collective-permute-start.31 = (bf16[64,1664]{1,0:T(8,128)(2,1)S(1)}, bf16[64,1664]{1,0:T(8,128)(2,1)S(1)}, u32[]{:S(2)}, u32[]{:S(2)}) collective-permute-start(bf16[64,1664]{1,0:T(8,128)(2,1)S(1)} %get-tuple-element.40.refs_0_), channel_id=1, source_target_pairs={{0,1},{1,0},{2,3},{3,2},{4,5},{5,4},{6,7},{7,6},{8,9},{9,8},{10,11... | collective-permute-start | bytes 638984 | tf_op jit(solution)/shard_map/ppermute | solution.py:25
  40.0 11.3 %collective-permute-start.5 = (bf16[64,1664]{1,0:T(8,128)(2,1)S(1)}, bf16[64,1664]{1,0:T(8,128)(2,1)S(1)}, u32[]{:S(2)}, u32[]{:S(2)}) collective-permute-start(bf16[64,1664]{1,0:T(8,128)(2,1)S(1)} %collective-permute-done.3.refs_0_), channel_id=1, source_target_pairs={{0,1},{1,0},{2,3},{3,2},{4,5},{5,4},{6,7},{7,6},{8,9},{9,8},{10,11... | collective-permute-start | bytes 638984 | tf_op jit(solution)/shard_map/ppermute | solution.py:25
  40.5 11.3 %collective-permute-start.6 = (bf16[64,1664]{1,0:T(8,128)(2,1)S(1)}, bf16[64,1664]{1,0:T(8,128)(2,1)S(1)}, u32[]{:S(2)}, u32[]{:S(2)}) collective-permute-start(bf16[64,1664]{1,0:T(8,128)(2,1)S(1)} %collective-permute-done.4.refs_1_), channel_id=1, source_target_pairs={{0,1},{1,0},{2,3},{3,2},{4,5},{5,4},{6,7},{7,6},{8,9},{9,8},{10,11... | collective-permute-start | bytes 638984 | tf_op jit(solution)/shard_map/ppermute | solution.py:25
  43.5 8.4 %collective-permute-start.18 = (bf16[32,1664]{1,0:T(8,128)(2,1)S(1)}, bf16[32,1664]{1,0:T(8,128)(2,1)S(1)}, u32[]{:S(2)}, u32[]{:S(2)}) collective-permute-start(bf16[32,1664]{1,0:T(8,128)(2,1)S(1)} %slice.43), channel_id=1, source_target_pairs={{0,4},{1,5},{4,8},{5,9},{8,12},{9,13},{12,14},{13,15},{14,10},{15,... | collective-permute-start | bytes 319496 | tf_op jit(solution)/shard_map/ppermute | solution.py:598
  44.3 8.0 %collective-permute-start.19 = (bf16[32,1664]{1,0:T(8,128)(2,1)S(1)}, bf16[32,1664]{1,0:T(8,128)(2,1)S(1)}, u32[]{:S(2)}, u32[]{:S(2)}) collective-permute-start(bf16[32,1664]{1,0:T(8,128)(2,1)S(1)} %slice.44), channel_id=1, source_target_pairs={{4,0},{5,1},{8,4},{9,5},{12,8},{13,9},{14,12},{15,13},{10,14},{11,... | collective-permute-start | bytes 319496 | tf_op jit(solution)/shard_map/ppermute | solution.py:599
  46.2 1.7 %copy-start.2 = (bf16[1,1536,768]{2,1,0:T(8,128)(2,1)S(1)}, bf16[1,1536,768]{2,1,0:T(8,128)(2,1)}, u32[]{:S(2)}) copy-start(bf16[1,1536,768]{2,1,0:T(8,128)(2,1)} %refs_1_.3) | copy-start | bytes 7077892
  47.9 1.7 %copy-start.3 = (bf16[1,768,1536]{2,1,0:T(8,128)(2,1)S(1)}, bf16[1,768,1536]{2,1,0:T(8,128)(2,1)}, u32[]{:S(2)}) copy-start(bf16[1,768,1536]{2,1,0:T(8,128)(2,1)} %refs_2_.1) | copy-start | bytes 7077892
  51.2 32.7 %collective-permute-start.32 = (bf16[64,1536]{1,0:T(8,128)(2,1)S(1)}, bf16[64,1536]{1,0:T(8,128)(2,1)S(1)}, u32[]{:S(2)}, u32[]{:S(2)}) collective-permute-start(bf16[64,1536]{1,0:T(8,128)(2,1)S(1)} %get-tuple-element.50), channel_id=1, source_target_pairs={{0,1},{1,0},{2,3},{3,2},{4,5},{5,4},{6,7},{7,6},{8,9},{9,8},{10,11... | collective-permute-start | bytes 589832 | tf_op jit(solution)/shard_map/ppermute | solution.py:25
  51.3 4.9 %collective-permute-start.10 = (bf16[64,1664]{1,0:T(8,128)(2,1)S(1)}, bf16[64,1664]{1,0:T(8,128)(2,1)S(1)}, u32[]{:S(2)}, u32[]{:S(2)}) collective-permute-start(bf16[64,1664]{1,0:T(8,128)(2,1)S(1)} %collective-permute-done.8.refs_0_), channel_id=1, source_target_pairs={{0,1},{1,0},{2,3},{3,2},{4,5},{5,4},{6,7},{7,6},{8,9},{9,8},{10,11... | collective-permute-start | bytes 638984 | tf_op jit(solution)/shard_map/ppermute | solution.py:25
  51.8 4.9 %collective-permute-start.11 = (bf16[64,1664]{1,0:T(8,128)(2,1)S(1)}, bf16[64,1664]{1,0:T(8,128)(2,1)S(1)}, u32[]{:S(2)}, u32[]{:S(2)}) collective-permute-start(bf16[64,1664]{1,0:T(8,128)(2,1)S(1)} %collective-permute-done.9.refs_1_), channel_id=1, source_target_pairs={{0,1},{1,0},{2,3},{3,2},{4,5},{5,4},{6,7},{7,6},{8,9},{9,8},{10,11... | collective-permute-start | bytes 638984 | tf_op jit(solution)/shard_map/ppermute | solution.py:25
  51.9 2.6 %collective-permute-start.20 = (bf16[32,1664]{1,0:T(8,128)(2,1)S(1)}, bf16[32,1664]{1,0:T(8,128)(2,1)S(1)}, u32[]{:S(2)}, u32[]{:S(2)}) collective-permute-start(bf16[32,1664]{1,0:T(8,128)(2,1)S(1)} %collective-permute-done.18.refs_0_), channel_id=1, source_target_pairs={{0,1},{1,0},{2,3},{3,2},{4,5},{5,4},{6,7},{7,6},{8,9},{9,8},{10,11... | collective-permute-start | bytes 319496 | tf_op jit(solution)/shard_map/ppermute | solution.py:25
  52.3 2.6 %collective-permute-start.21 = (bf16[32,1664]{1,0:T(8,128)(2,1)S(1)}, bf16[32,1664]{1,0:T(8,128)(2,1)S(1)}, u32[]{:S(2)}, u32[]{:S(2)}) collective-permute-start(bf16[32,1664]{1,0:T(8,128)(2,1)S(1)} %collective-permute-done.19.refs_1_), channel_id=1, source_target_pairs={{0,1},{1,0},{2,3},{3,2},{4,5},{5,4},{6,7},{7,6},{8,9},{9,8},{10,11... | collective-permute-start | bytes 319496 | tf_op jit(solution)/shard_map/ppermute | solution.py:25
  54.5 4.4 %collective-permute-start.15 = (bf16[64,1664]{1,0:T(8,128)(2,1)S(1)}, bf16[64,1664]{1,0:T(8,128)(2,1)S(1)}, u32[]{:S(2)}, u32[]{:S(2)}) collective-permute-start(bf16[64,1664]{1,0:T(8,128)(2,1)S(1)} %collective-permute-done.13.refs_0_), channel_id=1, source_target_pairs={{0,1},{1,0},{2,3},{3,2},{4,5},{5,4},{6,7},{7,6},{8,9},{9,8},{10,11... | collective-permute-start | bytes 638984 | tf_op jit(solution)/shard_map/ppermute | solution.py:25
  55.0 4.4 %collective-permute-start.16 = (bf16[64,1664]{1,0:T(8,128)(2,1)S(1)}, bf16[64,1664]{1,0:T(8,128)(2,1)S(1)}, u32[]{:S(2)}, u32[]{:S(2)}) collective-permute-start(bf16[64,1664]{1,0:T(8,128)(2,1)S(1)} %collective-permute-done.14.refs_1_), channel_id=1, source_target_pairs={{0,1},{1,0},{2,3},{3,2},{4,5},{5,4},{6,7},{7,6},{8,9},{9,8},{10,11... | collective-permute-start | bytes 638984 | tf_op jit(solution)/shard_map/ppermute | solution.py:25
  56.2 20.4 %collective-permute-start.7 = (bf16[128,1536]{1,0:T(8,128)(2,1)S(1)}, bf16[128,1536]{1,0:T(8,128)(2,1)S(1)}, u32[]{:S(2)}, u32[]{:S(2)}) collective-permute-start(bf16[128,1536]{1,0:T(8,128)(2,1)S(1)} %get-tuple-element.42), channel_id=1, source_target_pairs={{0,1},{1,0},{2,3},{3,2},{4,5},{5,4},{6,7},{7,6},{8,9},{9,8},{10,11... | collective-permute-start | bytes 1179656 | tf_op jit(solution)/shard_map/ppermute | solution.py:25
  56.7 4.9 %collective-permute-start.22 = (bf16[64,1536]{1,0:T(8,128)(2,1)S(1)}, bf16[64,1536]{1,0:T(8,128)(2,1)S(1)}, u32[]{:S(2)}, u32[]{:S(2)}) collective-permute-start(bf16[64,1536]{1,0:T(8,128)(2,1)S(1)} %get-tuple-element.48), channel_id=1, source_target_pairs={{0,1},{1,0},{2,3},{3,2},{4,5},{5,4},{6,7},{7,6},{8,9},{9,8},{10,11... | collective-permute-start | bytes 589832 | tf_op jit(solution)/shard_map/ppermute | solution.py:25
  58.9 11.3 %collective-permute-start.12 = (bf16[128,1536]{1,0:T(8,128)(2,1)S(1)}, bf16[128,1536]{1,0:T(8,128)(2,1)S(1)}, u32[]{:S(2)}, u32[]{:S(2)}) collective-permute-start(bf16[128,1536]{1,0:T(8,128)(2,1)S(1)} %get-tuple-element.44), channel_id=1, source_target_pairs={{0,1},{1,0},{2,3},{3,2},{4,5},{5,4},{6,7},{7,6},{8,9},{9,8},{10,11... | collective-permute-start | bytes 1179656 | tf_op jit(solution)/shard_map/ppermute | solution.py:25
  61.4 1.8 %collective-permute-start.17 = (bf16[128,1536]{1,0:T(8,128)(2,1)S(1)}, bf16[128,1536]{1,0:T(8,128)(2,1)S(1)}, u32[]{:S(2)}, u32[]{:S(2)}) collective-permute-start(bf16[128,1536]{1,0:T(8,128)(2,1)S(1)} %get-tuple-element.46), channel_id=1, source_target_pairs={{0,1},{1,0},{2,3},{3,2},{4,5},{5,4},{6,7},{7,6},{8,9},{9,8},{10,11... | collective-permute-start | bytes 1179656 | tf_op jit(solution)/shard_map/ppermute | solution.py:25
  61.7 5.2 %collective-permute-start.23 = (bf16[32,1536]{1,0:T(8,128)(2,1)S(1)}, bf16[32,1536]{1,0:T(8,128)(2,1)S(1)}, u32[]{:S(2)}, u32[]{:S(2)}) collective-permute-start(bf16[32,1536]{1,0:T(8,128)(2,1)S(1)} %get-tuple-element.57), channel_id=1, source_target_pairs={{0,4},{1,5},{4,8},{5,9},{8,12},{9,13},{12,14},{13,15},{14,10},{15,... | collective-permute-start | bytes 294920 | tf_op jit(solution)/shard_map/ppermute | solution.py:598
  63.2 4.8 %collective-permute-start.27 = (bf16[32,1536]{1,0:T(8,128)(2,1)S(1)}, bf16[32,1536]{1,0:T(8,128)(2,1)S(1)}, u32[]{:S(2)}, u32[]{:S(2)}) collective-permute-start(bf16[32,1536]{1,0:T(8,128)(2,1)S(1)} %get-tuple-element.58), channel_id=1, source_target_pairs={{4,0},{5,1},{8,4},{9,5},{12,8},{13,9},{14,12},{15,13},{10,14},{11,... | collective-permute-start | bytes 294920 | tf_op jit(solution)/shard_map/ppermute | solution.py:599
  68.1 6.1 %collective-permute-start.24 = (bf16[64,1536]{1,0:T(8,128)(2,1)S(1)}, bf16[64,1536]{1,0:T(8,128)(2,1)S(1)}, u32[]{:S(2)}, u32[]{:S(2)}) collective-permute-start(bf16[64,1536]{1,0:T(8,128)(2,1)S(1)} %get-tuple-element.55), channel_id=1, source_target_pairs={{0,4},{1,5},{4,8},{5,9},{8,12},{9,13},{12,14},{13,15},{14,10},{15,... | collective-permute-start | bytes 589832 | tf_op jit(solution)/shard_map/ppermute | solution.py:598
  68.6 5.8 %collective-permute-start.28 = (bf16[64,1536]{1,0:T(8,128)(2,1)S(1)}, bf16[64,1536]{1,0:T(8,128)(2,1)S(1)}, u32[]{:S(2)}, u32[]{:S(2)}) collective-permute-start(bf16[64,1536]{1,0:T(8,128)(2,1)S(1)} %get-tuple-element.56), channel_id=1, source_target_pairs={{4,0},{5,1},{8,4},{9,5},{12,8},{13,9},{14,12},{15,13},{10,14},{11,... | collective-permute-start | bytes 589832 | tf_op jit(solution)/shard_map/ppermute | solution.py:599
  74.5 5.7 %collective-permute-start.25 = (bf16[64,1536]{1,0:T(8,128)(2,1)S(1)}, bf16[64,1536]{1,0:T(8,128)(2,1)S(1)}, u32[]{:S(2)}, u32[]{:S(2)}) collective-permute-start(bf16[64,1536]{1,0:T(8,128)(2,1)S(1)} %get-tuple-element.53), channel_id=1, source_target_pairs={{0,4},{1,5},{4,8},{5,9},{8,12},{9,13},{12,14},{13,15},{14,10},{15,... | collective-permute-start | bytes 589832 | tf_op jit(solution)/shard_map/ppermute | solution.py:598
  76.1 5.7 %collective-permute-start.29 = (bf16[64,1536]{1,0:T(8,128)(2,1)S(1)}, bf16[64,1536]{1,0:T(8,128)(2,1)S(1)}, u32[]{:S(2)}, u32[]{:S(2)}) collective-permute-start(bf16[64,1536]{1,0:T(8,128)(2,1)S(1)} %get-tuple-element.54), channel_id=1, source_target_pairs={{4,0},{5,1},{8,4},{9,5},{12,8},{13,9},{14,12},{15,13},{10,14},{11,... | collective-permute-start | bytes 589832 | tf_op jit(solution)/shard_map/ppermute | solution.py:599
  81.8 5.7 %collective-permute-start.26 = (bf16[64,1536]{1,0:T(8,128)(2,1)S(1)}, bf16[64,1536]{1,0:T(8,128)(2,1)S(1)}, u32[]{:S(2)}, u32[]{:S(2)}) collective-permute-start(bf16[64,1536]{1,0:T(8,128)(2,1)S(1)} %get-tuple-element.51), channel_id=1, source_target_pairs={{0,4},{1,5},{4,8},{5,9},{8,12},{9,13},{12,14},{13,15},{14,10},{15,... | collective-permute-start | bytes 589832 | tf_op jit(solution)/shard_map/ppermute | solution.py:598
  82.8 5.7 %collective-permute-start.30 = (bf16[64,1536]{1,0:T(8,128)(2,1)S(1)}, bf16[64,1536]{1,0:T(8,128)(2,1)S(1)}, u32[]{:S(2)}, u32[]{:S(2)}) collective-permute-start(bf16[64,1536]{1,0:T(8,128)(2,1)S(1)} %get-tuple-element.52), channel_id=1, source_target_pairs={{4,0},{5,1},{8,4},{9,5},{12,8},{13,9},{14,12},{15,13},{10,14},{11,... | collective-permute-start | bytes 589832 | tf_op jit(solution)/shard_map/ppermute | solution.py:599

commit v3 on v2

--- a/solution.py
+++ b/solution.py
@@ -416,14 +416,14 @@
     )(*args)
 
 
-def loaded(args):
+def loaded(args, limit):
     return call(
         load_body,
         [(a.shape, a.dtype) for a in args],
         args,
         [HBM] * len(args),
         [pltpu.SemaphoreType.DMA((len(args),))],
-        limit=32 << 20,
+        limit=limit << 20,
     )
 
 
@@ -461,6 +461,7 @@
         [HBM] * 5,
         local(tokens - WINDOW, tokens) + scratch,
         flops * (tokens // WINDOW - 1),
+        60 << 20,
     )
     peers = lax.axis_size("seq")
     tail = lax.ppermute(tail, "seq", [(i, (i + 1) % peers) for i in range(peers)])
@@ -603,7 +604,7 @@
         return partner(value, "head", 0)
 
     bf16, f32 = jnp.bfloat16, jnp.float32
-    out_weight, residual = loaded([out_weight, residual])
+    out_weight, residual = loaded([out_weight, residual], 58)
     kept, given = projected_heads(
         query_states, key_states, value_states, sink_logits, segment_ids, out_weight, shard_rows
     )
@@ -618,7 +619,7 @@
     for step, value in enumerate(away):
         pairs = [(i, (i + 2 * (step + 1)) % head) for i in range(head)]
         arrived.append(lax.ppermute(value, "head", pairs))
-    gate_proj, up_proj, down_proj = loaded([gate_proj, up_proj, down_proj])
+    gate_proj, up_proj, down_proj = loaded([gate_proj, up_proj, down_proj], 54)
     packed = (shard_rows, width + LANES)
     hidden_state, mine = call(
         functools.partial(norm_body, len(arrived), chips),
@@ -653,21 +654,18 @@
         travelling = ring(travelling)
         sums.append(terms(list(travelling)))
     travelling = ring((travelling[0][:half], travelling[1][half:]))
-    total = terms(list(travelling)).astype(jnp.bfloat16)
-    passing = ring((total[:half], total[half:]))
-    for total in reversed(sums):
-        on, off = (value.astype(jnp.float32) for value in passing)
-        if on.shape[0] < shard_rows:
-            on = jnp.pad(on, ((0, half), (0, 0)))
-            off = jnp.pad(off, ((half, 0), (0, 0)))
-        on = (total[shard_rows:] + on).astype(jnp.bfloat16)
-        off = (total[:shard_rows] + off).astype(jnp.bfloat16)
-        passing = ring((on, off))
-    on, off = (value.astype(jnp.float32) for value in passing)
-    if on.shape[0] < shard_rows:
-        on = jnp.concatenate([on, off], 0)
-        off = 0.0
-    return (hidden_state + (on + off + own_term)).astype(jnp.bfloat16)
+    total = terms(list(travelling)).astype(bf16)
+    across = [(device(p, c), device(p + chips // 2, c)) for p in range(chips) for c in range(2)]
+    mixture = own_term + lax.ppermute(total, ("seq", "head"), across).astype(f32)
+    passing = None
+    for step in range(chips // 2 - 1, 0, -1):
+        on, off = sums[step - 1][shard_rows:], sums[step - 1][:shard_rows]
+        if passing is not None:
+            on, off = on + passing[0].astype(f32), off + passing[1].astype(f32)
+        passing = ring((on.astype(bf16), off.astype(bf16)))
+    if passing is not None:
+        mixture = mixture + (passing[0].astype(f32) + passing[1].astype(f32))
+    return (hidden_state + mixture).astype(bf16)
 
 
 def per_device(query_states, key_states, value_states, sink_logits, segment_ids, *rest):

time: 89.7 us -> 83.9 us (0.935)
  local copies, waits for them, and re-layouts: 10.5 us -> 0.28 us
  Pallas kernels: 14.2 us -> 18.8 us
  starting transfers between devices: 25.7 us -> 30.2 us
  waiting for transfers between devices: 37.2 us -> 32.8 us
    unnamed x38 -> x18, local copies, waits for them, and re-layouts: 10.5 us -> 0.23 us
    ppermute x8 -> x7, waiting for transfers between devices: 24.5 us -> 18.9 us  [ring(): on = lax.ppermute(pair[0], ('seq', 'head'), onward)]
    pallas_call x11, Pallas kernels: 14.2 us -> 18.8 us  [call(): pl.pallas_call(body, out_shape=[pltpu.VMEM(shape, dtype) for shape, dtype...]
    ppermute x8 -> x7, starting transfers between devices: 6.29 us -> 9.47 us  [ring(): on = lax.ppermute(pair[0], ('seq', 'head'), onward)]
    ppermute x0 -> x1, starting transfers between devices: none -> 2.84 us  [ring_layer(): lax.ppermute(total, ('seq', 'head'), across).astype(f32)]
    ppermute x1, waiting for transfers between devices: 0.97 us -> 2.35 us  [projected_heads(): lax.ppermute(tail, 'seq', [(i, (i + 1) % peers) for i in range(peers)])]
    ppermute x8 -> x7, starting transfers between devices: 11 us -> 9.8 us  [ring(): off = lax.ppermute(pair[1], ('seq', 'head'), back)]
    ppermute x15, waiting for transfers between devices: 2.84 us -> 1.75 us  [partner(): lax.ppermute(value, axis, [(i, i ^ 1 << distance) for i in range(lax.axis...]
  transfers between devices with their start and end apart: 33 -> 32, of which waited for: 15 -> 13; matrix products, arithmetic and copies ran while one was open for 1% -> 1% of each run, Pallas kernels for 11% -> 16%
where the time goes in v3:
time: 83.9 us; the launch traced here: 83.7 us
  waiting for transfers between devices  32.8 us (39%)
  starting transfers between devices  30.2 us (36%)
  Pallas kernels  18.8 us (22%)
  other arithmetic  1.28 us (2%)
    ppermute x7, waiting for transfers between devices, ring(): on = lax.ppermute(pair[0], ('seq', 'head'), onward)  18.9 us
    pallas_call x11, Pallas kernels, call(): pl.pallas_call(body, out_shape=[pltpu.VMEM(shape, dtype) for shape, dtype...  18.8 us
    ppermute x7, starting transfers between devices, ring(): off = lax.ppermute(pair[1], ('seq', 'head'), back)  9.8 us
    ppermute x7, starting transfers between devices, ring(): on = lax.ppermute(pair[0], ('seq', 'head'), onward)  9.47 us
    ppermute x1, waiting for transfers between devices, ring_layer(): arrived.append(lax.ppermute(value, 'head', pairs))  5.02 us
    ppermute x7, waiting for transfers between devices, ring(): off = lax.ppermute(pair[1], ('seq', 'head'), back)  4.82 us
    ppermute x15, starting transfers between devices, partner(): lax.ppermute(value, axis, [(i, i ^ 1 << distance) for i in range(lax.axis...  3.22 us
    ppermute x1, starting transfers between devices, projected_heads(): lax.ppermute(tail, 'seq', [(i, (i + 1) % peers) for i in range(peers)])  3.12 us
  transfers between devices with their start and end apart: 32, of which 13 were waited for; matrix products, arithmetic and copies ran while one was open for 1% of the time, Pallas kernels for 16%

profile of v3, /device:TPU:0, one launch (start us, length us, event | category | flops | bytes accessed | tf_op | source)
XLA Modules:
  0.0 83.7 jit_solution(5488338262126317955)
XLA Ops:
  0.0 2.3 %shard_map.127 = (bf16[128,1024]{1,0:T(8,128)(2,1)S(1)}, bf16[128,256]{1,0:T(8,128)(2,1)S(1)}) custom-call(f32[16]{0:T(128)} %sink_any.3, bf16[256,1024]{1,0:T(8,128)(2,1)} %query_any.3, bf16[256,128]{1,0:T(8,128)(2,1)} %key_any.3, bf16[256,128]{1,0:T(8,128)(2,1)} %value_any.3, s32[8,128]{1,0:T(8,128)} %bitcast.1), custom_call_target="tpu_custom_call" | custom-call | flops 268435456 | bytes 659520 | tf_op jit(solution)/shard_map/pallas_call | solution.py:408
  2.3 3.1 %collective-permute-start = (bf16[128,256]{1,0:T(8,128)(2,1)S(1)}, bf16[128,256]{1,0:T(8,128)(2,1)S(1)}, u32[]{:S(2)}, u32[]{:S(2)}) collective-permute-start(bf16[128,256]{1,0:T(8,128)(2,1)S(1)} %get-tuple-element.28), channel_id=1, source_target_pairs={{0,4},{4,8},{8,12},{12,0},{1,5},{5,9},{9,13},{13,1},{2,6},{6,10},{... | collective-permute-start | bytes 196616 | tf_op jit(solution)/shard_map/ppermute | solution.py:467
  5.5 1.9 %shard_map.128 = (bf16[1024,1536]{1,0:T(8,128)(2,1)S(1)}, bf16[64,1536]{1,0:T(8,128)(2,1)S(1)}) custom-call(bf16[1024,1536]{1,0:T(8,128)(2,1)} %refs_0_.2, bf16[64,1536]{1,0:T(8,128)(2,1)} %refs_1_.2), custom_call_target="tpu_custom_call" | custom-call | bytes 3342336 | tf_op jit(solution)/shard_map/pallas_call | solution.py:408
  7.4 2.4 %collective-permute-done.tail_ref = bf16[128,256]{1,0:T(8,128)(2,1)S(1)} collective-permute-done((bf16[128,256]{1,0:T(8,128)(2,1)S(1)}, bf16[128,256]{1,0:T(8,128)(2,1)S(1)}, u32[]{:S(2)}, u32[]{:S(2)}) %collective-permute-start) | collective-permute-done | bytes 65568 | tf_op jit(solution)/shard_map/ppermute | solution.py:467
  9.8 0.0 copy-start.6
  9.8 0.0 copy-start.7
  9.8 0.0 copy-start.5
  9.8 2.6 %shard_map.129 = (bf16[2,64,1536]{2,1,0:T(8,128)(2,1)S(1)}, bf16[2,64,1536]{2,1,0:T(8,128)(2,1)S(1)}) custom-call(f32[16]{0:T(128)S(1)} %copy-done.4, bf16[256,1024]{1,0:T(8,128)(2,1)S(1)} %copy-done, bf16[256,128]{1,0:T(8,128)(2,1)S(1)} %copy-done.1, bf16[256,128]{1,0:T(8,128)(2,1)S(1)} %copy-done.2, s32[8,128]{1,0:T(8,128)S(1)} %bitcast.2, ...), custom_call_target="tpu_custom_call" | custom-call | flops 1073741824 | bytes 4132928 | tf_op jit(solution)/shard_map/pallas_call | solution.py:408
  12.4 0.1 collective-permute-start.1
  12.5 1.7 %collective-permute-done.1.taken_ref = bf16[2,64,1536]{2,1,0:T(8,128)(2,1)S(1)} collective-permute-done((bf16[2,64,1536]{2,1,0:T(8,128)(2,1)S(1)}, bf16[2,64,1536]{2,1,0:T(8,128)(2,1)S(1)}, u32[]{:S(2)}, u32[]{:S(2)}) %collective-permute-start.1) | collective-permute-done | bytes 393248 | tf_op jit(solution)/shard_map/ppermute | solution.py:25
  14.2 0.1 shard_map.130
  14.3 1.8 %collective-permute-start.2 = (bf16[64,1536]{1,0:T(8,128)(2,1)S(1)}, bf16[64,1536]{1,0:T(8,128)(2,1)S(1)}, u32[]{:S(2)}, u32[]{:S(2)}) collective-permute-start(bf16[64,1536]{1,0:T(8,128)(2,1)S(1)} %get-tuple-element.35), channel_id=1, source_target_pairs={{0,2},{1,3},{2,0},{3,1},{4,6},{5,7},{6,4},{7,5},{8,10},{9,11},{10,... | collective-permute-start | bytes 589832 | tf_op jit(solution)/shard_map/ppermute | solution.py:621
  16.1 0.1 copy.14.ids_ref
  16.2 0.1 copy.15.route_ref
  16.3 5.0 %collective-permute-done.2.refs_0_ = bf16[64,1536]{1,0:T(8,128)(2,1)S(1)} collective-permute-done((bf16[64,1536]{1,0:T(8,128)(2,1)S(1)}, bf16[64,1536]{1,0:T(8,128)(2,1)S(1)}, u32[]{:S(2)}, u32[]{:S(2)}) %collective-permute-start.2) | collective-permute-done | bytes 196640 | tf_op jit(solution)/shard_map/ppermute | solution.py:621
  21.3 0.2 shard_map.131
  21.6 0.1 collective-permute-start.5
  21.7 2.0 %collective-permute-start.9 = (bf16[64,1664]{1,0:T(8,128)(2,1)S(1)}, bf16[64,1664]{1,0:T(8,128)(2,1)S(1)}, u32[]{:S(2)}, u32[]{:S(2)}) collective-permute-start(bf16[64,1664]{1,0:T(8,128)(2,1)S(1)} %get-tuple-element.40.refs_0_), channel_id=1, source_target_pairs={{4,0},{5,1},{8,4},{9,5},{12,8},{13,9},{14,12},{15,13},{10,14},{11,... | collective-permute-start | bytes 638984 | tf_op jit(solution)/shard_map/ppermute | solution.py:600
  23.7 4.4 %collective-permute-done.5.refs_0_ = bf16[64,1664]{1,0:T(8,128)(2,1)S(1)} collective-permute-done((bf16[64,1664]{1,0:T(8,128)(2,1)S(1)}, bf16[64,1664]{1,0:T(8,128)(2,1)S(1)}, u32[]{:S(2)}, u32[]{:S(2)}) %collective-permute-start.5) | collective-permute-done | bytes 213024 | tf_op jit(solution)/shard_map/ppermute | solution.py:599
  28.1 0.3 collective-permute-start.6
  28.4 0.0 collective-permute-done.9.refs_1_
  28.4 1.7 %collective-permute-start.10 = (bf16[64,1664]{1,0:T(8,128)(2,1)S(1)}, bf16[64,1664]{1,0:T(8,128)(2,1)S(1)}, u32[]{:S(2)}, u32[]{:S(2)}) collective-permute-start(bf16[64,1664]{1,0:T(8,128)(2,1)S(1)} %collective-permute-done.9.refs_1_), channel_id=1, source_target_pairs={{4,0},{5,1},{8,4},{9,5},{12,8},{13,9},{14,12},{15,13},{10,14},{11,... | collective-permute-start | bytes 638984 | tf_op jit(solution)/shard_map/ppermute | solution.py:600
  30.1 0.5 collective-permute-start.18
  30.6 3.4 %collective-permute-done.6.refs_0_ = bf16[64,1664]{1,0:T(8,128)(2,1)S(1)} collective-permute-done((bf16[64,1664]{1,0:T(8,128)(2,1)S(1)}, bf16[64,1664]{1,0:T(8,128)(2,1)S(1)}, u32[]{:S(2)}, u32[]{:S(2)}) %collective-permute-start.6) | collective-permute-done | bytes 213024 | tf_op jit(solution)/shard_map/ppermute | solution.py:599
  34.0 0.2 collective-permute-start.7
  34.2 2.1 %collective-permute-start.11 = (bf16[64,1664]{1,0:T(8,128)(2,1)S(1)}, bf16[64,1664]{1,0:T(8,128)(2,1)S(1)}, u32[]{:S(2)}, u32[]{:S(2)}) collective-permute-start(bf16[64,1664]{1,0:T(8,128)(2,1)S(1)} %collective-permute-done.10.refs_1_), channel_id=1, source_target_pairs={{4,0},{5,1},{8,4},{9,5},{12,8},{13,9},{14,12},{15,13},{10,14},{11,... | collective-permute-start | bytes 638984 | tf_op jit(solution)/shard_map/ppermute | solution.py:600
  36.4 3.1 %shard_map.132 = (bf16[1,1536,768]{2,1,0:T(8,128)(2,1)S(1)}, bf16[1,1536,768]{2,1,0:T(8,128)(2,1)S(1)}, bf16[1,768,1536]{2,1,0:T(8,128)(2,1)S(1)}) custom-call(bf16[1,1536,768]{2,1,0:T(8,128)(2,1)} %refs_0_.3, bf16[1,1536,768]{2,1,0:T(8,128)(2,1)} %refs_1_.3, bf16[1,768,1536]{2,1,0:T(8,128)(2,1)} %refs_2_.1), custom_call_target="tpu_custom_call" | custom-call | bytes 7077888 | tf_op jit(solution)/shard_map/pallas_call | solution.py:408
  39.5 0.1 collective-permute-start.20
  39.6 0.5 collective-permute-start.21
  40.1 2.0 %shard_map.135 = (bf16[128,1536]{1,0:T(8,128)(2,1)S(1)}, bf16[128,1536]{1,0:T(8,128)(2,1)S(1)}) custom-call(bf16[1,1536,768]{2,1,0:T(8,128)(2,1)S(1)} %get-tuple-element.37.gate_ref, bf16[1,1536,768]{2,1,0:T(8,128)(2,1)S(1)} %get-tuple-element.38.up_ref, bf16[1,768,1536]{2,1,0:T(8,128)(2,1)S(1)} %get-tuple-element.39.down_ref, ...), custom_call_target="tpu_custom_call" | custom-call | flops 1811939328 | bytes 7929856 | tf_op jit(solution)/shard_map/pallas_call | solution.py:408
  42.1 0.1 collective-permute-start.19
  42.3 0.4 collective-permute-start.23
  42.7 0.1 collective-permute-start.24
  42.8 1.1 %shard_map.133 = (bf16[64,1536]{1,0:T(8,128)(2,1)S(1)}, bf16[64,1536]{1,0:T(8,128)(2,1)S(1)}) custom-call(bf16[1,1536,768]{2,1,0:T(8,128)(2,1)S(1)} %get-tuple-element.37.gate_ref, bf16[1,1536,768]{2,1,0:T(8,128)(2,1)S(1)} %get-tuple-element.38.up_ref, bf16[1,768,1536]{2,1,0:T(8,128)(2,1)S(1)} %get-tuple-element.39.down_ref, ...), custom_call_target="tpu_custom_call" | custom-call | flops 905969664 | bytes 7503872 | tf_op jit(solution)/shard_map/pallas_call | solution.py:408
  44.0 0.1 collective-permute-start.8
  44.1 2.0 %collective-permute-start.12 = (bf16[32,1664]{1,0:T(8,128)(2,1)S(1)}, bf16[32,1664]{1,0:T(8,128)(2,1)S(1)}, u32[]{:S(2)}, u32[]{:S(2)}) collective-permute-start(bf16[32,1664]{1,0:T(8,128)(2,1)S(1)} %slice.35), channel_id=1, source_target_pairs={{4,0},{5,1},{8,4},{9,5},{12,8},{13,9},{14,12},{15,13},{10,14},{11,... | collective-permute-start | bytes 319496 | tf_op jit(solution)/shard_map/ppermute | solution.py:600
  46.1 2.0 %shard_map.136 = (bf16[128,1536]{1,0:T(8,128)(2,1)S(1)}, bf16[128,1536]{1,0:T(8,128)(2,1)S(1)}) custom-call(bf16[1,1536,768]{2,1,0:T(8,128)(2,1)S(1)} %get-tuple-element.37.gate_ref, bf16[1,1536,768]{2,1,0:T(8,128)(2,1)S(1)} %get-tuple-element.38.up_ref, bf16[1,768,1536]{2,1,0:T(8,128)(2,1)S(1)} %get-tuple-element.39.down_ref, ...), custom_call_target="tpu_custom_call" | custom-call | flops 1811939328 | bytes 7929856 | tf_op jit(solution)/shard_map/pallas_call | solution.py:408
  48.1 1.2 %collective-permute-done.8.refs_0_ = bf16[32,1664]{1,0:T(8,128)(2,1)S(1)} collective-permute-done((bf16[32,1664]{1,0:T(8,128)(2,1)S(1)}, bf16[32,1664]{1,0:T(8,128)(2,1)S(1)}, u32[]{:S(2)}, u32[]{:S(2)}) %collective-permute-start.8) | collective-permute-done | bytes 106528 | tf_op jit(solution)/shard_map/ppermute | solution.py:599
  49.4 0.3 collective-permute-done.12.refs_1_
  49.6 0.3 collective-permute-start.22
  49.9 0.3 collective-permute-start.13
  50.1 0.3 collective-permute-start.14
  50.4 2.0 %shard_map.137 = (bf16[128,1536]{1,0:T(8,128)(2,1)S(1)}, bf16[128,1536]{1,0:T(8,128)(2,1)S(1)}) custom-call(bf16[1,1536,768]{2,1,0:T(8,128)(2,1)S(1)} %get-tuple-element.37.gate_ref, bf16[1,1536,768]{2,1,0:T(8,128)(2,1)S(1)} %get-tuple-element.38.up_ref, bf16[1,768,1536]{2,1,0:T(8,128)(2,1)S(1)} %get-tuple-element.39.down_ref, ...), custom_call_target="tpu_custom_call" | custom-call | flops 1811939328 | bytes 7929856 | tf_op jit(solution)/shard_map/pallas_call | solution.py:408
  52.5 0.3 collective-permute-start.25
  52.8 0.1 convert_add_fusion.1
  52.9 1.2 %shard_map.134 = (bf16[64,1536]{1,0:T(8,128)(2,1)S(1)}, bf16[64,1536]{1,0:T(8,128)(2,1)S(1)}) custom-call(bf16[1,1536,768]{2,1,0:T(8,128)(2,1)S(1)} %get-tuple-element.37.gate_ref, bf16[1,1536,768]{2,1,0:T(8,128)(2,1)S(1)} %get-tuple-element.38.up_ref, bf16[1,768,1536]{2,1,0:T(8,128)(2,1)S(1)} %get-tuple-element.39.down_ref, ...), custom_call_target="tpu_custom_call" | custom-call | flops 905969664 | bytes 7503872 | tf_op jit(solution)/shard_map/pallas_call | solution.py:408
  54.1 0.3 collective-permute-start.15
  54.4 0.1 add_convert_fusion
  54.5 0.6 collective-permute-start.26
  55.2 1.5 %collective-permute-start.29 = (bf16[64,1536]{1,0:T(8,128)(2,1)S(1)}, bf16[64,1536]{1,0:T(8,128)(2,1)S(1)}, u32[]{:S(2)}, u32[]{:S(2)}) collective-permute-start(bf16[64,1536]{1,0:T(8,128)(2,1)S(1)} %get-tuple-element.56), channel_id=1, source_target_pairs={{4,0},{5,1},{8,4},{9,5},{12,8},{13,9},{14,12},{15,13},{10,14},{11,... | collective-permute-start | bytes 589832 | tf_op jit(solution)/shard_map/ppermute | solution.py:600
  56.6 0.1 convert_add_fusion
  56.7 4.9 %collective-permute-done.26 = bf16[64,1536]{1,0:T(8,128)(2,1)S(1)} collective-permute-done((bf16[64,1536]{1,0:T(8,128)(2,1)S(1)}, bf16[64,1536]{1,0:T(8,128)(2,1)S(1)}, u32[]{:S(2)}, u32[]{:S(2)}) %collective-permute-start.26) | collective-permute-done | bytes 196640 | tf_op jit(solution)/shard_map/ppermute | solution.py:599
  61.7 0.5 collective-permute-done.29
  62.1 0.1 fusion.2
  62.2 1.6 %collective-permute-start.27 = (bf16[64,1536]{1,0:T(8,128)(2,1)S(1)}, bf16[64,1536]{1,0:T(8,128)(2,1)S(1)}, u32[]{:S(2)}, u32[]{:S(2)}) collective-permute-start(bf16[64,1536]{1,0:T(8,128)(2,1)S(1)} %get-tuple-element.53), channel_id=1, source_target_pairs={{0,4},{1,5},{4,8},{5,9},{8,12},{9,13},{12,14},{13,15},{14,10},{15,... | collective-permute-start | bytes 589832 | tf_op jit(solution)/shard_map/ppermute | solution.py:599
  63.9 0.4 collective-permute-start.30
  64.3 2.8 %collective-permute-start.16 = (bf16[64,1536]{1,0:T(8,128)(2,1)S(1)}, bf16[64,1536]{1,0:T(8,128)(2,1)S(1)}, u32[]{:S(2)}, u32[]{:S(2)}) collective-permute-start(bf16[64,1536]{1,0:T(8,128)(2,1)S(1)} %add_convert_fusion.2), channel_id=1, source_target_pairs={{0,14},{1,15},{4,10},{5,11},{8,6},{9,7},{12,2},{13,3},{14,0},{15,1... | collective-permute-start | bytes 589832 | tf_op jit(solution)/shard_map/ppermute | solution.py:659
  67.2 1.7 %collective-permute-done.27 = bf16[64,1536]{1,0:T(8,128)(2,1)S(1)} collective-permute-done((bf16[64,1536]{1,0:T(8,128)(2,1)S(1)}, bf16[64,1536]{1,0:T(8,128)(2,1)S(1)}, u32[]{:S(2)}, u32[]{:S(2)}) %collective-permute-start.27) | collective-permute-done | bytes 196640 | tf_op jit(solution)/shard_map/ppermute | solution.py:599
  68.9 1.6 %collective-permute-done.30 = bf16[64,1536]{1,0:T(8,128)(2,1)S(1)} collective-permute-done((bf16[64,1536]{1,0:T(8,128)(2,1)S(1)}, bf16[64,1536]{1,0:T(8,128)(2,1)S(1)}, u32[]{:S(2)}, u32[]{:S(2)}) %collective-permute-start.30) | collective-permute-done | bytes 196640 | tf_op jit(solution)/shard_map/ppermute | solution.py:600
  70.5 0.1 fusion.3
  70.6 6.6 %collective-permute-start.28 = (bf16[64,1536]{1,0:T(8,128)(2,1)S(1)}, bf16[64,1536]{1,0:T(8,128)(2,1)S(1)}, u32[]{:S(2)}, u32[]{:S(2)}) collective-permute-start(bf16[64,1536]{1,0:T(8,128)(2,1)S(1)} %get-tuple-element.51), channel_id=1, source_target_pairs={{0,4},{1,5},{4,8},{5,9},{8,12},{9,13},{12,14},{13,15},{14,10},{15,... | collective-permute-start | bytes 589832 | tf_op jit(solution)/shard_map/ppermute | solution.py:599
  77.2 3.2 %collective-permute-done.28 = bf16[64,1536]{1,0:T(8,128)(2,1)S(1)} collective-permute-done((bf16[64,1536]{1,0:T(8,128)(2,1)S(1)}, bf16[64,1536]{1,0:T(8,128)(2,1)S(1)}, u32[]{:S(2)}, u32[]{:S(2)}) %collective-permute-start.28) | collective-permute-done | bytes 196640 | tf_op jit(solution)/shard_map/ppermute | solution.py:599
  80.4 2.5 %collective-permute-done.31 = bf16[64,1536]{1,0:T(8,128)(2,1)S(1)} collective-permute-done((bf16[64,1536]{1,0:T(8,128)(2,1)S(1)}, bf16[64,1536]{1,0:T(8,128)(2,1)S(1)}, u32[]{:S(2)}, u32[]{:S(2)}) %collective-permute-start.31) | collective-permute-done | bytes 196640 | tf_op jit(solution)/shard_map/ppermute | solution.py:600
  82.9 0.8 add_convert_fusion.1
  (40 shorter events, 0.2 us)
Async XLA Ops:
  0.0 9.7 %copy-start.3 = (s32[1024]{0:T(1024)S(1)}, s32[1024]{0:T(1024)}, u32[]{:S(2)}) copy-start(s32[1024]{0:T(1024)} %param.17) | copy-start | bytes 12292
  0.0 9.7 %copy-start = (bf16[256,1024]{1,0:T(8,128)(2,1)S(1)}, bf16[256,1024]{1,0:T(8,128)(2,1)}, u32[]{:S(2)}) copy-start(bf16[256,1024]{1,0:T(8,128)(2,1)} %query_any.3) | copy-start | bytes 1572868
  0.0 9.7 %copy-start.1 = (bf16[256,128]{1,0:T(8,128)(2,1)S(1)}, bf16[256,128]{1,0:T(8,128)(2,1)}, u32[]{:S(2)}) copy-start(bf16[256,128]{1,0:T(8,128)(2,1)} %key_any.3) | copy-start | bytes 196612
  0.0 9.7 %copy-start.2 = (bf16[256,128]{1,0:T(8,128)(2,1)S(1)}, bf16[256,128]{1,0:T(8,128)(2,1)}, u32[]{:S(2)}) copy-start(bf16[256,128]{1,0:T(8,128)(2,1)} %value_any.3) | copy-start | bytes 196612
  0.0 9.7 %copy-start.4 = (f32[16]{0:T(128)S(1)}, f32[16]{0:T(128)}, u32[]{:S(2)}) copy-start(f32[16]{0:T(128)} %sink_any.3) | copy-start | bytes 196
  2.3 7.4 %collective-permute-start = (bf16[128,256]{1,0:T(8,128)(2,1)S(1)}, bf16[128,256]{1,0:T(8,128)(2,1)S(1)}, u32[]{:S(2)}, u32[]{:S(2)}) collective-permute-start(bf16[128,256]{1,0:T(8,128)(2,1)S(1)} %get-tuple-element.28), channel_id=1, source_target_pairs={{0,4},{4,8},{8,12},{12,0},{1,5},{5,9},{9,13},{13,1},{2,6},{6,10},{... | collective-permute-start | bytes 196616 | tf_op jit(solution)/shard_map/ppermute | solution.py:467
  9.8 6.4 %copy-start.6 = (s32[64,4]{0,1:T(4,128)S(1)}, s32[64,4]{0,1:T(4,128)}, u32[]{:S(2)}) copy-start(s32[64,4]{0,1:T(4,128)} %param.21) | copy-start | bytes 3076
  9.8 6.5 %copy-start.7 = (f32[64,4]{0,1:T(4,128)S(1)}, f32[64,4]{0,1:T(4,128)}, u32[]{:S(2)}) copy-start(f32[64,4]{0,1:T(4,128)} %param.22) | copy-start | bytes 3076
  9.8 6.5 %copy-start.5 = (f32[1536]{0:T(1024)S(1)}, f32[1536]{0:T(1024)}, u32[]{:S(2)}) copy-start(f32[1536]{0:T(1024)} %param.20) | copy-start | bytes 18436
  12.4 1.8 %collective-permute-start.1 = (bf16[2,64,1536]{2,1,0:T(8,128)(2,1)S(1)}, bf16[2,64,1536]{2,1,0:T(8,128)(2,1)S(1)}, u32[]{:S(2)}, u32[]{:S(2)}) collective-permute-start(bf16[2,64,1536]{2,1,0:T(8,128)(2,1)S(1)} %get-tuple-element.32), channel_id=1, source_target_pairs={{0,1},{1,0},{2,3},{3,2},{4,5},{5,4},{6,7},{7,6},{8,9},{9,8},{10,11... | collective-permute-start | bytes 1179656 | tf_op jit(solution)/shard_map/ppermute | solution.py:25
  14.3 7.0 %collective-permute-start.2 = (bf16[64,1536]{1,0:T(8,128)(2,1)S(1)}, bf16[64,1536]{1,0:T(8,128)(2,1)S(1)}, u32[]{:S(2)}, u32[]{:S(2)}) collective-permute-start(bf16[64,1536]{1,0:T(8,128)(2,1)S(1)} %get-tuple-element.35), channel_id=1, source_target_pairs={{0,2},{1,3},{2,0},{3,1},{4,6},{5,7},{6,4},{7,5},{8,10},{9,11},{10,... | collective-permute-start | bytes 589832 | tf_op jit(solution)/shard_map/ppermute | solution.py:621
  21.6 6.5 %collective-permute-start.5 = (bf16[64,1664]{1,0:T(8,128)(2,1)S(1)}, bf16[64,1664]{1,0:T(8,128)(2,1)S(1)}, u32[]{:S(2)}, u32[]{:S(2)}) collective-permute-start(bf16[64,1664]{1,0:T(8,128)(2,1)S(1)} %get-tuple-element.40.refs_0_), channel_id=1, source_target_pairs={{0,4},{1,5},{4,8},{5,9},{8,12},{9,13},{12,14},{13,15},{14,10},{15,... | collective-permute-start | bytes 638984 | tf_op jit(solution)/shard_map/ppermute | solution.py:599
  21.7 6.7 %collective-permute-start.9 = (bf16[64,1664]{1,0:T(8,128)(2,1)S(1)}, bf16[64,1664]{1,0:T(8,128)(2,1)S(1)}, u32[]{:S(2)}, u32[]{:S(2)}) collective-permute-start(bf16[64,1664]{1,0:T(8,128)(2,1)S(1)} %get-tuple-element.40.refs_0_), channel_id=1, source_target_pairs={{4,0},{5,1},{8,4},{9,5},{12,8},{13,9},{14,12},{15,13},{10,14},{11,... | collective-permute-start | bytes 638984 | tf_op jit(solution)/shard_map/ppermute | solution.py:600
  28.1 6.0 %collective-permute-start.6 = (bf16[64,1664]{1,0:T(8,128)(2,1)S(1)}, bf16[64,1664]{1,0:T(8,128)(2,1)S(1)}, u32[]{:S(2)}, u32[]{:S(2)}) collective-permute-start(bf16[64,1664]{1,0:T(8,128)(2,1)S(1)} %collective-permute-done.5.refs_0_), channel_id=1, source_target_pairs={{0,4},{1,5},{4,8},{5,9},{8,12},{9,13},{12,14},{13,15},{14,10},{15,... | collective-permute-start | bytes 638984 | tf_op jit(solution)/shard_map/ppermute | solution.py:599
  28.4 5.9 %collective-permute-start.10 = (bf16[64,1664]{1,0:T(8,128)(2,1)S(1)}, bf16[64,1664]{1,0:T(8,128)(2,1)S(1)}, u32[]{:S(2)}, u32[]{:S(2)}) collective-permute-start(bf16[64,1664]{1,0:T(8,128)(2,1)S(1)} %collective-permute-done.9.refs_1_), channel_id=1, source_target_pairs={{4,0},{5,1},{8,4},{9,5},{12,8},{13,9},{14,12},{15,13},{10,14},{11,... | collective-permute-start | bytes 638984 | tf_op jit(solution)/shard_map/ppermute | solution.py:600
  30.1 9.4 %collective-permute-start.17 = (bf16[64,1664]{1,0:T(8,128)(2,1)S(1)}, bf16[64,1664]{1,0:T(8,128)(2,1)S(1)}, u32[]{:S(2)}, u32[]{:S(2)}) collective-permute-start(bf16[64,1664]{1,0:T(8,128)(2,1)S(1)} %collective-permute-done.5.refs_0_), channel_id=1, source_target_pairs={{0,1},{1,0},{2,3},{3,2},{4,5},{5,4},{6,7},{7,6},{8,9},{9,8},{10,11... | collective-permute-start | bytes 638984 | tf_op jit(solution)/shard_map/ppermute | solution.py:25
  30.1 9.5 %collective-permute-start.18 = (bf16[64,1664]{1,0:T(8,128)(2,1)S(1)}, bf16[64,1664]{1,0:T(8,128)(2,1)S(1)}, u32[]{:S(2)}, u32[]{:S(2)}) collective-permute-start(bf16[64,1664]{1,0:T(8,128)(2,1)S(1)} %collective-permute-done.9.refs_1_), channel_id=1, source_target_pairs={{0,1},{1,0},{2,3},{3,2},{4,5},{5,4},{6,7},{7,6},{8,9},{9,8},{10,11... | collective-permute-start | bytes 638984 | tf_op jit(solution)/shard_map/ppermute | solution.py:25
  30.6 11.5 %collective-permute-start.3 = (bf16[64,1664]{1,0:T(8,128)(2,1)S(1)}, bf16[64,1664]{1,0:T(8,128)(2,1)S(1)}, u32[]{:S(2)}, u32[]{:S(2)}) collective-permute-start(bf16[64,1664]{1,0:T(8,128)(2,1)S(1)} %get-tuple-element.40.refs_0_), channel_id=1, source_target_pairs={{0,1},{1,0},{2,3},{3,2},{4,5},{5,4},{6,7},{7,6},{8,9},{9,8},{10,11... | collective-permute-start | bytes 638984 | tf_op jit(solution)/shard_map/ppermute | solution.py:25
  34.0 8.2 %collective-permute-start.7 = (bf16[64,1664]{1,0:T(8,128)(2,1)S(1)}, bf16[64,1664]{1,0:T(8,128)(2,1)S(1)}, u32[]{:S(2)}, u32[]{:S(2)}) collective-permute-start(bf16[64,1664]{1,0:T(8,128)(2,1)S(1)} %collective-permute-done.6.refs_0_), channel_id=1, source_target_pairs={{0,4},{1,5},{4,8},{5,9},{8,12},{9,13},{12,14},{13,15},{14,10},{15,... | collective-permute-start | bytes 638984 | tf_op jit(solution)/shard_map/ppermute | solution.py:599
  34.2 8.5 %collective-permute-start.11 = (bf16[64,1664]{1,0:T(8,128)(2,1)S(1)}, bf16[64,1664]{1,0:T(8,128)(2,1)S(1)}, u32[]{:S(2)}, u32[]{:S(2)}) collective-permute-start(bf16[64,1664]{1,0:T(8,128)(2,1)S(1)} %collective-permute-done.10.refs_1_), channel_id=1, source_target_pairs={{4,0},{5,1},{8,4},{9,5},{12,8},{13,9},{14,12},{15,13},{10,14},{11,... | collective-permute-start | bytes 638984 | tf_op jit(solution)/shard_map/ppermute | solution.py:600
  39.5 4.5 %collective-permute-start.20 = (bf16[64,1664]{1,0:T(8,128)(2,1)S(1)}, bf16[64,1664]{1,0:T(8,128)(2,1)S(1)}, u32[]{:S(2)}, u32[]{:S(2)}) collective-permute-start(bf16[64,1664]{1,0:T(8,128)(2,1)S(1)} %collective-permute-done.6.refs_0_), channel_id=1, source_target_pairs={{0,1},{1,0},{2,3},{3,2},{4,5},{5,4},{6,7},{7,6},{8,9},{9,8},{10,11... | collective-permute-start | bytes 638984 | tf_op jit(solution)/shard_map/ppermute | solution.py:25
  39.6 4.5 %collective-permute-start.21 = (bf16[64,1664]{1,0:T(8,128)(2,1)S(1)}, bf16[64,1664]{1,0:T(8,128)(2,1)S(1)}, u32[]{:S(2)}, u32[]{:S(2)}) collective-permute-start(bf16[64,1664]{1,0:T(8,128)(2,1)S(1)} %collective-permute-done.10.refs_1_), channel_id=1, source_target_pairs={{0,1},{1,0},{2,3},{3,2},{4,5},{5,4},{6,7},{7,6},{8,9},{9,8},{10,11... | collective-permute-start | bytes 638984 | tf_op jit(solution)/shard_map/ppermute | solution.py:25
  42.1 10.3 %collective-permute-start.19 = (bf16[128,1536]{1,0:T(8,128)(2,1)S(1)}, bf16[128,1536]{1,0:T(8,128)(2,1)S(1)}, u32[]{:S(2)}, u32[]{:S(2)}) collective-permute-start(bf16[128,1536]{1,0:T(8,128)(2,1)S(1)} %get-tuple-element.46), channel_id=1, source_target_pairs={{0,1},{1,0},{2,3},{3,2},{4,5},{5,4},{6,7},{7,6},{8,9},{9,8},{10,11... | collective-permute-start | bytes 1179656 | tf_op jit(solution)/shard_map/ppermute | solution.py:25
  42.3 7.6 %collective-permute-start.23 = (bf16[64,1664]{1,0:T(8,128)(2,1)S(1)}, bf16[64,1664]{1,0:T(8,128)(2,1)S(1)}, u32[]{:S(2)}, u32[]{:S(2)}) collective-permute-start(bf16[64,1664]{1,0:T(8,128)(2,1)S(1)} %collective-permute-done.7.refs_0_), channel_id=1, source_target_pairs={{0,1},{1,0},{2,3},{3,2},{4,5},{5,4},{6,7},{7,6},{8,9},{9,8},{10,11... | collective-permute-start | bytes 638984 | tf_op jit(solution)/shard_map/ppermute | solution.py:25
  42.7 7.4 %collective-permute-start.24 = (bf16[64,1664]{1,0:T(8,128)(2,1)S(1)}, bf16[64,1664]{1,0:T(8,128)(2,1)S(1)}, u32[]{:S(2)}, u32[]{:S(2)}) collective-permute-start(bf16[64,1664]{1,0:T(8,128)(2,1)S(1)} %collective-permute-done.11.refs_1_), channel_id=1, source_target_pairs={{0,1},{1,0},{2,3},{3,2},{4,5},{5,4},{6,7},{7,6},{8,9},{9,8},{10,11... | collective-permute-start | bytes 638984 | tf_op jit(solution)/shard_map/ppermute | solution.py:25
  44.0 5.4 %collective-permute-start.8 = (bf16[32,1664]{1,0:T(8,128)(2,1)S(1)}, bf16[32,1664]{1,0:T(8,128)(2,1)S(1)}, u32[]{:S(2)}, u32[]{:S(2)}) collective-permute-start(bf16[32,1664]{1,0:T(8,128)(2,1)S(1)} %slice.34), channel_id=1, source_target_pairs={{0,4},{1,5},{4,8},{5,9},{8,12},{9,13},{12,14},{13,15},{14,10},{15,... | collective-permute-start | bytes 319496 | tf_op jit(solution)/shard_map/ppermute | solution.py:599
  44.1 5.5 %collective-permute-start.12 = (bf16[32,1664]{1,0:T(8,128)(2,1)S(1)}, bf16[32,1664]{1,0:T(8,128)(2,1)S(1)}, u32[]{:S(2)}, u32[]{:S(2)}) collective-permute-start(bf16[32,1664]{1,0:T(8,128)(2,1)S(1)} %slice.35), channel_id=1, source_target_pairs={{4,0},{5,1},{8,4},{9,5},{12,8},{13,9},{14,12},{15,13},{10,14},{11,... | collective-permute-start | bytes 319496 | tf_op jit(solution)/shard_map/ppermute | solution.py:600
  49.4 27.9 %collective-permute-start.4 = (bf16[64,1536]{1,0:T(8,128)(2,1)S(1)}, bf16[64,1536]{1,0:T(8,128)(2,1)S(1)}, u32[]{:S(2)}, u32[]{:S(2)}) collective-permute-start(bf16[64,1536]{1,0:T(8,128)(2,1)S(1)} %get-tuple-element.42), channel_id=1, source_target_pairs={{0,1},{1,0},{2,3},{3,2},{4,5},{5,4},{6,7},{7,6},{8,9},{9,8},{10,11... | collective-permute-start | bytes 589832 | tf_op jit(solution)/shard_map/ppermute | solution.py:25
  49.6 7.0 %collective-permute-start.22 = (bf16[128,1536]{1,0:T(8,128)(2,1)S(1)}, bf16[128,1536]{1,0:T(8,128)(2,1)S(1)}, u32[]{:S(2)}, u32[]{:S(2)}) collective-permute-start(bf16[128,1536]{1,0:T(8,128)(2,1)S(1)} %get-tuple-element.48), channel_id=1, source_target_pairs={{0,1},{1,0},{2,3},{3,2},{4,5},{5,4},{6,7},{7,6},{8,9},{9,8},{10,11... | collective-permute-start | bytes 1179656 | tf_op jit(solution)/shard_map/ppermute | solution.py:25
  49.9 3.0 %collective-permute-start.13 = (bf16[32,1664]{1,0:T(8,128)(2,1)S(1)}, bf16[32,1664]{1,0:T(8,128)(2,1)S(1)}, u32[]{:S(2)}, u32[]{:S(2)}) collective-permute-start(bf16[32,1664]{1,0:T(8,128)(2,1)S(1)} %collective-permute-done.8.refs_0_), channel_id=1, source_target_pairs={{0,1},{1,0},{2,3},{3,2},{4,5},{5,4},{6,7},{7,6},{8,9},{9,8},{10,11... | collective-permute-start | bytes 319496 | tf_op jit(solution)/shard_map/ppermute | solution.py:25
  50.1 2.8 %collective-permute-start.14 = (bf16[32,1664]{1,0:T(8,128)(2,1)S(1)}, bf16[32,1664]{1,0:T(8,128)(2,1)S(1)}, u32[]{:S(2)}, u32[]{:S(2)}) collective-permute-start(bf16[32,1664]{1,0:T(8,128)(2,1)S(1)} %collective-permute-done.12.refs_1_), channel_id=1, source_target_pairs={{0,1},{1,0},{2,3},{3,2},{4,5},{5,4},{6,7},{7,6},{8,9},{9,8},{10,11... | collective-permute-start | bytes 319496 | tf_op jit(solution)/shard_map/ppermute | solution.py:25
  52.5 2.0 %collective-permute-start.25 = (bf16[128,1536]{1,0:T(8,128)(2,1)S(1)}, bf16[128,1536]{1,0:T(8,128)(2,1)S(1)}, u32[]{:S(2)}, u32[]{:S(2)}) collective-permute-start(bf16[128,1536]{1,0:T(8,128)(2,1)S(1)} %get-tuple-element.50), channel_id=1, source_target_pairs={{0,1},{1,0},{2,3},{3,2},{4,5},{5,4},{6,7},{7,6},{8,9},{9,8},{10,11... | collective-permute-start | bytes 1179656 | tf_op jit(solution)/shard_map/ppermute | solution.py:25
  54.1 10.2 %collective-permute-start.15 = (bf16[64,1536]{1,0:T(8,128)(2,1)S(1)}, bf16[64,1536]{1,0:T(8,128)(2,1)S(1)}, u32[]{:S(2)}, u32[]{:S(2)}) collective-permute-start(bf16[64,1536]{1,0:T(8,128)(2,1)S(1)} %get-tuple-element.44), channel_id=1, source_target_pairs={{0,1},{1,0},{2,3},{3,2},{4,5},{5,4},{6,7},{7,6},{8,9},{9,8},{10,11... | collective-permute-start | bytes 589832 | tf_op jit(solution)/shard_map/ppermute | solution.py:25
  54.5 7.1 %collective-permute-start.26 = (bf16[64,1536]{1,0:T(8,128)(2,1)S(1)}, bf16[64,1536]{1,0:T(8,128)(2,1)S(1)}, u32[]{:S(2)}, u32[]{:S(2)}) collective-permute-start(bf16[64,1536]{1,0:T(8,128)(2,1)S(1)} %get-tuple-element.55), channel_id=1, source_target_pairs={{0,4},{1,5},{4,8},{5,9},{8,12},{9,13},{12,14},{13,15},{14,10},{15,... | collective-permute-start | bytes 589832 | tf_op jit(solution)/shard_map/ppermute | solution.py:599
  55.2 7.0 %collective-permute-start.29 = (bf16[64,1536]{1,0:T(8,128)(2,1)S(1)}, bf16[64,1536]{1,0:T(8,128)(2,1)S(1)}, u32[]{:S(2)}, u32[]{:S(2)}) collective-permute-start(bf16[64,1536]{1,0:T(8,128)(2,1)S(1)} %get-tuple-element.56), channel_id=1, source_target_pairs={{4,0},{5,1},{8,4},{9,5},{12,8},{13,9},{14,12},{15,13},{10,14},{11,... | collective-permute-start | bytes 589832 | tf_op jit(solution)/shard_map/ppermute | solution.py:600
  62.2 6.7 %collective-permute-start.27 = (bf16[64,1536]{1,0:T(8,128)(2,1)S(1)}, bf16[64,1536]{1,0:T(8,128)(2,1)S(1)}, u32[]{:S(2)}, u32[]{:S(2)}) collective-permute-start(bf16[64,1536]{1,0:T(8,128)(2,1)S(1)} %get-tuple-element.53), channel_id=1, source_target_pairs={{0,4},{1,5},{4,8},{5,9},{8,12},{9,13},{12,14},{13,15},{14,10},{15,... | collective-permute-start | bytes 589832 | tf_op jit(solution)/shard_map/ppermute | solution.py:599
  63.9 6.7 %collective-permute-start.30 = (bf16[64,1536]{1,0:T(8,128)(2,1)S(1)}, bf16[64,1536]{1,0:T(8,128)(2,1)S(1)}, u32[]{:S(2)}, u32[]{:S(2)}) collective-permute-start(bf16[64,1536]{1,0:T(8,128)(2,1)S(1)} %get-tuple-element.54), channel_id=1, source_target_pairs={{4,0},{5,1},{8,4},{9,5},{12,8},{13,9},{14,12},{15,13},{10,14},{11,... | collective-permute-start | bytes 589832 | tf_op jit(solution)/shard_map/ppermute | solution.py:600
  64.3 12.9 %collective-permute-start.16 = (bf16[64,1536]{1,0:T(8,128)(2,1)S(1)}, bf16[64,1536]{1,0:T(8,128)(2,1)S(1)}, u32[]{:S(2)}, u32[]{:S(2)}) collective-permute-start(bf16[64,1536]{1,0:T(8,128)(2,1)S(1)} %add_convert_fusion.2), channel_id=1, source_target_pairs={{0,14},{1,15},{4,10},{5,11},{8,6},{9,7},{12,2},{13,3},{14,0},{15,1... | collective-permute-start | bytes 589832 | tf_op jit(solution)/shard_map/ppermute | solution.py:659
  70.6 9.8 %collective-permute-start.28 = (bf16[64,1536]{1,0:T(8,128)(2,1)S(1)}, bf16[64,1536]{1,0:T(8,128)(2,1)S(1)}, u32[]{:S(2)}, u32[]{:S(2)}) collective-permute-start(bf16[64,1536]{1,0:T(8,128)(2,1)S(1)} %get-tuple-element.51), channel_id=1, source_target_pairs={{0,4},{1,5},{4,8},{5,9},{8,12},{9,13},{12,14},{13,15},{14,10},{15,... | collective-permute-start | bytes 589832 | tf_op jit(solution)/shard_map/ppermute | solution.py:599
  77.2 5.7 %collective-permute-start.31 = (bf16[64,1536]{1,0:T(8,128)(2,1)S(1)}, bf16[64,1536]{1,0:T(8,128)(2,1)S(1)}, u32[]{:S(2)}, u32[]{:S(2)}) collective-permute-start(bf16[64,1536]{1,0:T(8,128)(2,1)S(1)} %get-tuple-element.52), channel_id=1, source_target_pairs={{4,0},{5,1},{8,4},{9,5},{12,8},{13,9},{14,12},{15,13},{10,14},{11,... | collective-permute-start | bytes 589832 | tf_op jit(solution)/shard_map/ppermute | solution.py:600
